TPU v7x, 256 devices: a whole 4x4x8 slice. The times are simulated.
256 devices in a mesh: strike: 32 (over y_lo, z, core), depth: 8 (over x, y_hi).
Axes of the slice: x: 4, y: 4 (y_hi: 2, y_lo: 2; y = y_hi * 2 + y_lo), z: 8, core: 2. Of those that a mesh axis runs over, the one named last changes fastest.
Arguments:
- velocity: float32 [3, 64, 32, 4096], P(None, 'depth', None, 'strike'), may hold values from -6 to 6
- stress: float32 [6, 64, 32, 4096], P(None, 'depth', None, 'strike'), may hold values from -6 to 6
- buoyancy: float32 [64, 32, 4096], P('depth', None, 'strike'), may hold values from 0.5 to 1
- lame_lambda: float32 [64, 32, 4096], P('depth', None, 'strike'), may hold values from 0.3 to 0.8
- shear_modulus: float32 [64, 32, 4096], P('depth', None, 'strike'), may hold values from 0.3 to 0.8
- past_rates: float32 [64, 64, 4096], P(None, 'depth', 'strike'), may hold values from -6 to 6
- memory_coefs: float32 [64], replicated, may hold values from 0.02 to 0.2
- prestress: float32 [64, 4096], P('depth', 'strike'), may hold values from -6 to 6
- fault_mask: int32 [64, 4096], P('depth', 'strike'), may hold values 0 or 1
Outputs:
- velocity_out: float32 [3, 64, 32, 4096], P(None, 'depth', None, 'strike')
- stress_out: float32 [6, 64, 32, 4096], P(None, 'depth', None, 'strike')
All inputs are finite; a program needn't handle non-finite values. No bound on the sum of `fault_mask` on one device may be relied on, other than what follows from the above.
Results may differ from a plain program's by a relative error of at most 0.0001.
Values sent between devices are 32-bit elements; how exact they have to be, the bound alone decides.
No kernel may reach another device: no remote copies, remote signals or barrier semaphores. Data moves between devices by JAX's collectives and lax.ppermute only.
A program may use at most 64 MiB of HBM per device.

v0:
```python
import functools

import jax
import jax.numpy as jnp
from jax import lax
from jax.experimental import pallas as pl
from jax.experimental.pallas import tpu as pltpu
from jax.sharding import PartitionSpec as P

HIST = 64
STEPS = 8
DT = 0.3
FRIC = 0.5

NY = 32
Y0 = NY // 2
LANES = 128
EXT = 2 * LANES
W = STEPS
ROWS = 16
VMEM = pl.BlockSpec(memory_space=pltpu.VMEM)
SMEM = pl.BlockSpec(memory_space=pltpu.SMEM)

VX, VY, VZ, SXX, SXZ, SYZ, SZZ, SYY, SXY, B, LAM, MU = range(12)

UP = ((VX, 2), (VX, 3), (VY, 2), (VY, 3), (VZ, 2), (SXX, 2), (SXZ, 2), (SYZ, 2), (SZZ, 2), (SYY, 2), (SXY, 2))
DOWN = ((VX, 9), (VY, 9), (VZ, 8), (VZ, 9), (SXZ, 9), (SYZ, 9), (SZZ, 9))
UP_TO = tuple((f, z + 8) for f, z in UP)
DOWN_TO = tuple((f, z - 8) for f, z in DOWN)
UP_FIRST = UP + ((B, 2), (LAM, 2), (MU, 2))
DOWN_FIRST = DOWN + ((B, 9), (LAM, 9), (MU, 9))


def tiles(planes):
    return len(planes) + -(-len(planes) // 8)


def call(body, outs, ins, aliases=None, smem=()):
    return pl.pallas_call(
        body,
        out_shape=[jax.ShapeDtypeStruct(s, jnp.float32) for s in outs],
        in_specs=[SMEM if i in smem else VMEM for i in range(len(ins))],
        out_specs=[VMEM] * len(outs),
        input_output_aliases=aliases or {},
        compiler_params=pltpu.CompilerParams(vmem_limit_bytes=32 * 1024 * 1024),
        cost_estimate=pl.CostEstimate(flops=4_000_000, bytes_accessed=4_000_000, transcendentals=0),
    )(*ins)


def lane_of(rows):
    return lax.broadcasted_iota(jnp.int32, (rows, LANES), 1)


def rolled(tile, by):
    by %= LANES
    return tile if by == 0 else pltpu.roll(tile, by, 1)


def ahead_x(f):
    return pltpu.roll(f, f.shape[1] - 1, 1)


def behind_x(f):
    return pltpu.roll(f, 1, 1)


def ahead_y(f):
    row = lax.broadcasted_iota(jnp.int32, f.shape, 0)
    return jnp.where(row == NY - 1, 0.0, pltpu.roll(f, NY - 1, 0))


def behind_y(f):
    row = lax.broadcasted_iota(jnp.int32, f.shape, 0)
    return jnp.where(row == 0, 0.0, pltpu.roll(f, 1, 0))


def plane_of(refs, f, z):
    v, s, q, m = refs
    if f < SXX:
        return v.at[f, z]
    if f < SXY:
        return s.at[f - SXX, z]
    if f == SXY:
        return q.at[z]
    return m.at[f - B, z - 2]


def velocity_change(stress, z, b, want):
    sxy, sxz, syz, szz = stress(SXY, z), stress(SXZ, z), stress(SYZ, z), stress(SZZ, z)
    out = {}
    if VX in want:
        sxx = stress(SXX, z)
        out[VX] = b * ((ahead_x(sxx) - sxx) + (sxy - behind_y(sxy)) + (sxz - stress(SXZ, z - 1)))
    if VY in want:
        syy = stress(SYY, z)
        out[VY] = b * ((sxy - behind_x(sxy)) + (ahead_y(syy) - syy) + (syz - stress(SYZ, z - 1)))
    if VZ in want:
        out[VZ] = b * ((sxz - behind_x(sxz)) + (syz - behind_y(syz)) + (stress(SZZ, z + 1) - szz))
    return out


def stress_change(v, z, lam, mu, want):
    vx, vy, vz = v[VX, z], v[VY, z], v[VZ, z]
    ex = vx - behind_x(vx)
    ey = vy - behind_y(vy)
    ez = vz - v[VZ, z - 1]
    spread = lam * (ex + ey + ez)
    twice = mu + mu
    out = {}
    if SXX in want:
        out[SXX] = spread + twice * ex
        out[SYY] = spread + twice * ey
        out[SXY] = mu * ((ahead_y(vx) - vx) + (ahead_x(vy) - vy))
    out[SZZ] = spread + twice * ez
    out[SXZ] = mu * ((v[VX, z + 1] - vx) + (ahead_x(vz) - vz))
    out[SYZ] = mu * ((v[VY, z + 1] - vy) + (ahead_y(vz) - vz))
    return out


ALL_V = (VX, VY, VZ)
ALL_S = (SXX, SXZ, SYZ, SZZ, SYY, SXY)


def rate_at(v, z):
    return v[VX, z, Y0 + 1 : Y0 + 2, :] - v[VX, z, Y0 : Y0 + 1, :]


def slide(q, fp, z, traction):
    slides = fp[1, pl.ds(z, 1), :] > 0.5
    q[z, Y0 : Y0 + 1, :] = jnp.where(slides, traction, q[z, Y0 : Y0 + 1, :])


def pack(refs, planes, out):
    lane = lane_of(NY)
    for first in range(0, len(planes), 8):
        edges = jnp.zeros((NY, LANES), jnp.float32)
        for i, (f, z) in enumerate(planes[first : first + 8]):
            ref = plane_of(refs, f, z)
            out[first + i] = ref[:, :LANES]
            moved = rolled(ref[:, LANES:], W + 2 * W * i)
            edges = jnp.where((lane >= 2 * W * i) & (lane < 2 * W * (i + 1)), moved, edges)
        out[len(planes) + first // 8] = edges


def unpacked(got, planes, i, rows=slice(None)):
    edges = got[len(planes) + i // 8, rows, :]
    return jnp.concatenate([got[i, rows, :], rolled(edges, -(W + 2 * W * (i % 8)))], axis=1)


def edges_kernel(coefs, past, vel, str_, b, lam, mu, pre, mask, to_next, to_prev, owed):
    lane8 = lane_of(8)
    sums = [None] * STEPS
    for j in range(STEPS):
        parts = [None] * 4
        for k in range(HIST - j):
            term = coefs[j + k] * past[k]
            parts[k % 4] = term if parts[k % 4] is None else parts[k % 4] + term
        sums[j] = (parts[0] + parts[1]) + (parts[2] + parts[3])
        owed[j] = sums[j]
    nxt = jnp.zeros((8, LANES), jnp.float32)
    prv = jnp.zeros((8, LANES), jnp.float32)
    for i, plane in enumerate(sums + [pre[...], mask[...]]):
        here = (lane8 >= W * i) & (lane8 < W * (i + 1))
        nxt = jnp.where(here, rolled(plane, W * i - (LANES - W)), nxt)
        prv = jnp.where(here, rolled(plane, W * i), prv)
    to_next[6] = jnp.zeros((NY, LANES), jnp.float32)
    to_prev[6] = jnp.zeros((NY, LANES), jnp.float32)
    to_next[6, 0:8, :] = nxt
    to_prev[6, 0:8, :] = prv
    lane = lane_of(NY)
    fields = [(vel, f) for f in range(3)] + [(str_, f) for f in range(6)] + [(b, None), (lam, None), (mu, None)]
    for t in range(6):
        nxt = jnp.zeros((NY, LANES), jnp.float32)
        prv = jnp.zeros((NY, LANES), jnp.float32)
        for i in range(16):
            ref, f = fields[2 * t + i // 8]
            plane = ref[i % 8] if f is None else ref[f, i % 8]
            here = (lane >= W * i) & (lane < W * (i + 1))
            nxt = jnp.where(here, rolled(plane, W * i - (LANES - W)), nxt)
            prv = jnp.where(here, rolled(plane, W * i), prv)
        to_next[t] = nxt
        to_prev[t] = prv


def move_first(refs, z, q_now=None):
    v, s, q, m = refs

    def stress(f, at):
        return (q if q_now is None else q_now)[at] if f == SXY else s[f - SXX, at]

    return velocity_change(stress, z, m[0, z - 2], ALL_V)


def start_kernel(vel, str_, b, lam, mu, pre, mask, owed, from_prev, from_next, v, s, q, m, fp, lists, up, down):
    lane = lane_of(NY)
    lane8 = lane_of(8)
    empty = jnp.zeros((NY, EXT), jnp.float32)
    s[SXZ - SXX, 1] = empty
    s[SYZ - SXX, 1] = empty
    s[SZZ - SXX, 10] = empty
    refs = (v, s, q, m)
    fields = [(vel, f, f) for f in range(3)] + [(str_, i, f) for i, f in enumerate((SXX, SXY, SXZ, SYZ, SZZ, SYY))]
    fields += [(b, None, B), (lam, None, LAM), (mu, None, MU)]
    for k, (ref, i, f) in enumerate(fields):
        for z in range(8):
            at = (k % 2) * 8 + z
            plane = ref[z] if i is None else ref[i, z]
            edge = jnp.where(
                lane < LANES // 2,
                rolled(from_next[k // 2], -W * at),
                rolled(from_prev[k // 2], LANES - W - W * at),
            )
            if f >= B:
                plane, edge = DT * plane, DT * edge
            to = plane_of(refs, f, z + 2)
            to[:, :LANES] = plane
            to[:, LANES:] = edge
    fp[...] = jnp.zeros_like(fp)
    lists[...] = jnp.zeros_like(lists)
    for i in range(STEPS + 2):
        plane = owed[i] if i < STEPS else (pre, mask)[i - STEPS][...]
        edge = jnp.where(
            lane8 < LANES // 2,
            rolled(from_next[6, 0:8, :], -W * i),
            rolled(from_prev[6, 0:8, :], LANES - W - W * i),
        )
        to, j = (lists, i) if i < STEPS else (fp, i - STEPS)
        to[j, 2:10, :LANES] = plane
        to[j, 2:10, LANES:] = edge

    def step(z, carry):
        for f, change in move_first(refs, z).items():
            v[f, z] += change
        return carry

    lax.fori_loop(2, 10, step, 0)
    pack(refs, UP_FIRST, up)
    pack(refs, DOWN_FIRST, down)
    last = tiles(UP_FIRST)
    up[last] = jnp.zeros((NY, LANES), jnp.float32)
    for i in range(STEPS + 2):
        to, j = (lists, i) if i < STEPS else (fp, i - STEPS)
        up[last, i : i + 1, :] = to[j, 2:3, :LANES]
        up[last, 16 + i : 17 + i, :] = to[j, 2:3, LANES:]


def meet_kernel(first, coefs, got_up, got_down, v, s, m, edge_m, fp, lists, sent, *more):
    up, down = (UP_FIRST, DOWN_FIRST) if first else (UP, DOWN)
    if first:
        edge_out, fp_out, lists_out = more
        for k in range(3):
            edge_out[k, 0] = unpacked(got_down, down, down.index((B + k, 9)))
            edge_out[k, 1] = unpacked(got_up, up, up.index((B + k, 2)))
        fp_out[...] = fp[...]
        lists_out[...] = lists[...]
        last = tiles(up)
        for i in range(STEPS + 2):
            to, j = (lists_out, i) if i < STEPS else (fp_out, i - STEPS)
            to[j, 10:11, :LANES] = got_up[last, i : i + 1, :]
            to[j, 10:11, LANES:] = got_up[last, 16 + i : 17 + i, :]
        edge_m, lists = edge_out, lists_out
    rows = slice(Y0, Y0 + 8)
    for z in range(2, 11):
        if z < 10:
            vx = v[VX, z, rows, :]
        else:
            vx = unpacked(got_up, up, up.index((VX, 2)), rows) - edge_m[0, 1, rows, :] * s[SXZ - SXX, 9, rows, :]
        if z == 2:
            vx = vx - m[0, 0, rows, :] * unpacked(got_down, down, down.index((SXZ, 9)), rows)
        rate = vx[1:2, :] - vx[0:1, :]
        for j in range(lists.shape[0] - 1):
            sent[j, z : z + 1, :] = lists[j + 1, z : z + 1, :] + coefs[j] * rate


def two_steps_kernel(first, m, edge_m, fp, lists, got_up, got_down, v_in, s_in, q_in, v, s, q, rates):
    up, down = (UP_FIRST, DOWN_FIRST) if first else (UP, DOWN)
    refs = (v, s, q, m)
    for i, (f, z) in enumerate(UP):
        plane_of(refs, f, z + 8)[...] = unpacked(got_up, up, i)
    for i, (f, z) in enumerate(DOWN):
        plane_of(refs, f, z - 8)[...] = unpacked(got_down, down, i)
    sxz, syz, szz = SXZ - SXX, SYZ - SXX, SZZ - SXX
    for z in range(2, 10):
        for f in ALL_V:
            plane = v_in[f, z]
            if z == 2 and f == VX:
                plane = plane - m[0, 0] * s[sxz, 1]
            if z == 2 and f == VY:
                plane = plane - m[0, 0] * s[syz, 1]
            if z == 9 and f == VZ:
                plane = plane + m[0, 7] * s[szz, 10]
            v[f, z] = plane
    v[VX, 10] -= edge_m[0, 1] * s_in[sxz, 9]
    v[VY, 10] -= edge_m[0, 1] * s_in[syz, 9]
    v[VZ, 1] += edge_m[0, 0] * s_in[szz, 2]

    def stress(f, z):
        return q[z] if f == SXY else s[f - SXX, z]

    def stress_a(z, s_from, q_from, lam, mu, want):
        for f, change in stress_change(v, z, lam, mu, want).items():
            if f == SXY:
                q[z] = q_from[z] + change
            else:
                s[f - SXX, z] = s_from[f - SXX, z] + change
        if SXY in want:
            slide(q, fp, z, fp[0, pl.ds(z, 1), :] + FRIC * rate_at(v, z) - lists[0, pl.ds(z, 1), :])

    def velocity_b(z, b, want):
        for f, change in velocity_change(stress, z, b, want).items():
            v[f, z] += change

    def own_stress_a(z, carry):
        stress_a(z, s_in, q_in, m[1, z - 2], m[2, z - 2], ALL_S)
        return carry

    def own_velocity_b(z, carry):
        velocity_b(z, m[0, z - 2], ALL_V)
        return carry

    def own_stress_b(z, carry):
        for f, change in stress_change(v, z, m[1, z - 2], m[2, z - 2], ALL_S).items():
            if f == SXY:
                q[z] += change
            else:
                s[f - SXX, z] += change
        slide(q, fp, z, fp[0, pl.ds(z, 1), :] + FRIC * rate_at(v, z))
        return carry

    stress_a(1, s, q, edge_m[1, 0], edge_m[2, 0], (SZZ, SXZ, SYZ))
    lax.fori_loop(2, 10, own_stress_a, 0)
    stress_a(10, s, q, edge_m[1, 1], edge_m[2, 1], ALL_S)
    velocity_b(1, edge_m[0, 0], (VZ,))
    lax.fori_loop(2, 10, own_velocity_b, 0)
    velocity_b(10, edge_m[0, 1], (VX, VY))
    rates[...] = jnp.zeros_like(rates)
    for z in range(2, 11):
        rates[z : z + 1, :] = rate_at(v, z)
    lax.fori_loop(2, 10, own_stress_b, 0)
    empty = jnp.zeros((NY, EXT), jnp.float32)
    s[sxz, 1] = empty
    s[syz, 1] = empty
    s[szz, 10] = empty


def part_kernel(coefs, m, fp, lists, rates, s, v_in, q_in, v, q, sent, up, down):
    for j in range(lists.shape[0] - 1):
        sent[j] = lists[j + 1] + coefs[j] * rates[...]
    refs = (v, s, q, m)

    def step(z, carry):
        q[z] = q_in[z]
        slide(q, fp, z, q[z, Y0 : Y0 + 1, :] - lists[0, pl.ds(z, 1), :])
        for f, change in move_first(refs, z).items():
            v[f, z] = v_in[f, z] + change
        return carry

    lax.fori_loop(2, 10, step, 0)
    pack(refs, UP, up)
    pack(refs, DOWN, down)


def end_kernel(fp, lists, v, s, q, vel, str_):
    for z in range(8):
        for f in ALL_V:
            vel[f, z] = v[f, z + 2, :, :LANES]
        for i, f in enumerate((SXX, None, SXZ, SYZ, SZZ, SYY)):
            str_[i, z] = q[z + 2, :, :LANES] if f is None else s[f - SXX, z + 2, :, :LANES]
        row = q[z + 2, Y0 : Y0 + 1, :LANES]
        slides = fp[1, z + 2 : z + 3, :LANES] > 0.5
        str_[1, z, Y0 : Y0 + 1, :] = jnp.where(slides, row - lists[0, z + 2 : z + 3, :LANES], row)


def along_strike(value, by):
    n = lax.axis_size("strike")
    return lax.ppermute(value, "strike", [(i, (i + by) % n) for i in range(n)])


def along_depth(value, by):
    n = lax.axis_size("depth")
    return lax.ppermute(value, "depth", [(i, i + by) for i in range(n) if 0 <= i + by < n])


def per_device(velocity, stress, b, lam, mu, past, coefs, pre, fault_mask):
    mask = fault_mask.astype(jnp.float32)
    edge = (7, NY, LANES)
    to_next, to_prev, owed = call(
        edges_kernel, [edge, edge, (STEPS, 8, LANES)], [coefs, past, velocity, stress, b, lam, mu, pre, mask], smem=(0,)
    )
    from_prev = along_strike(to_next, 1)
    from_next = along_strike(to_prev, -1)
    v3, s5, q1, m3 = (3, 12, NY, EXT), (5, 12, NY, EXT), (12, NY, EXT), (3, 8, NY, EXT)
    edge, plane = (3, 2, NY, EXT), (ROWS, EXT)
    v, s, q, m, fp, lists, up, down = call(
        start_kernel,
        [v3, s5, q1, m3, (2, *plane), (STEPS, *plane), (tiles(UP_FIRST) + 1, NY, LANES), (tiles(DOWN_FIRST), NY, LANES)],
        [velocity, stress, b, lam, mu, pre, mask, owed, from_prev, from_next],
    )
    edge_m = m
    for step in range(0, STEPS, 2):
        first = step == 0
        got_up = along_depth(up, -1)
        got_down = along_depth(down, 1)
        left = STEPS - step - 1
        more = call(
            functools.partial(meet_kernel, first),
            [(left, *plane)] + ([edge, (2, *plane), (STEPS, *plane)] if first else []),
            [coefs, got_up, got_down, v, s, m, edge_m, fp, lists],
            smem=(0,),
        )
        if first:
            edge_m, fp, lists = more[1:]
        got = along_strike(more[0], 1)
        v, s, q, rates = call(
            functools.partial(two_steps_kernel, first),
            [v3, s5, q1, plane],
            [m, edge_m, fp, lists, got_up, got_down, v, s, q],
            {6: 0, 7: 1, 8: 2},
        )
        if step + 2 < STEPS:
            v, q, sent, up, down = call(
                part_kernel,
                [v3, q1, (left - 1, *plane), (tiles(UP), NY, LANES), (tiles(DOWN), NY, LANES)],
                [coefs, m, fp, got, rates, s, v, q],
                {6: 0, 7: 1},
                smem=(0,),
            )
            lists = along_strike(sent, 1)
    return tuple(call(end_kernel, [velocity.shape, stress.shape], [fp, got, v, s, q]))


def solution(mesh):
    placed = (
        P(None, "depth", None, "strike"),
        P(None, "depth", None, "strike"),
        P("depth", None, "strike"),
        P("depth", None, "strike"),
        P("depth", None, "strike"),
        P(None, "depth", "strike"),
        P(),
        P("depth", "strike"),
        P("depth", "strike"),
    )
    return jax.shard_map(
        per_device,
        mesh=mesh,
        in_specs=placed,
        out_specs=(P(None, "depth", None, "strike"), P(None, "depth", None, "strike")),
        check_vma=False,
    )
```

profile of v0, /device:TPU:6, one launch (start us, length us, event | category | flops | bytes accessed | tf_op | source)
XLA Modules:
  0.0 111.9 jit_solution(9653350504340592419)
XLA Ops:
  0.6 0.7 convert_element_type.3.mask
  1.3 1.1 %copy-done = f32[6,8,32,128]{3,2,1,0:T(8,128)S(1)} copy-done((f32[6,8,32,128]{3,2,1,0:T(8,128)S(1)}, f32[6,8,32,128]{3,2,1,0:T(8,128)}, u32[]{:S(2)}) %copy-start) | copy-done | bytes 786456
  2.5 1.0 copy-done.2
  3.5 0.9 copy-done.3
  4.4 0.9 copy-done.5
  5.3 0.9 copy-done.7
  6.2 0.9 copy-done.9
  7.1 0.7 copy-done.10
  7.8 0.7 copy-done.12
  8.5 1.6 %shard_map.104 = (f32[7,32,128]{2,1,0:T(8,128)S(1)}, f32[7,32,128]{2,1,0:T(8,128)S(1)}, f32[8,8,128]{2,1,0:T(8,128)S(1)}) custom-call(f32[64]{0:T(128)S(1)} %copy-done.10, f32[64,8,128]{2,1,0:T(8,128)S(1)} %copy-done.9, f32[3,8,32,128]{3,2,1,0:T(8,128)S(1)} %copy-done.2, f32[6,8,32,128]{3,2,1,0:T(8,128)S(1)} %copy-done, f32[8,32,128]{2,1,0:T(8,128)S(1)} %copy-done.3, ...), custom_call_target="tpu_custom_call" | custom-call | flops 4000000 | bytes 4000000 | tf_op jit(solution)/shard_map/pallas_call | solution.py:39
  10.1 0.1 collective-permute-start
  10.2 6.4 %collective-permute-start.1 = (f32[7,32,128]{2,1,0:T(8,128)S(1)}, f32[7,32,128]{2,1,0:T(8,128)S(1)}, u32[]{:S(2)}, u32[]{:S(2)}) collective-permute-start(f32[7,32,128]{2,1,0:T(8,128)S(1)} %get-tuple-element.49), channel_id=1, source_target_pairs={{0,248},{8,0},{16,8},{24,16},{32,24},{40,32},{48,40},{56,48},{64,5... | collective-permute-start | bytes 344072 | tf_op jit(solution)/shard_map/ppermute | solution.py:376
  16.5 2.4 %collective-permute-done.from_prev = f32[7,32,128]{2,1,0:T(8,128)S(1)} collective-permute-done((f32[7,32,128]{2,1,0:T(8,128)S(1)}, f32[7,32,128]{2,1,0:T(8,128)S(1)}, u32[]{:S(2)}, u32[]{:S(2)}) %collective-permute-start) | collective-permute-done | bytes 114720 | tf_op jit(solution)/shard_map/ppermute | solution.py:376
  19.0 1.9 %shard_map.105 = (f32[3,12,32,256]{3,2,1,0:T(8,128)S(1)}, f32[5,12,32,256]{3,2,1,0:T(8,128)S(1)}, f32[12,32,256]{2,1,0:T(8,128)S(1)}, f32[3,8,32,256]{3,2,1,0:T(...) custom-call(f32[3,8,32,128]{3,2,1,0:T(8,128)S(1)} %copy-done.2, ...), custom_call_target="tpu_custom_call" | custom-call | flops 4000000 | bytes 4000000 | tf_op jit(solution)/shard_map/pallas_call | solution.py:39
  20.9 5.1 %collective-permute-start.2 = (f32[17,32,128]{2,1,0:T(8,128)S(1)}, f32[17,32,128]{2,1,0:T(8,128)S(1)}, u32[]{:S(2)}, u32[]{:S(2)}) collective-permute-start(f32[17,32,128]{2,1,0:T(8,128)S(1)} %get-tuple-element.50), channel_id=1, source_target_pairs={{1,0},{2,1},{3,2},{4,3},{5,4},{6,5},{7,6},{9,8},{10,9},{11,10},{12... | collective-permute-start | bytes 835592 | tf_op jit(solution)/shard_map/ppermute | solution.py:381
  26.0 2.3 %collective-permute-start.3 = (f32[12,32,128]{2,1,0:T(8,128)S(1)}, f32[12,32,128]{2,1,0:T(8,128)S(1)}, u32[]{:S(2)}, u32[]{:S(2)}) collective-permute-start(f32[12,32,128]{2,1,0:T(8,128)S(1)} %get-tuple-element.51), channel_id=1, source_target_pairs={{0,1},{1,2},{2,3},{3,4},{4,5},{5,6},{6,7},{8,9},{9,10},{10,11},{11... | collective-permute-start | bytes 589832 | tf_op jit(solution)/shard_map/ppermute | solution.py:381
  28.3 7.7 %collective-permute-done.3.got_down = f32[12,32,128]{2,1,0:T(8,128)S(1)} collective-permute-done((f32[12,32,128]{2,1,0:T(8,128)S(1)}, f32[12,32,128]{2,1,0:T(8,128)S(1)}, u32[]{:S(2)}, u32[]{:S(2)}) %collective-permute-start.3) | collective-permute-done | bytes 196640 | tf_op jit(solution)/shard_map/ppermute | solution.py:381
  36.0 0.6 shard_map.106
  36.7 3.2 %shard_map.107 = (f32[3,12,32,256]{3,2,1,0:T(8,128)S(1)}, f32[5,12,32,256]{3,2,1,0:T(8,128)S(1)}, f32[12,32,256]{2,1,0:T(8,128)S(1)}, f32[16,256]{1,0:T(8,128)S(1)}) custom-call(f32[3,8,32,256]{3,2,1,0:T(8,128)S(1)} %get-tuple-element.54.m.edge_m, ...), custom_call_target="tpu_custom_call", output_to_operand_aliasing={{0}: (6, {}), {1}: (7, {}), {2}: (8, {})} | custom-call | flops 4000000 | bytes 4000000 | tf_op jit(solution)/shard_map/pallas_call | solution.py:39
  39.9 3.1 %collective-permute-done.4.lists = f32[7,16,256]{2,1,0:T(8,128)S(1)} collective-permute-done((f32[7,16,256]{2,1,0:T(8,128)S(1)}, f32[7,16,256]{2,1,0:T(8,128)S(1)}, u32[]{:S(2)}, u32[]{:S(2)}) %collective-permute-start.4) | collective-permute-done | bytes 114720 | tf_op jit(solution)/shard_map/ppermute | solution.py:376
  43.0 1.6 %shard_map.108 = (f32[3,12,32,256]{3,2,1,0:T(8,128)S(1)}, f32[12,32,256]{2,1,0:T(8,128)S(1)}, f32[6,16,256]{2,1,0:T(8,128)S(1)}, f32[13,32,128]{2,1,0:T(8,128)S(1)}, f32[8,32,128]{2,1,0:T(8,128)S(1)}) custom-call(f32[64]{0:T(128)S(1)} %copy-done.11, f32[3,8,32,256]{3,2,1,0:T(8,128)S(1)} %get-tuple-element.54.m.edge_m, ...), custom_call_target="tpu_custom_call", output_to_operand_aliasing={{0}: (6, {}), {1}: (7, {})} | custom-call | flops 4000000 | bytes 4000000 | tf_op jit(solution)/shard_map/pallas_call | solution.py:39
  44.6 6.2 %collective-permute-start.5 = (f32[13,32,128]{2,1,0:T(8,128)S(1)}, f32[13,32,128]{2,1,0:T(8,128)S(1)}, u32[]{:S(2)}, u32[]{:S(2)}) collective-permute-start(f32[13,32,128]{2,1,0:T(8,128)S(1)} %get-tuple-element.66), channel_id=1, source_target_pairs={{1,0},{2,1},{3,2},{4,3},{5,4},{6,5},{7,6},{9,8},{10,9},{11,10},{12... | collective-permute-start | bytes 638984 | tf_op jit(solution)/shard_map/ppermute | solution.py:381
  50.8 1.9 %collective-permute-start.6 = (f32[8,32,128]{2,1,0:T(8,128)S(1)}, f32[8,32,128]{2,1,0:T(8,128)S(1)}, u32[]{:S(2)}, u32[]{:S(2)}) collective-permute-start(f32[8,32,128]{2,1,0:T(8,128)S(1)} %get-tuple-element.67), channel_id=1, source_target_pairs={{0,1},{1,2},{2,3},{3,4},{4,5},{5,6},{6,7},{8,9},{9,10},{10,11},{11... | collective-permute-start | bytes 393224 | tf_op jit(solution)/shard_map/ppermute | solution.py:381
  52.7 0.1 collective-permute-start.7
  52.8 6.1 %collective-permute-done.7.lists = f32[6,16,256]{2,1,0:T(8,128)S(1)} collective-permute-done((f32[6,16,256]{2,1,0:T(8,128)S(1)}, f32[6,16,256]{2,1,0:T(8,128)S(1)}, u32[]{:S(2)}, u32[]{:S(2)}) %collective-permute-start.7) | collective-permute-done | bytes 98336 | tf_op jit(solution)/shard_map/ppermute | solution.py:376
  58.9 1.1 collective-permute-done.6.got_down
  60.0 0.6 shard_map.109
  60.8 3.2 %shard_map.110 = (f32[3,12,32,256]{3,2,1,0:T(8,128)S(1)}, f32[5,12,32,256]{3,2,1,0:T(8,128)S(1)}, f32[12,32,256]{2,1,0:T(8,128)S(1)}, f32[16,256]{1,0:T(8,128)S(1)}) custom-call(f32[3,8,32,256]{3,2,1,0:T(8,128)S(1)} %get-tuple-element.54.m.edge_m, ...), custom_call_target="tpu_custom_call", output_to_operand_aliasing={{0}: (6, {}), {1}: (7, {}), {2}: (8, {})} | custom-call | flops 4000000 | bytes 4000000 | tf_op jit(solution)/shard_map/pallas_call | solution.py:39
  64.0 2.7 %collective-permute-done.8.lists = f32[5,16,256]{2,1,0:T(8,128)S(1)} collective-permute-done((f32[5,16,256]{2,1,0:T(8,128)S(1)}, f32[5,16,256]{2,1,0:T(8,128)S(1)}, u32[]{:S(2)}, u32[]{:S(2)}) %collective-permute-start.8) | collective-permute-done | bytes 81952 | tf_op jit(solution)/shard_map/ppermute | solution.py:376
  66.7 1.6 %shard_map.111 = (f32[3,12,32,256]{3,2,1,0:T(8,128)S(1)}, f32[12,32,256]{2,1,0:T(8,128)S(1)}, f32[4,16,256]{2,1,0:T(8,128)S(1)}, f32[13,32,128]{2,1,0:T(8,128)S(1)}, f32[8,32,128]{2,1,0:T(8,128)S(1)}) custom-call(f32[64]{0:T(128)S(1)} %copy-done.11, f32[3,8,32,256]{3,2,1,0:T(8,128)S(1)} %get-tuple-element.54.m.edge_m, ...), custom_call_target="tpu_custom_call", output_to_operand_aliasing={{0}: (6, {}), {1}: (7, {})} | custom-call | flops 4000000 | bytes 4000000 | tf_op jit(solution)/shard_map/pallas_call | solution.py:39
  68.3 5.2 %collective-permute-start.9 = (f32[13,32,128]{2,1,0:T(8,128)S(1)}, f32[13,32,128]{2,1,0:T(8,128)S(1)}, u32[]{:S(2)}, u32[]{:S(2)}) collective-permute-start(f32[13,32,128]{2,1,0:T(8,128)S(1)} %get-tuple-element.75), channel_id=1, source_target_pairs={{1,0},{2,1},{3,2},{4,3},{5,4},{6,5},{7,6},{9,8},{10,9},{11,10},{12... | collective-permute-start | bytes 638984 | tf_op jit(solution)/shard_map/ppermute | solution.py:381
  73.5 2.1 %collective-permute-start.10 = (f32[8,32,128]{2,1,0:T(8,128)S(1)}, f32[8,32,128]{2,1,0:T(8,128)S(1)}, u32[]{:S(2)}, u32[]{:S(2)}) collective-permute-start(f32[8,32,128]{2,1,0:T(8,128)S(1)} %get-tuple-element.76), channel_id=1, source_target_pairs={{0,1},{1,2},{2,3},{3,4},{4,5},{5,6},{6,7},{8,9},{9,10},{10,11},{11... | collective-permute-start | bytes 393224 | tf_op jit(solution)/shard_map/ppermute | solution.py:381
  75.7 0.1 collective-permute-start.11
  75.8 5.8 %collective-permute-done.11.lists = f32[4,16,256]{2,1,0:T(8,128)S(1)} collective-permute-done((f32[4,16,256]{2,1,0:T(8,128)S(1)}, f32[4,16,256]{2,1,0:T(8,128)S(1)}, u32[]{:S(2)}, u32[]{:S(2)}) %collective-permute-start.11) | collective-permute-done | bytes 65568 | tf_op jit(solution)/shard_map/ppermute | solution.py:376
  81.5 1.2 %collective-permute-done.10.got_down = f32[8,32,128]{2,1,0:T(8,128)S(1)} collective-permute-done((f32[8,32,128]{2,1,0:T(8,128)S(1)}, f32[8,32,128]{2,1,0:T(8,128)S(1)}, u32[]{:S(2)}, u32[]{:S(2)}) %collective-permute-start.10) | collective-permute-done | bytes 131104 | tf_op jit(solution)/shard_map/ppermute | solution.py:381
  82.8 0.6 shard_map.112
  83.4 0.1 collective-permute-start.12
  83.5 3.2 %shard_map.113 = (f32[3,12,32,256]{3,2,1,0:T(8,128)S(1)}, f32[5,12,32,256]{3,2,1,0:T(8,128)S(1)}, f32[12,32,256]{2,1,0:T(8,128)S(1)}, f32[16,256]{1,0:T(8,128)S(1)}) custom-call(f32[3,8,32,256]{3,2,1,0:T(8,128)S(1)} %get-tuple-element.54.m.edge_m, ...), custom_call_target="tpu_custom_call", output_to_operand_aliasing={{0}: (6, {}), {1}: (7, {}), {2}: (8, {})} | custom-call | flops 4000000 | bytes 4000000 | tf_op jit(solution)/shard_map/pallas_call | solution.py:39
  86.7 2.4 %collective-permute-done.12.lists = f32[3,16,256]{2,1,0:T(8,128)S(1)} collective-permute-done((f32[3,16,256]{2,1,0:T(8,128)S(1)}, f32[3,16,256]{2,1,0:T(8,128)S(1)}, u32[]{:S(2)}, u32[]{:S(2)}) %collective-permute-start.12) | collective-permute-done | bytes 49184 | tf_op jit(solution)/shard_map/ppermute | solution.py:376
  89.1 1.6 %shard_map.114 = (f32[3,12,32,256]{3,2,1,0:T(8,128)S(1)}, f32[12,32,256]{2,1,0:T(8,128)S(1)}, f32[2,16,256]{2,1,0:T(8,128)S(1)}, f32[13,32,128]{2,1,0:T(8,128)S(1)}, f32[8,32,128]{2,1,0:T(8,128)S(1)}) custom-call(f32[64]{0:T(128)S(1)} %copy-done.11, f32[3,8,32,256]{3,2,1,0:T(8,128)S(1)} %get-tuple-element.54.m.edge_m, ...), custom_call_target="tpu_custom_call", output_to_operand_aliasing={{0}: (6, {}), {1}: (7, {})} | custom-call | flops 4000000 | bytes 4000000 | tf_op jit(solution)/shard_map/pallas_call | solution.py:39
  90.7 4.9 %collective-permute-start.13 = (f32[13,32,128]{2,1,0:T(8,128)S(1)}, f32[13,32,128]{2,1,0:T(8,128)S(1)}, u32[]{:S(2)}, u32[]{:S(2)}) collective-permute-start(f32[13,32,128]{2,1,0:T(8,128)S(1)} %get-tuple-element.84), channel_id=1, source_target_pairs={{1,0},{2,1},{3,2},{4,3},{5,4},{6,5},{7,6},{9,8},{10,9},{11,10},{12... | collective-permute-start | bytes 638984 | tf_op jit(solution)/shard_map/ppermute | solution.py:381
  95.6 2.5 %collective-permute-start.14 = (f32[8,32,128]{2,1,0:T(8,128)S(1)}, f32[8,32,128]{2,1,0:T(8,128)S(1)}, u32[]{:S(2)}, u32[]{:S(2)}) collective-permute-start(f32[8,32,128]{2,1,0:T(8,128)S(1)} %get-tuple-element.85), channel_id=1, source_target_pairs={{0,1},{1,2},{2,3},{3,4},{4,5},{5,6},{6,7},{8,9},{9,10},{10,11},{11... | collective-permute-start | bytes 393224 | tf_op jit(solution)/shard_map/ppermute | solution.py:381
  98.2 5.4 %collective-permute-done.15.lists = f32[2,16,256]{2,1,0:T(8,128)S(1)} collective-permute-done((f32[2,16,256]{2,1,0:T(8,128)S(1)}, f32[2,16,256]{2,1,0:T(8,128)S(1)}, u32[]{:S(2)}, u32[]{:S(2)}) %collective-permute-start.15) | collective-permute-done | bytes 32800 | tf_op jit(solution)/shard_map/ppermute | solution.py:376
  103.6 1.2 %collective-permute-done.14.got_down = f32[8,32,128]{2,1,0:T(8,128)S(1)} collective-permute-done((f32[8,32,128]{2,1,0:T(8,128)S(1)}, f32[8,32,128]{2,1,0:T(8,128)S(1)}, u32[]{:S(2)}, u32[]{:S(2)}) %collective-permute-start.14) | collective-permute-done | bytes 131104 | tf_op jit(solution)/shard_map/ppermute | solution.py:381
  104.8 0.6 shard_map.115
  105.5 3.8 %shard_map.116 = (f32[3,12,32,256]{3,2,1,0:T(8,128)S(1)}, f32[5,12,32,256]{3,2,1,0:T(8,128)S(1)}, f32[12,32,256]{2,1,0:T(8,128)S(1)}, f32[16,256]{1,0:T(8,128)}) custom-call(f32[3,8,32,256]{3,2,1,0:T(8,128)S(1)} %get-tuple-element.54.m.edge_m, ...), custom_call_target="tpu_custom_call", output_to_operand_aliasing={{0}: (6, {}), {1}: (7, {}), {2}: (8, {})} | custom-call | flops 4000000 | bytes 4000000 | tf_op jit(solution)/shard_map/pallas_call | solution.py:39
  109.3 1.4 %collective-permute-done.16.lists = f32[1,16,256]{2,1,0:T(8,128)S(1)} collective-permute-done((f32[1,16,256]{2,1,0:T(8,128)S(1)}, f32[1,16,256]{2,1,0:T(8,128)S(1)}, u32[]{:S(2)}, u32[]{:S(2)}) %collective-permute-start.16) | collective-permute-done | bytes 16416 | tf_op jit(solution)/shard_map/ppermute | solution.py:376
  110.8 1.1 shard_map.117
  (27 shorter events, 0.3 us)
Async XLA Ops:
  1.3 1.1 %copy-start = (f32[6,8,32,128]{3,2,1,0:T(8,128)S(1)}, f32[6,8,32,128]{3,2,1,0:T(8,128)}, u32[]{:S(2)}) copy-start(f32[6,8,32,128]{3,2,1,0:T(8,128)} %str_.3) | copy-start | bytes 2359300
  2.5 1.0 copy-start.2
  3.4 0.9 copy-start.3
  4.4 0.9 copy-start.5
  5.3 0.9 copy-start.7
  6.2 0.9 copy-start.9
  7.1 0.7 copy-start.10
  7.8 0.7 copy-start.12
  8.5 10.5 %copy-start.1 = (f32[6,8,32,128]{3,2,1,0:T(8,128)S(1)}, f32[6,8,32,128]{3,2,1,0:T(8,128)}, u32[]{:S(2)}) copy-start(f32[6,8,32,128]{3,2,1,0:T(8,128)} %str_.3) | copy-start | bytes 2359300
  8.5 10.5 %copy-start.4 = (f32[8,32,128]{2,1,0:T(8,128)S(1)}, f32[8,32,128]{2,1,0:T(8,128)}, u32[]{:S(2)}) copy-start(f32[8,32,128]{2,1,0:T(8,128)} %b.3) | copy-start | bytes 393220
  8.5 10.5 %copy-start.6 = (f32[8,32,128]{2,1,0:T(8,128)S(1)}, f32[8,32,128]{2,1,0:T(8,128)}, u32[]{:S(2)}) copy-start(f32[8,32,128]{2,1,0:T(8,128)} %lam.3) | copy-start | bytes 393220
  8.5 10.5 %copy-start.8 = (f32[8,32,128]{2,1,0:T(8,128)S(1)}, f32[8,32,128]{2,1,0:T(8,128)}, u32[]{:S(2)}) copy-start(f32[8,32,128]{2,1,0:T(8,128)} %mu.3) | copy-start | bytes 393220
  10.1 25.9 %copy-start.11 = (f32[64]{0:T(128)S(1)}, f32[64]{0:T(128)}, u32[]{:S(2)}) copy-start(f32[64]{0:T(128)} %coefs.15) | copy-start | bytes 772
  10.1 8.9 %collective-permute-start = (f32[7,32,128]{2,1,0:T(8,128)S(1)}, f32[7,32,128]{2,1,0:T(8,128)S(1)}, u32[]{:S(2)}, u32[]{:S(2)}) collective-permute-start(f32[7,32,128]{2,1,0:T(8,128)S(1)} %get-tuple-element.48), channel_id=1, source_target_pairs={{0,8},{8,16},{16,24},{24,32},{32,40},{40,48},{48,56},{56,64},{64,7... | collective-permute-start | bytes 344072 | tf_op jit(solution)/shard_map/ppermute | solution.py:376
  10.2 8.8 %collective-permute-start.1 = (f32[7,32,128]{2,1,0:T(8,128)S(1)}, f32[7,32,128]{2,1,0:T(8,128)S(1)}, u32[]{:S(2)}, u32[]{:S(2)}) collective-permute-start(f32[7,32,128]{2,1,0:T(8,128)S(1)} %get-tuple-element.49), channel_id=1, source_target_pairs={{0,248},{8,0},{16,8},{24,16},{32,24},{40,32},{48,40},{56,48},{64,5... | collective-permute-start | bytes 344072 | tf_op jit(solution)/shard_map/ppermute | solution.py:376
  20.9 15.1 %collective-permute-start.2 = (f32[17,32,128]{2,1,0:T(8,128)S(1)}, f32[17,32,128]{2,1,0:T(8,128)S(1)}, u32[]{:S(2)}, u32[]{:S(2)}) collective-permute-start(f32[17,32,128]{2,1,0:T(8,128)S(1)} %get-tuple-element.50), channel_id=1, source_target_pairs={{1,0},{2,1},{3,2},{4,3},{5,4},{6,5},{7,6},{9,8},{10,9},{11,10},{12... | collective-permute-start | bytes 835592 | tf_op jit(solution)/shard_map/ppermute | solution.py:381
  26.0 10.0 %collective-permute-start.3 = (f32[12,32,128]{2,1,0:T(8,128)S(1)}, f32[12,32,128]{2,1,0:T(8,128)S(1)}, u32[]{:S(2)}, u32[]{:S(2)}) collective-permute-start(f32[12,32,128]{2,1,0:T(8,128)S(1)} %get-tuple-element.51), channel_id=1, source_target_pairs={{0,1},{1,2},{2,3},{3,4},{4,5},{5,6},{6,7},{8,9},{9,10},{10,11},{11... | collective-permute-start | bytes 589832 | tf_op jit(solution)/shard_map/ppermute | solution.py:381
  36.6 6.4 %collective-permute-start.4 = (f32[7,16,256]{2,1,0:T(8,128)S(1)}, f32[7,16,256]{2,1,0:T(8,128)S(1)}, u32[]{:S(2)}, u32[]{:S(2)}) collective-permute-start(f32[7,16,256]{2,1,0:T(8,128)S(1)} %get-tuple-element.58), channel_id=1, source_target_pairs={{0,8},{8,16},{16,24},{24,32},{32,40},{40,48},{48,56},{56,64},{64,7... | collective-permute-start | bytes 344072 | tf_op jit(solution)/shard_map/ppermute | solution.py:376
  44.6 15.4 %collective-permute-start.5 = (f32[13,32,128]{2,1,0:T(8,128)S(1)}, f32[13,32,128]{2,1,0:T(8,128)S(1)}, u32[]{:S(2)}, u32[]{:S(2)}) collective-permute-start(f32[13,32,128]{2,1,0:T(8,128)S(1)} %get-tuple-element.66), channel_id=1, source_target_pairs={{1,0},{2,1},{3,2},{4,3},{5,4},{6,5},{7,6},{9,8},{10,9},{11,10},{12... | collective-permute-start | bytes 638984 | tf_op jit(solution)/shard_map/ppermute | solution.py:381
  50.8 9.3 %collective-permute-start.6 = (f32[8,32,128]{2,1,0:T(8,128)S(1)}, f32[8,32,128]{2,1,0:T(8,128)S(1)}, u32[]{:S(2)}, u32[]{:S(2)}) collective-permute-start(f32[8,32,128]{2,1,0:T(8,128)S(1)} %get-tuple-element.67), channel_id=1, source_target_pairs={{0,1},{1,2},{2,3},{3,4},{4,5},{5,6},{6,7},{8,9},{9,10},{10,11},{11... | collective-permute-start | bytes 393224 | tf_op jit(solution)/shard_map/ppermute | solution.py:381
  52.7 6.2 %collective-permute-start.7 = (f32[6,16,256]{2,1,0:T(8,128)S(1)}, f32[6,16,256]{2,1,0:T(8,128)S(1)}, u32[]{:S(2)}, u32[]{:S(2)}) collective-permute-start(f32[6,16,256]{2,1,0:T(8,128)S(1)} %get-tuple-element.69), channel_id=1, source_target_pairs={{0,8},{8,16},{16,24},{24,32},{32,40},{40,48},{48,56},{56,64},{64,7... | collective-permute-start | bytes 294920 | tf_op jit(solution)/shard_map/ppermute | solution.py:376
  60.7 6.1 %collective-permute-start.8 = (f32[5,16,256]{2,1,0:T(8,128)S(1)}, f32[5,16,256]{2,1,0:T(8,128)S(1)}, u32[]{:S(2)}, u32[]{:S(2)}) collective-permute-start(f32[5,16,256]{2,1,0:T(8,128)S(1)} %shard_map.109), channel_id=1, source_target_pairs={{0,8},{8,16},{16,24},{24,32},{32,40},{40,48},{48,56},{56,64},{64,7... | collective-permute-start | bytes 245768 | tf_op jit(solution)/shard_map/ppermute | solution.py:376
  68.3 14.5 %collective-permute-start.9 = (f32[13,32,128]{2,1,0:T(8,128)S(1)}, f32[13,32,128]{2,1,0:T(8,128)S(1)}, u32[]{:S(2)}, u32[]{:S(2)}) collective-permute-start(f32[13,32,128]{2,1,0:T(8,128)S(1)} %get-tuple-element.75), channel_id=1, source_target_pairs={{1,0},{2,1},{3,2},{4,3},{5,4},{6,5},{7,6},{9,8},{10,9},{11,10},{12... | collective-permute-start | bytes 638984 | tf_op jit(solution)/shard_map/ppermute | solution.py:381
  73.5 9.3 %collective-permute-start.10 = (f32[8,32,128]{2,1,0:T(8,128)S(1)}, f32[8,32,128]{2,1,0:T(8,128)S(1)}, u32[]{:S(2)}, u32[]{:S(2)}) collective-permute-start(f32[8,32,128]{2,1,0:T(8,128)S(1)} %get-tuple-element.76), channel_id=1, source_target_pairs={{0,1},{1,2},{2,3},{3,4},{4,5},{5,6},{6,7},{8,9},{9,10},{10,11},{11... | collective-permute-start | bytes 393224 | tf_op jit(solution)/shard_map/ppermute | solution.py:381
  75.7 5.9 %collective-permute-start.11 = (f32[4,16,256]{2,1,0:T(8,128)S(1)}, f32[4,16,256]{2,1,0:T(8,128)S(1)}, u32[]{:S(2)}, u32[]{:S(2)}) collective-permute-start(f32[4,16,256]{2,1,0:T(8,128)S(1)} %get-tuple-element.78), channel_id=1, source_target_pairs={{0,8},{8,16},{16,24},{24,32},{32,40},{40,48},{48,56},{56,64},{64,7... | collective-permute-start | bytes 196616 | tf_op jit(solution)/shard_map/ppermute | solution.py:376
  83.4 5.7 %collective-permute-start.12 = (f32[3,16,256]{2,1,0:T(8,128)S(1)}, f32[3,16,256]{2,1,0:T(8,128)S(1)}, u32[]{:S(2)}, u32[]{:S(2)}) collective-permute-start(f32[3,16,256]{2,1,0:T(8,128)S(1)} %shard_map.112), channel_id=1, source_target_pairs={{0,8},{8,16},{16,24},{24,32},{32,40},{40,48},{48,56},{56,64},{64,7... | collective-permute-start | bytes 147464 | tf_op jit(solution)/shard_map/ppermute | solution.py:376
  90.7 14.1 %collective-permute-start.13 = (f32[13,32,128]{2,1,0:T(8,128)S(1)}, f32[13,32,128]{2,1,0:T(8,128)S(1)}, u32[]{:S(2)}, u32[]{:S(2)}) collective-permute-start(f32[13,32,128]{2,1,0:T(8,128)S(1)} %get-tuple-element.84), channel_id=1, source_target_pairs={{1,0},{2,1},{3,2},{4,3},{5,4},{6,5},{7,6},{9,8},{10,9},{11,10},{12... | collective-permute-start | bytes 638984 | tf_op jit(solution)/shard_map/ppermute | solution.py:381
  95.6 9.3 %collective-permute-start.14 = (f32[8,32,128]{2,1,0:T(8,128)S(1)}, f32[8,32,128]{2,1,0:T(8,128)S(1)}, u32[]{:S(2)}, u32[]{:S(2)}) collective-permute-start(f32[8,32,128]{2,1,0:T(8,128)S(1)} %get-tuple-element.85), channel_id=1, source_target_pairs={{0,1},{1,2},{2,3},{3,4},{4,5},{5,6},{6,7},{8,9},{9,10},{10,11},{11... | collective-permute-start | bytes 393224 | tf_op jit(solution)/shard_map/ppermute | solution.py:381
  98.1 5.5 %collective-permute-start.15 = (f32[2,16,256]{2,1,0:T(8,128)S(1)}, f32[2,16,256]{2,1,0:T(8,128)S(1)}, u32[]{:S(2)}, u32[]{:S(2)}) collective-permute-start(f32[2,16,256]{2,1,0:T(8,128)S(1)} %get-tuple-element.87), channel_id=1, source_target_pairs={{0,8},{8,16},{16,24},{24,32},{32,40},{40,48},{48,56},{56,64},{64,7... | collective-permute-start | bytes 98312 | tf_op jit(solution)/shard_map/ppermute | solution.py:376
  105.5 5.3 %collective-permute-start.16 = (f32[1,16,256]{2,1,0:T(8,128)S(1)}, f32[1,16,256]{2,1,0:T(8,128)S(1)}, u32[]{:S(2)}, u32[]{:S(2)}) collective-permute-start(f32[1,16,256]{2,1,0:T(8,128)S(1)} %shard_map.115), channel_id=1, source_target_pairs={{0,8},{8,16},{16,24},{24,32},{32,40},{40,48},{48,56},{56,64},{64,7... | collective-permute-start | bytes 49160 | tf_op jit(solution)/shard_map/ppermute | solution.py:376
where the time goes:
time: 112 us
  waiting for transfers between devices  40.7 us (36%)
  starting transfers between devices  37.2 us (33%)
  Pallas kernels  25.3 us (23%)
  local copies, waits for them, and re-layouts  7.15 us (6%)
    ppermute x8, starting transfers between devices, along_depth(): lax.ppermute(value, 'depth', [(i, i + by) for i in range(n) if 0 <= i + b...  30.2 us
    ppermute x9, waiting for transfers between devices, along_strike(): return lax.ppermute(value, 'strike', [(i, (i + by) % n) for i in range(n)])  29.4 us
    pallas_call x14, Pallas kernels, call(): pl.pallas_call(body, out_shape=[jax.ShapeDtypeStruct(s, jnp.float32) for...  25.3 us
    ppermute x8, waiting for transfers between devices, along_depth(): lax.ppermute(value, 'depth', [(i, i + by) for i in range(n) if 0 <= i + b...  11.3 us
    unnamed x26, local copies, waits for them, and re-layouts  7.15 us
    ppermute x9, starting transfers between devices, along_strike(): return lax.ppermute(value, 'strike', [(i, (i + by) % n) for i in range(n)])  7.01 us
  transfers between devices with their start and end apart: 17, of which 12 were waited for; matrix products, arithmetic and copies ran while one was open for 0% of the time, Pallas kernels for 12%

commit v1 on v0

--- a/solution.py
+++ b/solution.py
@@ -6,6 +6,7 @@
 from jax.experimental import pallas as pl
 from jax.experimental.pallas import tpu as pltpu
 from jax.sharding import PartitionSpec as P
+
 
 HIST = 64
 STEPS = 8
@@ -25,8 +26,6 @@
 
 UP = ((VX, 2), (VX, 3), (VY, 2), (VY, 3), (VZ, 2), (SXX, 2), (SXZ, 2), (SYZ, 2), (SZZ, 2), (SYY, 2), (SXY, 2))
 DOWN = ((VX, 9), (VY, 9), (VZ, 8), (VZ, 9), (SXZ, 9), (SYZ, 9), (SZZ, 9))
-UP_TO = tuple((f, z + 8) for f, z in UP)
-DOWN_TO = tuple((f, z - 8) for f, z in DOWN)
 UP_FIRST = UP + ((B, 2), (LAM, 2), (MU, 2))
 DOWN_FIRST = DOWN + ((B, 9), (LAM, 9), (MU, 9))
 
@@ -147,19 +146,20 @@
     return jnp.concatenate([got[i, rows, :], rolled(edges, -(W + 2 * W * (i % 8)))], axis=1)
 
 
-def edges_kernel(coefs, past, vel, str_, b, lam, mu, pre, mask, to_next, to_prev, owed):
-    lane8 = lane_of(8)
-    sums = [None] * STEPS
+def owed_kernel(coefs, past, owed):
     for j in range(STEPS):
         parts = [None] * 4
         for k in range(HIST - j):
             term = coefs[j + k] * past[k]
             parts[k % 4] = term if parts[k % 4] is None else parts[k % 4] + term
-        sums[j] = (parts[0] + parts[1]) + (parts[2] + parts[3])
-        owed[j] = sums[j]
+        owed[j] = (parts[0] + parts[1]) + (parts[2] + parts[3])
+
+
+def edges_kernel(fields, pre, mask, owed, to_next, to_prev):
+    lane8 = lane_of(8)
     nxt = jnp.zeros((8, LANES), jnp.float32)
     prv = jnp.zeros((8, LANES), jnp.float32)
-    for i, plane in enumerate(sums + [pre[...], mask[...]]):
+    for i, plane in enumerate([owed[j] for j in range(STEPS)] + [pre[...], mask[...].astype(jnp.float32)]):
         here = (lane8 >= W * i) & (lane8 < W * (i + 1))
         nxt = jnp.where(here, rolled(plane, W * i - (LANES - W)), nxt)
         prv = jnp.where(here, rolled(plane, W * i), prv)
@@ -168,13 +168,11 @@
     to_next[6, 0:8, :] = nxt
     to_prev[6, 0:8, :] = prv
     lane = lane_of(NY)
-    fields = [(vel, f) for f in range(3)] + [(str_, f) for f in range(6)] + [(b, None), (lam, None), (mu, None)]
     for t in range(6):
         nxt = jnp.zeros((NY, LANES), jnp.float32)
         prv = jnp.zeros((NY, LANES), jnp.float32)
         for i in range(16):
-            ref, f = fields[2 * t + i // 8]
-            plane = ref[i % 8] if f is None else ref[f, i % 8]
+            plane = fields[2 * t + i // 8, i % 8]
             here = (lane >= W * i) & (lane < W * (i + 1))
             nxt = jnp.where(here, rolled(plane, W * i - (LANES - W)), nxt)
             prv = jnp.where(here, rolled(plane, W * i), prv)
@@ -183,7 +181,7 @@
 
 
 def move_first(refs, z, q_now=None):
-    v, s, q, m = refs
+    _, s, q, m = refs
 
     def stress(f, at):
         return (q if q_now is None else q_now)[at] if f == SXY else s[f - SXX, at]
@@ -191,7 +189,7 @@
     return velocity_change(stress, z, m[0, z - 2], ALL_V)
 
 
-def start_kernel(vel, str_, b, lam, mu, pre, mask, owed, from_prev, from_next, v, s, q, m, fp, lists, up, down):
+def start_kernel(fields, pre, mask, owed, from_prev, from_next, v, s, q, m, fp, lists, up, down):
     lane = lane_of(NY)
     lane8 = lane_of(8)
     empty = jnp.zeros((NY, EXT), jnp.float32)
@@ -199,26 +197,21 @@
     s[SYZ - SXX, 1] = empty
     s[SZZ - SXX, 10] = empty
     refs = (v, s, q, m)
-    fields = [(vel, f, f) for f in range(3)] + [(str_, i, f) for i, f in enumerate((SXX, SXY, SXZ, SYZ, SZZ, SYY))]
-    fields += [(b, None, B), (lam, None, LAM), (mu, None, MU)]
-    for k, (ref, i, f) in enumerate(fields):
+    for k, f in enumerate((VX, VY, VZ, SXX, SXY, SXZ, SYZ, SZZ, SYY, B, LAM, MU)):
         for z in range(8):
             at = (k % 2) * 8 + z
-            plane = ref[z] if i is None else ref[i, z]
             edge = jnp.where(
                 lane < LANES // 2,
                 rolled(from_next[k // 2], -W * at),
                 rolled(from_prev[k // 2], LANES - W - W * at),
             )
-            if f >= B:
-                plane, edge = DT * plane, DT * edge
             to = plane_of(refs, f, z + 2)
-            to[:, :LANES] = plane
+            to[:, :LANES] = fields[k, z]
             to[:, LANES:] = edge
     fp[...] = jnp.zeros_like(fp)
     lists[...] = jnp.zeros_like(lists)
     for i in range(STEPS + 2):
-        plane = owed[i] if i < STEPS else (pre, mask)[i - STEPS][...]
+        plane = owed[i] if i < STEPS else (pre, mask)[i - STEPS][...].astype(jnp.float32)
         edge = jnp.where(
             lane8 < LANES // 2,
             rolled(from_next[6, 0:8, :], -W * i),
@@ -233,7 +226,7 @@
             v[f, z] += change
         return carry
 
-    lax.fori_loop(2, 10, step, 0)
+    lax.fori_loop(2, 10, step, 0, unroll=4)
     pack(refs, UP_FIRST, up)
     pack(refs, DOWN_FIRST, down)
     last = tiles(UP_FIRST)
@@ -328,24 +321,22 @@
         return carry
 
     stress_a(1, s, q, edge_m[1, 0], edge_m[2, 0], (SZZ, SXZ, SYZ))
-    lax.fori_loop(2, 10, own_stress_a, 0)
+    lax.fori_loop(2, 10, own_stress_a, 0, unroll=4)
     stress_a(10, s, q, edge_m[1, 1], edge_m[2, 1], ALL_S)
     velocity_b(1, edge_m[0, 0], (VZ,))
-    lax.fori_loop(2, 10, own_velocity_b, 0)
+    lax.fori_loop(2, 10, own_velocity_b, 0, unroll=4)
     velocity_b(10, edge_m[0, 1], (VX, VY))
     rates[...] = jnp.zeros_like(rates)
     for z in range(2, 11):
         rates[z : z + 1, :] = rate_at(v, z)
-    lax.fori_loop(2, 10, own_stress_b, 0)
+    lax.fori_loop(2, 10, own_stress_b, 0, unroll=4)
     empty = jnp.zeros((NY, EXT), jnp.float32)
     s[sxz, 1] = empty
     s[syz, 1] = empty
     s[szz, 10] = empty
 
 
-def part_kernel(coefs, m, fp, lists, rates, s, v_in, q_in, v, q, sent, up, down):
-    for j in range(lists.shape[0] - 1):
-        sent[j] = lists[j + 1] + coefs[j] * rates[...]
+def part_kernel(m, fp, lists, s, v_in, q_in, v, q, up, down):
     refs = (v, s, q, m)
 
     def step(z, carry):
@@ -355,7 +346,7 @@
             v[f, z] = v_in[f, z] + change
         return carry
 
-    lax.fori_loop(2, 10, step, 0)
+    lax.fori_loop(2, 10, step, 0, unroll=4)
     pack(refs, UP, up)
     pack(refs, DOWN, down)
 
@@ -381,12 +372,11 @@
     return lax.ppermute(value, "depth", [(i, i + by) for i in range(n) if 0 <= i + by < n])
 
 
-def per_device(velocity, stress, b, lam, mu, past, coefs, pre, fault_mask):
-    mask = fault_mask.astype(jnp.float32)
+def per_device(velocity, stress, b, lam, mu, past, coefs, pre, mask):
     edge = (7, NY, LANES)
-    to_next, to_prev, owed = call(
-        edges_kernel, [edge, edge, (STEPS, 8, LANES)], [coefs, past, velocity, stress, b, lam, mu, pre, mask], smem=(0,)
-    )
+    (owed,) = call(owed_kernel, [(STEPS, 8, LANES)], [coefs, past], smem=(0,))
+    fields = jnp.concatenate([velocity, stress, DT * b[None], DT * lam[None], DT * mu[None]])
+    to_next, to_prev = call(edges_kernel, [edge, edge], [fields, pre, mask, owed])
     from_prev = along_strike(to_next, 1)
     from_next = along_strike(to_prev, -1)
     v3, s5, q1, m3 = (3, 12, NY, EXT), (5, 12, NY, EXT), (12, NY, EXT), (3, 8, NY, EXT)
@@ -394,7 +384,7 @@
     v, s, q, m, fp, lists, up, down = call(
         start_kernel,
         [v3, s5, q1, m3, (2, *plane), (STEPS, *plane), (tiles(UP_FIRST) + 1, NY, LANES), (tiles(DOWN_FIRST), NY, LANES)],
-        [velocity, stress, b, lam, mu, pre, mask, owed, from_prev, from_next],
+        [fields, pre, mask, owed, from_prev, from_next],
     )
     edge_m = m
     for step in range(0, STEPS, 2):
@@ -418,14 +408,13 @@
             {6: 0, 7: 1, 8: 2},
         )
         if step + 2 < STEPS:
-            v, q, sent, up, down = call(
+            lists = along_strike(got[1:] + coefs[: left - 1, None, None] * rates[None], 1)
+            v, q, up, down = call(
                 part_kernel,
-                [v3, q1, (left - 1, *plane), (tiles(UP), NY, LANES), (tiles(DOWN), NY, LANES)],
-                [coefs, m, fp, got, rates, s, v, q],
-                {6: 0, 7: 1},
-                smem=(0,),
+                [v3, q1, (tiles(UP), NY, LANES), (tiles(DOWN), NY, LANES)],
+                [m, fp, got, s, v, q],
+                {4: 0, 5: 1},
             )
-            lists = along_strike(sent, 1)
     return tuple(call(end_kernel, [velocity.shape, stress.shape], [fp, got, v, s, q]))
 
 

time: 112 us -> 104 us (0.929)
  Pallas kernels: 25.3 us -> 18 us
  local copies, waits for them, and re-layouts: 7.15 us -> 2.34 us
  waiting for transfers between devices: 40.7 us -> 45 us
    pallas_call x14 -> x15, Pallas kernels: 25.3 us -> 18 us  [call(): pl.pallas_call(body, out_shape=[jax.ShapeDtypeStruct(s, jnp.float32) for...]
    unnamed x26 -> x16, local copies, waits for them, and re-layouts: 7.15 us -> 2.34 us
    ppermute x9, waiting for transfers between devices: 29.4 us -> 33.7 us  [along_strike(): return lax.ppermute(value, 'strike', [(i, (i + by) % n) for i in range(n)])]
  transfers between devices with their start and end apart: 17 -> 17, of which waited for: 12 -> 12; matrix products, arithmetic and copies ran while one was open for 0% -> 0% of each run, Pallas kernels for 12% -> 9%
where the time goes in v1:
time: 104 us
  waiting for transfers between devices  45 us (43%)
  starting transfers between devices  37.2 us (36%)
  Pallas kernels  18 us (17%)
  local copies, waits for them, and re-layouts  2.34 us (2%)
    ppermute x9, waiting for transfers between devices, along_strike(): return lax.ppermute(value, 'strike', [(i, (i + by) % n) for i in range(n)])  33.7 us
    ppermute x8, starting transfers between devices, along_depth(): lax.ppermute(value, 'depth', [(i, i + by) for i in range(n) if 0 <= i + b...  30.2 us
    pallas_call x15, Pallas kernels, call(): pl.pallas_call(body, out_shape=[jax.ShapeDtypeStruct(s, jnp.float32) for...  18 us
    ppermute x8, waiting for transfers between devices, along_depth(): lax.ppermute(value, 'depth', [(i, i + by) for i in range(n) if 0 <= i + b...  11.3 us
    ppermute x9, starting transfers between devices, along_strike(): return lax.ppermute(value, 'strike', [(i, (i + by) % n) for i in range(n)])  7.07 us
    unnamed x16, local copies, waits for them, and re-layouts  2.34 us
  transfers between devices with their start and end apart: 17, of which 12 were waited for; matrix products, arithmetic and copies ran while one was open for 0% of the time, Pallas kernels for 9%

profile of v1, /device:TPU:6, one launch (start us, length us, event | category | flops | bytes accessed | tf_op | source)
XLA Modules:
  0.0 103.9 jit_solution(3515100899120862456)
XLA Ops:
  0.7 1.1 %constant_dynamic-update-slice_fusion.1 = f32[12,8,32,128]{3,2,1,0:T(8,128)S(1)} fusion(f32[3,8,32,128]{3,2,1,0:T(8,128)} %param.9), kind=kLoop, calls=%fused_computation.7 | loop fusion | bytes 786432
  1.8 1.2 %constant_dynamic-update-slice_fusion = f32[12,8,32,128]{3,2,1,0:T(8,128)S(1)} fusion(f32[12,8,32,128]{3,2,1,0:T(8,128)S(1)} %constant_dynamic-update-slice_fusion.1, f32[6,8,32,128]{3,2,1,0:T(8,128)} %param.10), kind=kLoop, calls=%fused_computation.6 | loop fusion | bytes 1572864
  3.1 0.7 shard_map.104.owed
  3.9 0.9 shard_map.105
  4.8 0.1 collective-permute-start
  4.9 6.4 %collective-permute-start.1 = (f32[7,32,128]{2,1,0:T(8,128)S(1)}, f32[7,32,128]{2,1,0:T(8,128)S(1)}, u32[]{:S(2)}, u32[]{:S(2)}) collective-permute-start(f32[7,32,128]{2,1,0:T(8,128)S(1)} %get-tuple-element.44), channel_id=1, source_target_pairs={{0,248},{8,0},{16,8},{24,16},{32,24},{40,32},{48,40},{56,48},{64,5... | collective-permute-start | bytes 344072 | tf_op jit(solution)/shard_map/ppermute | solution.py:367
  11.3 2.4 %collective-permute-done.from_prev = f32[7,32,128]{2,1,0:T(8,128)S(1)} collective-permute-done((f32[7,32,128]{2,1,0:T(8,128)S(1)}, f32[7,32,128]{2,1,0:T(8,128)S(1)}, u32[]{:S(2)}, u32[]{:S(2)}) %collective-permute-start) | collective-permute-done | bytes 114720 | tf_op jit(solution)/shard_map/ppermute | solution.py:367
  13.6 1.6 %shard_map.106 = (f32[3,12,32,256]{3,2,1,0:T(8,128)S(1)}, f32[5,12,32,256]{3,2,1,0:T(8,128)S(1)}, f32[12,32,256]{2,1,0:T(8,128)S(1)}, f32[3,8,32,256]{3,2,1,0:T(...) custom-call(f32[12,8,32,128]{3,2,1,0:T(8,128)S(1)} %bitcast_dynamic-, ...), custom_call_target="tpu_custom_call" | custom-call | flops 4000000 | bytes 4000000 | tf_op jit(solution)/shard_map/pallas_call | solution.py:38
  15.2 5.1 %collective-permute-start.2 = (f32[17,32,128]{2,1,0:T(8,128)S(1)}, f32[17,32,128]{2,1,0:T(8,128)S(1)}, u32[]{:S(2)}, u32[]{:S(2)}) collective-permute-start(f32[17,32,128]{2,1,0:T(8,128)S(1)} %get-tuple-element.45), channel_id=1, source_target_pairs={{1,0},{2,1},{3,2},{4,3},{5,4},{6,5},{7,6},{9,8},{10,9},{11,10},{12... | collective-permute-start | bytes 835592 | tf_op jit(solution)/shard_map/ppermute | solution.py:372
  20.3 2.3 %collective-permute-start.3 = (f32[12,32,128]{2,1,0:T(8,128)S(1)}, f32[12,32,128]{2,1,0:T(8,128)S(1)}, u32[]{:S(2)}, u32[]{:S(2)}) collective-permute-start(f32[12,32,128]{2,1,0:T(8,128)S(1)} %get-tuple-element.46), channel_id=1, source_target_pairs={{0,1},{1,2},{2,3},{3,4},{4,5},{5,6},{6,7},{8,9},{9,10},{10,11},{11... | collective-permute-start | bytes 589832 | tf_op jit(solution)/shard_map/ppermute | solution.py:372
  22.6 7.7 %collective-permute-done.3.got_down = f32[12,32,128]{2,1,0:T(8,128)S(1)} collective-permute-done((f32[12,32,128]{2,1,0:T(8,128)S(1)}, f32[12,32,128]{2,1,0:T(8,128)S(1)}, u32[]{:S(2)}, u32[]{:S(2)}) %collective-permute-start.3) | collective-permute-done | bytes 196640 | tf_op jit(solution)/shard_map/ppermute | solution.py:372
  30.3 0.6 shard_map.107
  30.9 0.1 collective-permute-start.4
  31.0 2.1 %shard_map.108 = (f32[3,12,32,256]{3,2,1,0:T(8,128)S(1)}, f32[5,12,32,256]{3,2,1,0:T(8,128)S(1)}, f32[12,32,256]{2,1,0:T(8,128)S(1)}, f32[16,256]{1,0:T(8,128)S(1)}) custom-call(f32[3,8,32,256]{3,2,1,0:T(8,128)S(1)} %get-tuple-element.49.m.edge_m, ...), custom_call_target="tpu_custom_call", output_to_operand_aliasing={{0}: (6, {}), {1}: (7, {}), {2}: (8, {})} | custom-call | flops 4000000 | bytes 4000000 | tf_op jit(solution)/shard_map/pallas_call | solution.py:38
  33.2 4.2 %collective-permute-done.4.lists = f32[7,16,256]{2,1,0:T(8,128)S(1)} collective-permute-done((f32[7,16,256]{2,1,0:T(8,128)S(1)}, f32[7,16,256]{2,1,0:T(8,128)S(1)}, u32[]{:S(2)}, u32[]{:S(2)}) %collective-permute-start.4) | collective-permute-done | bytes 114720 | tf_op jit(solution)/shard_map/ppermute | solution.py:367
  37.3 0.7 shard_map.109
  38.0 6.2 %collective-permute-start.5 = (f32[13,32,128]{2,1,0:T(8,128)S(1)}, f32[13,32,128]{2,1,0:T(8,128)S(1)}, u32[]{:S(2)}, u32[]{:S(2)}) collective-permute-start(f32[13,32,128]{2,1,0:T(8,128)S(1)} %get-tuple-element.60), channel_id=1, source_target_pairs={{1,0},{2,1},{3,2},{4,3},{5,4},{6,5},{7,6},{9,8},{10,9},{11,10},{12... | collective-permute-start | bytes 638984 | tf_op jit(solution)/shard_map/ppermute | solution.py:372
  44.2 1.9 %collective-permute-start.6 = (f32[8,32,128]{2,1,0:T(8,128)S(1)}, f32[8,32,128]{2,1,0:T(8,128)S(1)}, u32[]{:S(2)}, u32[]{:S(2)}) collective-permute-start(f32[8,32,128]{2,1,0:T(8,128)S(1)} %get-tuple-element.61), channel_id=1, source_target_pairs={{0,1},{1,2},{2,3},{3,4},{4,5},{5,6},{6,7},{8,9},{9,10},{10,11},{11... | collective-permute-start | bytes 393224 | tf_op jit(solution)/shard_map/ppermute | solution.py:372
  46.1 0.1 slice_add_fusion
  46.2 0.1 collective-permute-start.7
  46.3 6.1 %collective-permute-done.7.lists = f32[6,16,256]{2,1,0:T(8,128)S(1)} collective-permute-done((f32[6,16,256]{2,1,0:T(8,128)S(1)}, f32[6,16,256]{2,1,0:T(8,128)S(1)}, u32[]{:S(2)}, u32[]{:S(2)}) %collective-permute-start.7) | collective-permute-done | bytes 98336 | tf_op jit(solution)/shard_map/ppermute | solution.py:367
  52.4 1.0 collective-permute-done.6.got_down
  53.5 0.6 shard_map.110
  54.1 0.1 collective-permute-start.8
  54.2 2.1 %shard_map.111 = (f32[3,12,32,256]{3,2,1,0:T(8,128)S(1)}, f32[5,12,32,256]{3,2,1,0:T(8,128)S(1)}, f32[12,32,256]{2,1,0:T(8,128)S(1)}, f32[16,256]{1,0:T(8,128)S(1)}) custom-call(f32[3,8,32,256]{3,2,1,0:T(8,128)S(1)} %get-tuple-element.49.m.edge_m, ...), custom_call_target="tpu_custom_call", output_to_operand_aliasing={{0}: (6, {}), {1}: (7, {}), {2}: (8, {})} | custom-call | flops 4000000 | bytes 4000000 | tf_op jit(solution)/shard_map/pallas_call | solution.py:38
  56.3 3.8 %collective-permute-done.8.lists = f32[5,16,256]{2,1,0:T(8,128)S(1)} collective-permute-done((f32[5,16,256]{2,1,0:T(8,128)S(1)}, f32[5,16,256]{2,1,0:T(8,128)S(1)}, u32[]{:S(2)}, u32[]{:S(2)}) %collective-permute-start.8) | collective-permute-done | bytes 81952 | tf_op jit(solution)/shard_map/ppermute | solution.py:367
  60.1 0.7 shard_map.112
  60.8 5.4 %collective-permute-start.9 = (f32[13,32,128]{2,1,0:T(8,128)S(1)}, f32[13,32,128]{2,1,0:T(8,128)S(1)}, u32[]{:S(2)}, u32[]{:S(2)}) collective-permute-start(f32[13,32,128]{2,1,0:T(8,128)S(1)} %get-tuple-element.68), channel_id=1, source_target_pairs={{1,0},{2,1},{3,2},{4,3},{5,4},{6,5},{7,6},{9,8},{10,9},{11,10},{12... | collective-permute-start | bytes 638984 | tf_op jit(solution)/shard_map/ppermute | solution.py:372
  66.2 2.0 %collective-permute-start.10 = (f32[8,32,128]{2,1,0:T(8,128)S(1)}, f32[8,32,128]{2,1,0:T(8,128)S(1)}, u32[]{:S(2)}, u32[]{:S(2)}) collective-permute-start(f32[8,32,128]{2,1,0:T(8,128)S(1)} %get-tuple-element.69), channel_id=1, source_target_pairs={{0,1},{1,2},{2,3},{3,4},{4,5},{5,6},{6,7},{8,9},{9,10},{10,11},{11... | collective-permute-start | bytes 393224 | tf_op jit(solution)/shard_map/ppermute | solution.py:372
  68.2 0.1 slice_add_fusion.1
  68.3 0.0 collective-permute-start.11
  68.3 5.8 %collective-permute-done.11.lists = f32[4,16,256]{2,1,0:T(8,128)S(1)} collective-permute-done((f32[4,16,256]{2,1,0:T(8,128)S(1)}, f32[4,16,256]{2,1,0:T(8,128)S(1)}, u32[]{:S(2)}, u32[]{:S(2)}) %collective-permute-start.11) | collective-permute-done | bytes 65568 | tf_op jit(solution)/shard_map/ppermute | solution.py:367
  74.1 1.4 %collective-permute-done.10.got_down = f32[8,32,128]{2,1,0:T(8,128)S(1)} collective-permute-done((f32[8,32,128]{2,1,0:T(8,128)S(1)}, f32[8,32,128]{2,1,0:T(8,128)S(1)}, u32[]{:S(2)}, u32[]{:S(2)}) %collective-permute-start.10) | collective-permute-done | bytes 131104 | tf_op jit(solution)/shard_map/ppermute | solution.py:372
  75.5 0.6 shard_map.113
  76.1 0.3 collective-permute-start.12
  76.4 2.1 %shard_map.114 = (f32[3,12,32,256]{3,2,1,0:T(8,128)S(1)}, f32[5,12,32,256]{3,2,1,0:T(8,128)S(1)}, f32[12,32,256]{2,1,0:T(8,128)S(1)}, f32[16,256]{1,0:T(8,128)S(1)}) custom-call(f32[3,8,32,256]{3,2,1,0:T(8,128)S(1)} %get-tuple-element.49.m.edge_m, ...), custom_call_target="tpu_custom_call", output_to_operand_aliasing={{0}: (6, {}), {1}: (7, {}), {2}: (8, {})} | custom-call | flops 4000000 | bytes 4000000 | tf_op jit(solution)/shard_map/pallas_call | solution.py:38
  78.5 3.5 %collective-permute-done.12.lists = f32[3,16,256]{2,1,0:T(8,128)S(1)} collective-permute-done((f32[3,16,256]{2,1,0:T(8,128)S(1)}, f32[3,16,256]{2,1,0:T(8,128)S(1)}, u32[]{:S(2)}, u32[]{:S(2)}) %collective-permute-start.12) | collective-permute-done | bytes 49184 | tf_op jit(solution)/shard_map/ppermute | solution.py:367
  82.0 0.7 shard_map.115
  82.7 4.9 %collective-permute-start.13 = (f32[13,32,128]{2,1,0:T(8,128)S(1)}, f32[13,32,128]{2,1,0:T(8,128)S(1)}, u32[]{:S(2)}, u32[]{:S(2)}) collective-permute-start(f32[13,32,128]{2,1,0:T(8,128)S(1)} %get-tuple-element.76), channel_id=1, source_target_pairs={{1,0},{2,1},{3,2},{4,3},{5,4},{6,5},{7,6},{9,8},{10,9},{11,10},{12... | collective-permute-start | bytes 638984 | tf_op jit(solution)/shard_map/ppermute | solution.py:372
  87.6 2.5 %collective-permute-start.14 = (f32[8,32,128]{2,1,0:T(8,128)S(1)}, f32[8,32,128]{2,1,0:T(8,128)S(1)}, u32[]{:S(2)}, u32[]{:S(2)}) collective-permute-start(f32[8,32,128]{2,1,0:T(8,128)S(1)} %get-tuple-element.77), channel_id=1, source_target_pairs={{0,1},{1,2},{2,3},{3,4},{4,5},{5,6},{6,7},{8,9},{9,10},{10,11},{11... | collective-permute-start | bytes 393224 | tf_op jit(solution)/shard_map/ppermute | solution.py:372
  90.0 0.1 slice_add_fusion.2
  90.2 5.4 %collective-permute-done.15.lists = f32[2,16,256]{2,1,0:T(8,128)S(1)} collective-permute-done((f32[2,16,256]{2,1,0:T(8,128)S(1)}, f32[2,16,256]{2,1,0:T(8,128)S(1)}, u32[]{:S(2)}, u32[]{:S(2)}) %collective-permute-start.15) | collective-permute-done | bytes 32800 | tf_op jit(solution)/shard_map/ppermute | solution.py:367
  95.6 1.2 %collective-permute-done.14.got_down = f32[8,32,128]{2,1,0:T(8,128)S(1)} collective-permute-done((f32[8,32,128]{2,1,0:T(8,128)S(1)}, f32[8,32,128]{2,1,0:T(8,128)S(1)}, u32[]{:S(2)}, u32[]{:S(2)}) %collective-permute-start.14) | collective-permute-done | bytes 131104 | tf_op jit(solution)/shard_map/ppermute | solution.py:372
  96.8 0.6 shard_map.116
  97.5 0.0 collective-permute-start.16
  97.5 2.7 %shard_map.117 = (f32[3,12,32,256]{3,2,1,0:T(8,128)S(1)}, f32[5,12,32,256]{3,2,1,0:T(8,128)S(1)}, f32[12,32,256]{2,1,0:T(8,128)S(1)}, f32[16,256]{1,0:T(8,128)}) custom-call(f32[3,8,32,256]{3,2,1,0:T(8,128)S(1)} %get-tuple-element.49.m.edge_m, ...), custom_call_target="tpu_custom_call", output_to_operand_aliasing={{0}: (6, {}), {1}: (7, {}), {2}: (8, {})} | custom-call | flops 4000000 | bytes 4000000 | tf_op jit(solution)/shard_map/pallas_call | solution.py:38
  100.3 2.5 %collective-permute-done.16.lists = f32[1,16,256]{2,1,0:T(8,128)S(1)} collective-permute-done((f32[1,16,256]{2,1,0:T(8,128)S(1)}, f32[1,16,256]{2,1,0:T(8,128)S(1)}, u32[]{:S(2)}, u32[]{:S(2)}) %collective-permute-start.16) | collective-permute-done | bytes 16416 | tf_op jit(solution)/shard_map/ppermute | solution.py:367
  102.8 1.1 %shard_map.118 = (f32[3,8,32,128]{3,2,1,0:T(8,128)}, f32[6,8,32,128]{3,2,1,0:T(8,128)}) custom-call(f32[2,16,256]{2,1,0:T(8,128)S(1)} %get-tuple-element.52.fp, f32[1,16,256]{2,1,0:T(8,128)S(1)} %collective-permute-done.16.lists, f32[3,12,32,256]{3,2,1,0:T(8,128)S(1)} %get-tuple-element.81.v, f32[5,12,32,256]{3,2,1,0:T(8,128)S(1)} %get-tuple-element.82.s, ...), custom_call_target="tpu_custom_call" | custom-call | flops 4000000 | bytes 4000000 | tf_op jit(solution)/shard_map/pallas_call | solution.py:38
  (23 shorter events, 0.1 us)
Async XLA Ops:
  0.6 2.4 %copy-start.4 = (f32[8,32,128]{2,1,0:T(8,128)S(1)}, f32[8,32,128]{2,1,0:T(8,128)}, u32[]{:S(2)}) copy-start(f32[8,32,128]{2,1,0:T(8,128)} %param.11) | copy-start | bytes 393220
  0.6 2.4 %copy-start.5 = (f32[8,32,128]{2,1,0:T(8,128)S(1)}, f32[8,32,128]{2,1,0:T(8,128)}, u32[]{:S(2)}) copy-start(f32[8,32,128]{2,1,0:T(8,128)} %param.12) | copy-start | bytes 393220
  0.7 2.4 %copy-start.6 = (f32[8,32,128]{2,1,0:T(8,128)S(1)}, f32[8,32,128]{2,1,0:T(8,128)}, u32[]{:S(2)}) copy-start(f32[8,32,128]{2,1,0:T(8,128)} %param.13) | copy-start | bytes 393220
  0.7 2.5 %copy-start.1 = (f32[64]{0:T(128)S(1)}, f32[64]{0:T(128)}, u32[]{:S(2)}) copy-start(f32[64]{0:T(128)} %coefs.9) | copy-start | bytes 772
  0.7 2.5 %copy-start = (f32[64,8,128]{2,1,0:T(8,128)S(1)}, f32[64,8,128]{2,1,0:T(8,128)}, u32[]{:S(2)}) copy-start(f32[64,8,128]{2,1,0:T(8,128)} %past.1) | copy-start | bytes 786436
  0.7 3.2 %copy-start.2 = (f32[8,128]{1,0:T(8,128)S(1)}, f32[8,128]{1,0:T(8,128)}, u32[]{:S(2)}) copy-start(f32[8,128]{1,0:T(8,128)} %pre.3) | copy-start | bytes 12292
  0.7 3.2 %copy-start.3 = (s32[8,128]{1,0:T(8,128)S(1)}, s32[8,128]{1,0:T(8,128)}, u32[]{:S(2)}) copy-start(s32[8,128]{1,0:T(8,128)} %mask.3) | copy-start | bytes 12292
  4.8 8.9 %collective-permute-start = (f32[7,32,128]{2,1,0:T(8,128)S(1)}, f32[7,32,128]{2,1,0:T(8,128)S(1)}, u32[]{:S(2)}, u32[]{:S(2)}) collective-permute-start(f32[7,32,128]{2,1,0:T(8,128)S(1)} %get-tuple-element.43), channel_id=1, source_target_pairs={{0,8},{8,16},{16,24},{24,32},{32,40},{40,48},{48,56},{56,64},{64,7... | collective-permute-start | bytes 344072 | tf_op jit(solution)/shard_map/ppermute | solution.py:367
  4.9 8.8 %collective-permute-start.1 = (f32[7,32,128]{2,1,0:T(8,128)S(1)}, f32[7,32,128]{2,1,0:T(8,128)S(1)}, u32[]{:S(2)}, u32[]{:S(2)}) collective-permute-start(f32[7,32,128]{2,1,0:T(8,128)S(1)} %get-tuple-element.44), channel_id=1, source_target_pairs={{0,248},{8,0},{16,8},{24,16},{32,24},{40,32},{48,40},{56,48},{64,5... | collective-permute-start | bytes 344072 | tf_op jit(solution)/shard_map/ppermute | solution.py:367
  15.2 15.1 %collective-permute-start.2 = (f32[17,32,128]{2,1,0:T(8,128)S(1)}, f32[17,32,128]{2,1,0:T(8,128)S(1)}, u32[]{:S(2)}, u32[]{:S(2)}) collective-permute-start(f32[17,32,128]{2,1,0:T(8,128)S(1)} %get-tuple-element.45), channel_id=1, source_target_pairs={{1,0},{2,1},{3,2},{4,3},{5,4},{6,5},{7,6},{9,8},{10,9},{11,10},{12... | collective-permute-start | bytes 835592 | tf_op jit(solution)/shard_map/ppermute | solution.py:372
  20.3 10.0 %collective-permute-start.3 = (f32[12,32,128]{2,1,0:T(8,128)S(1)}, f32[12,32,128]{2,1,0:T(8,128)S(1)}, u32[]{:S(2)}, u32[]{:S(2)}) collective-permute-start(f32[12,32,128]{2,1,0:T(8,128)S(1)} %get-tuple-element.46), channel_id=1, source_target_pairs={{0,1},{1,2},{2,3},{3,4},{4,5},{5,6},{6,7},{8,9},{9,10},{10,11},{11... | collective-permute-start | bytes 589832 | tf_op jit(solution)/shard_map/ppermute | solution.py:372
  30.9 6.4 %collective-permute-start.4 = (f32[7,16,256]{2,1,0:T(8,128)S(1)}, f32[7,16,256]{2,1,0:T(8,128)S(1)}, u32[]{:S(2)}, u32[]{:S(2)}) collective-permute-start(f32[7,16,256]{2,1,0:T(8,128)S(1)} %get-tuple-element.53), channel_id=1, source_target_pairs={{0,8},{8,16},{16,24},{24,32},{32,40},{40,48},{48,56},{56,64},{64,7... | collective-permute-start | bytes 344072 | tf_op jit(solution)/shard_map/ppermute | solution.py:367
  38.0 15.4 %collective-permute-start.5 = (f32[13,32,128]{2,1,0:T(8,128)S(1)}, f32[13,32,128]{2,1,0:T(8,128)S(1)}, u32[]{:S(2)}, u32[]{:S(2)}) collective-permute-start(f32[13,32,128]{2,1,0:T(8,128)S(1)} %get-tuple-element.60), channel_id=1, source_target_pairs={{1,0},{2,1},{3,2},{4,3},{5,4},{6,5},{7,6},{9,8},{10,9},{11,10},{12... | collective-permute-start | bytes 638984 | tf_op jit(solution)/shard_map/ppermute | solution.py:372
  44.2 9.3 %collective-permute-start.6 = (f32[8,32,128]{2,1,0:T(8,128)S(1)}, f32[8,32,128]{2,1,0:T(8,128)S(1)}, u32[]{:S(2)}, u32[]{:S(2)}) collective-permute-start(f32[8,32,128]{2,1,0:T(8,128)S(1)} %get-tuple-element.61), channel_id=1, source_target_pairs={{0,1},{1,2},{2,3},{3,4},{4,5},{5,6},{6,7},{8,9},{9,10},{10,11},{11... | collective-permute-start | bytes 393224 | tf_op jit(solution)/shard_map/ppermute | solution.py:372
  46.2 6.2 %collective-permute-start.7 = (f32[6,16,256]{2,1,0:T(8,128)S(1)}, f32[6,16,256]{2,1,0:T(8,128)S(1)}, u32[]{:S(2)}, u32[]{:S(2)}) collective-permute-start(f32[6,16,256]{2,1,0:T(8,128)S(1)} %slice_add_fusion), channel_id=1, source_target_pairs={{0,8},{8,16},{16,24},{24,32},{32,40},{40,48},{48,56},{56,64},{64,7... | collective-permute-start | bytes 294920 | tf_op jit(solution)/shard_map/ppermute | solution.py:367
  54.1 6.1 %collective-permute-start.8 = (f32[5,16,256]{2,1,0:T(8,128)S(1)}, f32[5,16,256]{2,1,0:T(8,128)S(1)}, u32[]{:S(2)}, u32[]{:S(2)}) collective-permute-start(f32[5,16,256]{2,1,0:T(8,128)S(1)} %shard_map.110), channel_id=1, source_target_pairs={{0,8},{8,16},{16,24},{24,32},{32,40},{40,48},{48,56},{56,64},{64,7... | collective-permute-start | bytes 245768 | tf_op jit(solution)/shard_map/ppermute | solution.py:367
  60.8 14.6 %collective-permute-start.9 = (f32[13,32,128]{2,1,0:T(8,128)S(1)}, f32[13,32,128]{2,1,0:T(8,128)S(1)}, u32[]{:S(2)}, u32[]{:S(2)}) collective-permute-start(f32[13,32,128]{2,1,0:T(8,128)S(1)} %get-tuple-element.68), channel_id=1, source_target_pairs={{1,0},{2,1},{3,2},{4,3},{5,4},{6,5},{7,6},{9,8},{10,9},{11,10},{12... | collective-permute-start | bytes 638984 | tf_op jit(solution)/shard_map/ppermute | solution.py:372
  66.2 9.3 %collective-permute-start.10 = (f32[8,32,128]{2,1,0:T(8,128)S(1)}, f32[8,32,128]{2,1,0:T(8,128)S(1)}, u32[]{:S(2)}, u32[]{:S(2)}) collective-permute-start(f32[8,32,128]{2,1,0:T(8,128)S(1)} %get-tuple-element.69), channel_id=1, source_target_pairs={{0,1},{1,2},{2,3},{3,4},{4,5},{5,6},{6,7},{8,9},{9,10},{10,11},{11... | collective-permute-start | bytes 393224 | tf_op jit(solution)/shard_map/ppermute | solution.py:372
  68.3 5.8 %collective-permute-start.11 = (f32[4,16,256]{2,1,0:T(8,128)S(1)}, f32[4,16,256]{2,1,0:T(8,128)S(1)}, u32[]{:S(2)}, u32[]{:S(2)}) collective-permute-start(f32[4,16,256]{2,1,0:T(8,128)S(1)} %slice_add_fusion.1), channel_id=1, source_target_pairs={{0,8},{8,16},{16,24},{24,32},{32,40},{40,48},{48,56},{56,64},{64,7... | collective-permute-start | bytes 196616 | tf_op jit(solution)/shard_map/ppermute | solution.py:367
  76.1 5.9 %collective-permute-start.12 = (f32[3,16,256]{2,1,0:T(8,128)S(1)}, f32[3,16,256]{2,1,0:T(8,128)S(1)}, u32[]{:S(2)}, u32[]{:S(2)}) collective-permute-start(f32[3,16,256]{2,1,0:T(8,128)S(1)} %shard_map.113), channel_id=1, source_target_pairs={{0,8},{8,16},{16,24},{24,32},{32,40},{40,48},{48,56},{56,64},{64,7... | collective-permute-start | bytes 147464 | tf_op jit(solution)/shard_map/ppermute | solution.py:367
  82.7 14.2 %collective-permute-start.13 = (f32[13,32,128]{2,1,0:T(8,128)S(1)}, f32[13,32,128]{2,1,0:T(8,128)S(1)}, u32[]{:S(2)}, u32[]{:S(2)}) collective-permute-start(f32[13,32,128]{2,1,0:T(8,128)S(1)} %get-tuple-element.76), channel_id=1, source_target_pairs={{1,0},{2,1},{3,2},{4,3},{5,4},{6,5},{7,6},{9,8},{10,9},{11,10},{12... | collective-permute-start | bytes 638984 | tf_op jit(solution)/shard_map/ppermute | solution.py:372
  87.6 9.3 %collective-permute-start.14 = (f32[8,32,128]{2,1,0:T(8,128)S(1)}, f32[8,32,128]{2,1,0:T(8,128)S(1)}, u32[]{:S(2)}, u32[]{:S(2)}) collective-permute-start(f32[8,32,128]{2,1,0:T(8,128)S(1)} %get-tuple-element.77), channel_id=1, source_target_pairs={{0,1},{1,2},{2,3},{3,4},{4,5},{5,6},{6,7},{8,9},{9,10},{10,11},{11... | collective-permute-start | bytes 393224 | tf_op jit(solution)/shard_map/ppermute | solution.py:372
  90.1 5.5 %collective-permute-start.15 = (f32[2,16,256]{2,1,0:T(8,128)S(1)}, f32[2,16,256]{2,1,0:T(8,128)S(1)}, u32[]{:S(2)}, u32[]{:S(2)}) collective-permute-start(f32[2,16,256]{2,1,0:T(8,128)S(1)} %slice_add_fusion.2), channel_id=1, source_target_pairs={{0,8},{8,16},{16,24},{24,32},{32,40},{40,48},{48,56},{56,64},{64,7... | collective-permute-start | bytes 98312 | tf_op jit(solution)/shard_map/ppermute | solution.py:367
  97.5 5.3 %collective-permute-start.16 = (f32[1,16,256]{2,1,0:T(8,128)S(1)}, f32[1,16,256]{2,1,0:T(8,128)S(1)}, u32[]{:S(2)}, u32[]{:S(2)}) collective-permute-start(f32[1,16,256]{2,1,0:T(8,128)S(1)} %shard_map.116), channel_id=1, source_target_pairs={{0,8},{8,16},{16,24},{24,32},{32,40},{40,48},{48,56},{56,64},{64,7... | collective-permute-start | bytes 49160 | tf_op jit(solution)/shard_map/ppermute | solution.py:367

commit v2 on v1

--- a/solution.py
+++ b/solution.py
@@ -24,22 +24,19 @@
 
 VX, VY, VZ, SXX, SXZ, SYZ, SZZ, SYY, SXY, B, LAM, MU = range(12)
 
-UP = ((VX, 2), (VX, 3), (VY, 2), (VY, 3), (VZ, 2), (SXX, 2), (SXZ, 2), (SYZ, 2), (SZZ, 2), (SYY, 2), (SXY, 2))
-DOWN = ((VX, 9), (VY, 9), (VZ, 8), (VZ, 9), (SXZ, 9), (SYZ, 9), (SZZ, 9))
-UP_FIRST = UP + ((B, 2), (LAM, 2), (MU, 2))
-DOWN_FIRST = DOWN + ((B, 9), (LAM, 9), (MU, 9))
-
-
-def tiles(planes):
-    return len(planes) + -(-len(planes) // 8)
-
-
-def call(body, outs, ins, aliases=None, smem=()):
+TRACES = 6
+TILES = TRACES + 1
+FIRST = TRACES + 3
+FIRST_TILES = FIRST + 3
+
+
+def call(body, outs, ins, aliases=None, smem=(), scratch=()):
     return pl.pallas_call(
         body,
         out_shape=[jax.ShapeDtypeStruct(s, jnp.float32) for s in outs],
         in_specs=[SMEM if i in smem else VMEM for i in range(len(ins))],
         out_specs=[VMEM] * len(outs),
+        scratch_shapes=scratch,
         input_output_aliases=aliases or {},
         compiler_params=pltpu.CompilerParams(vmem_limit_bytes=32 * 1024 * 1024),
         cost_estimate=pl.CostEstimate(flops=4_000_000, bytes_accessed=4_000_000, transcendentals=0),
@@ -98,11 +95,11 @@
     return out
 
 
-def stress_change(v, z, lam, mu, want):
-    vx, vy, vz = v[VX, z], v[VY, z], v[VZ, z]
+def stress_change(velocity, z, lam, mu, want):
+    vx, vy, vz = velocity(VX, z), velocity(VY, z), velocity(VZ, z)
     ex = vx - behind_x(vx)
     ey = vy - behind_y(vy)
-    ez = vz - v[VZ, z - 1]
+    ez = vz - velocity(VZ, z - 1)
     spread = lam * (ex + ey + ez)
     twice = mu + mu
     out = {}
@@ -111,8 +108,8 @@
         out[SYY] = spread + twice * ey
         out[SXY] = mu * ((ahead_y(vx) - vx) + (ahead_x(vy) - vy))
     out[SZZ] = spread + twice * ez
-    out[SXZ] = mu * ((v[VX, z + 1] - vx) + (ahead_x(vz) - vz))
-    out[SYZ] = mu * ((v[VY, z + 1] - vy) + (ahead_y(vz) - vz))
+    out[SXZ] = mu * ((velocity(VX, z + 1) - vx) + (ahead_x(vz) - vz))
+    out[SYZ] = mu * ((velocity(VY, z + 1) - vy) + (ahead_y(vz) - vz))
     return out
 
 
@@ -129,21 +126,69 @@
     q[z, Y0 : Y0 + 1, :] = jnp.where(slides, traction, q[z, Y0 : Y0 + 1, :])
 
 
-def pack(refs, planes, out):
+def slid(plane, fp, z, traction):
+    row = lax.broadcasted_iota(jnp.int32, plane.shape, 0)
+    return jnp.where((row == Y0) & (fp[1, z : z + 1, :] > 0.5), traction, plane)
+
+
+def packed(planes):
     lane = lane_of(NY)
+    out = [plane[:, :LANES] for plane in planes]
     for first in range(0, len(planes), 8):
         edges = jnp.zeros((NY, LANES), jnp.float32)
-        for i, (f, z) in enumerate(planes[first : first + 8]):
-            ref = plane_of(refs, f, z)
-            out[first + i] = ref[:, :LANES]
-            moved = rolled(ref[:, LANES:], W + 2 * W * i)
+        for i, plane in enumerate(planes[first : first + 8]):
+            moved = rolled(plane[:, LANES:], W + 2 * W * i)
             edges = jnp.where((lane >= 2 * W * i) & (lane < 2 * W * (i + 1)), moved, edges)
-        out[len(planes) + first // 8] = edges
-
-
-def unpacked(got, planes, i, rows=slice(None)):
-    edges = got[len(planes) + i // 8, rows, :]
-    return jnp.concatenate([got[i, rows, :], rolled(edges, -(W + 2 * W * (i % 8)))], axis=1)
+        out.append(edges)
+    return out
+
+
+def even_depth():
+    return lax.axis_index("depth") % 2 == 0
+
+
+def post(up, down, one, two):
+    even = even_depth()
+    for i, (u, d) in enumerate(zip(up, down, strict=True)):
+        one[i] = jnp.where(even, d, u)
+        two[i] = jnp.where(even, u, d)
+
+
+class Got:
+    def __init__(self, one, two, count):
+        self.one, self.two, self.count, self.even = one, two, count, even_depth()
+
+    def tile(self, above, i, rows):
+        first, second = (self.one, self.two) if above else (self.two, self.one)
+        return jnp.where(self.even, first[i, rows, :], second[i, rows, :])
+
+    def plane(self, above, i, rows=slice(None)):
+        edges = self.tile(above, self.count + i // 8, rows)
+        return jnp.concatenate([self.tile(above, i, rows), rolled(edges, -(W + 2 * W * (i % 8)))], axis=1)
+
+
+def traces(refs, fp):
+    v, s, q, m = refs
+    nothing = jnp.zeros((NY, EXT), jnp.float32)
+
+    def alone(f, z):
+        return v[f, z] if 2 <= z < 10 else nothing
+
+    def before(f, z):
+        return q[z] if f == SXY else s[f - SXX, z]
+
+    def carried(z, want_s, want_v):
+        now = {f: before(f, z) + c for f, c in stress_change(alone, z, m[1, z - 2], m[2, z - 2], want_s).items()}
+        if SXY in now:
+            now[SXY] = slid(now[SXY], fp, z, fp[0, z : z + 1, :] + FRIC * rate_at(v, z))
+        change = velocity_change(lambda f, at: now.get(f, nothing) if at == z else nothing, z, m[0, z - 2], want_v)
+        return now, {f: v[f, z] + c for f, c in change.items()}
+
+    now, then = carried(2, ALL_S, (VX, VY))
+    up = [v[VX, 2], v[VY, 2], before(SZZ, 2), now[SZZ], then[VX], then[VY]]
+    now, then = carried(9, (SZZ, SXZ, SYZ), (VZ,))
+    down = [before(SXZ, 9), before(SYZ, 9), v[VZ, 9], now[SXZ], now[SYZ], then[VZ]]
+    return up, down
 
 
 def owed_kernel(coefs, past, owed):
@@ -189,7 +234,7 @@
     return velocity_change(stress, z, m[0, z - 2], ALL_V)
 
 
-def start_kernel(fields, pre, mask, owed, from_prev, from_next, v, s, q, m, fp, lists, up, down):
+def start_kernel(fields, pre, mask, owed, from_prev, from_next, v, s, q, m, fp, lists, one, two):
     lane = lane_of(NY)
     lane8 = lane_of(8)
     empty = jnp.zeros((NY, EXT), jnp.float32)
@@ -227,92 +272,110 @@
         return carry
 
     lax.fori_loop(2, 10, step, 0, unroll=4)
-    pack(refs, UP_FIRST, up)
-    pack(refs, DOWN_FIRST, down)
-    last = tiles(UP_FIRST)
-    up[last] = jnp.zeros((NY, LANES), jnp.float32)
+    up, down = traces(refs, fp)
+    up = packed(up + [m[k, 0] for k in range(3)])
+    down = packed(down + [m[k, 7] for k in range(3)])
+    post(up, down, one, two)
+    last = len(up)
+    one[last] = jnp.zeros((NY, LANES), jnp.float32)
+    two[last] = jnp.zeros((NY, LANES), jnp.float32)
     for i in range(STEPS + 2):
         to, j = (lists, i) if i < STEPS else (fp, i - STEPS)
-        up[last, i : i + 1, :] = to[j, 2:3, :LANES]
-        up[last, 16 + i : 17 + i, :] = to[j, 2:3, LANES:]
-
-
-def meet_kernel(first, coefs, got_up, got_down, v, s, m, edge_m, fp, lists, sent, *more):
-    up, down = (UP_FIRST, DOWN_FIRST) if first else (UP, DOWN)
+        for out in (one, two):
+            out[last, i : i + 1, :] = to[j, 2:3, :LANES]
+            out[last, 16 + i : 17 + i, :] = to[j, 2:3, LANES:]
+
+
+def meet_kernel(first, coefs, one, two, v, s, m, edge_m, fp, lists, sent, *more):
+    *more, rates = more
+    got = Got(one, two, FIRST if first else TRACES)
     if first:
         edge_out, fp_out, lists_out = more
         for k in range(3):
-            edge_out[k, 0] = unpacked(got_down, down, down.index((B + k, 9)))
-            edge_out[k, 1] = unpacked(got_up, up, up.index((B + k, 2)))
+            edge_out[k, 0] = got.plane(False, TRACES + k)
+            edge_out[k, 1] = got.plane(True, TRACES + k)
         fp_out[...] = fp[...]
         lists_out[...] = lists[...]
-        last = tiles(up)
         for i in range(STEPS + 2):
             to, j = (lists_out, i) if i < STEPS else (fp_out, i - STEPS)
-            to[j, 10:11, :LANES] = got_up[last, i : i + 1, :]
-            to[j, 10:11, LANES:] = got_up[last, 16 + i : 17 + i, :]
+            to[j, 10:11, :LANES] = got.tile(True, FIRST_TILES - 1, slice(i, i + 1))
+            to[j, 10:11, LANES:] = got.tile(True, FIRST_TILES - 1, slice(16 + i, 17 + i))
         edge_m, lists = edge_out, lists_out
     rows = slice(Y0, Y0 + 8)
+    rates[...] = jnp.zeros_like(rates)
     for z in range(2, 11):
         if z < 10:
             vx = v[VX, z, rows, :]
         else:
-            vx = unpacked(got_up, up, up.index((VX, 2)), rows) - edge_m[0, 1, rows, :] * s[SXZ - SXX, 9, rows, :]
+            vx = got.plane(True, 0, rows) - edge_m[0, 1, rows, :] * s[SXZ - SXX, 9, rows, :]
         if z == 2:
-            vx = vx - m[0, 0, rows, :] * unpacked(got_down, down, down.index((SXZ, 9)), rows)
-        rate = vx[1:2, :] - vx[0:1, :]
-        for j in range(lists.shape[0] - 1):
-            sent[j, z : z + 1, :] = lists[j + 1, z : z + 1, :] + coefs[j] * rate
-
-
-def two_steps_kernel(first, m, edge_m, fp, lists, got_up, got_down, v_in, s_in, q_in, v, s, q, rates):
-    up, down = (UP_FIRST, DOWN_FIRST) if first else (UP, DOWN)
-    refs = (v, s, q, m)
-    for i, (f, z) in enumerate(UP):
-        plane_of(refs, f, z + 8)[...] = unpacked(got_up, up, i)
-    for i, (f, z) in enumerate(DOWN):
-        plane_of(refs, f, z - 8)[...] = unpacked(got_down, down, i)
+            vx = vx - m[0, 0, rows, :] * got.plane(False, 0, rows)
+        rates[z : z + 1, :] = vx[1:2, :] - vx[0:1, :]
+    for j in range(lists.shape[0] - 1):
+        sent[j] = lists[j + 1] + coefs[j] * rates[...]
+
+
+def two_steps_kernel(first, m, edge_m, fp, lists, one, two, v_in, s_in, q_in, v, s, q, rates):
+    got = Got(one, two, FIRST if first else TRACES)
     sxz, syz, szz = SXZ - SXX, SYZ - SXX, SZZ - SXX
+    nothing = jnp.zeros((NY, EXT), jnp.float32)
     for z in range(2, 10):
         for f in ALL_V:
             plane = v_in[f, z]
             if z == 2 and f == VX:
-                plane = plane - m[0, 0] * s[sxz, 1]
+                plane = plane - m[0, 0] * got.plane(False, 0)
             if z == 2 and f == VY:
-                plane = plane - m[0, 0] * s[syz, 1]
+                plane = plane - m[0, 0] * got.plane(False, 1)
             if z == 9 and f == VZ:
-                plane = plane + m[0, 7] * s[szz, 10]
+                plane = plane + m[0, 7] * got.plane(True, 2)
             v[f, z] = plane
-    v[VX, 10] -= edge_m[0, 1] * s_in[sxz, 9]
-    v[VY, 10] -= edge_m[0, 1] * s_in[syz, 9]
-    v[VZ, 1] += edge_m[0, 0] * s_in[szz, 2]
+    above = {VX: -(edge_m[0, 1] * s_in[sxz, 9]), VY: -(edge_m[0, 1] * s_in[syz, 9])}
+    below = {VZ: edge_m[0, 0] * s_in[szz, 2]}
+    v[VX, 10] = got.plane(True, 0) + above[VX]
+    v[VY, 10] = got.plane(True, 1) + above[VY]
+    v[VZ, 1] = got.plane(False, 2) + below[VZ]
+    more_above = stress_change(
+        lambda f, z: above.get(f, nothing) if z == 10 else v[f, z] if z == 9 else nothing,
+        10,
+        edge_m[1, 1],
+        edge_m[2, 1],
+        ALL_S,
+    )
+    slip = above[VX][Y0 + 1 : Y0 + 2, :] - above[VX][Y0 : Y0 + 1, :]
+    more_above[SXY] = slid(more_above[SXY], fp, 10, FRIC * slip - lists[0, 10:11, :])
+    more_below = stress_change(
+        lambda f, z: below.get(f, nothing) if z == 1 else v[f, z] if z == 2 else nothing,
+        1,
+        edge_m[1, 0],
+        edge_m[2, 0],
+        (SZZ, SXZ, SYZ),
+    )
+    s[szz, 10] = got.plane(True, 3) + more_above[SZZ]
+    s[sxz, 1] = got.plane(False, 3) + more_below[SXZ]
+    s[syz, 1] = got.plane(False, 4) + more_below[SYZ]
+
+    def velocity(f, z):
+        return v[f, z]
 
     def stress(f, z):
         return q[z] if f == SXY else s[f - SXX, z]
 
-    def stress_a(z, s_from, q_from, lam, mu, want):
-        for f, change in stress_change(v, z, lam, mu, want).items():
+    def own_stress_a(z, carry):
+        for f, change in stress_change(velocity, z, m[1, z - 2], m[2, z - 2], ALL_S).items():
             if f == SXY:
-                q[z] = q_from[z] + change
+                q[z] = q_in[z] + change
             else:
-                s[f - SXX, z] = s_from[f - SXX, z] + change
-        if SXY in want:
-            slide(q, fp, z, fp[0, pl.ds(z, 1), :] + FRIC * rate_at(v, z) - lists[0, pl.ds(z, 1), :])
-
-    def velocity_b(z, b, want):
-        for f, change in velocity_change(stress, z, b, want).items():
+                s[f - SXX, z] = s_in[f - SXX, z] + change
+        slide(q, fp, z, fp[0, pl.ds(z, 1), :] + FRIC * rate_at(v, z) - lists[0, pl.ds(z, 1), :])
+        return carry
+
+    def own_velocity_b(z, carry):
+        for f, change in velocity_change(stress, z, m[0, z - 2], ALL_V).items():
             v[f, z] += change
-
-    def own_stress_a(z, carry):
-        stress_a(z, s_in, q_in, m[1, z - 2], m[2, z - 2], ALL_S)
         return carry
 
-    def own_velocity_b(z, carry):
-        velocity_b(z, m[0, z - 2], ALL_V)
-        return carry
-
     def own_stress_b(z, carry):
-        for f, change in stress_change(v, z, m[1, z - 2], m[2, z - 2], ALL_S).items():
+        for f, change in stress_change(velocity, z, m[1, z - 2], m[2, z - 2], ALL_S).items():
             if f == SXY:
                 q[z] += change
             else:
@@ -320,23 +383,27 @@
         slide(q, fp, z, fp[0, pl.ds(z, 1), :] + FRIC * rate_at(v, z))
         return carry
 
-    stress_a(1, s, q, edge_m[1, 0], edge_m[2, 0], (SZZ, SXZ, SYZ))
     lax.fori_loop(2, 10, own_stress_a, 0, unroll=4)
-    stress_a(10, s, q, edge_m[1, 1], edge_m[2, 1], ALL_S)
-    velocity_b(1, edge_m[0, 0], (VZ,))
+    change = velocity_change(
+        lambda f, z: more_above[f] if z == 10 else s[f - SXX, 9], 10, edge_m[0, 1], (VX, VY)
+    )
+    v[VX, 10] = got.plane(True, 4) + above[VX] + change[VX]
+    v[VY, 10] = got.plane(True, 5) + above[VY] + change[VY]
+    change = velocity_change(
+        lambda f, z: more_below.get(f, nothing) if z == 1 else s[f - SXX, 2], 1, edge_m[0, 0], (VZ,)
+    )
+    v[VZ, 1] = got.plane(False, 5) + below[VZ] + change[VZ]
     lax.fori_loop(2, 10, own_velocity_b, 0, unroll=4)
-    velocity_b(10, edge_m[0, 1], (VX, VY))
     rates[...] = jnp.zeros_like(rates)
     for z in range(2, 11):
         rates[z : z + 1, :] = rate_at(v, z)
     lax.fori_loop(2, 10, own_stress_b, 0, unroll=4)
-    empty = jnp.zeros((NY, EXT), jnp.float32)
-    s[sxz, 1] = empty
-    s[syz, 1] = empty
-    s[szz, 10] = empty
-
-
-def part_kernel(m, fp, lists, s, v_in, q_in, v, q, up, down):
+    s[sxz, 1] = nothing
+    s[syz, 1] = nothing
+    s[szz, 10] = nothing
+
+
+def part_kernel(m, fp, lists, s, v_in, q_in, v, q, one, two):
     refs = (v, s, q, m)
 
     def step(z, carry):
@@ -347,8 +414,8 @@
         return carry
 
     lax.fori_loop(2, 10, step, 0, unroll=4)
-    pack(refs, UP, up)
-    pack(refs, DOWN, down)
+    up, down = traces(refs, fp)
+    post(packed(up), packed(down), one, two)
 
 
 def end_kernel(fp, lists, v, s, q, vel, str_):
@@ -367,9 +434,10 @@
     return lax.ppermute(value, "strike", [(i, (i + by) % n) for i in range(n)])
 
 
-def along_depth(value, by):
+def swapped(value, first):
     n = lax.axis_size("depth")
-    return lax.ppermute(value, "depth", [(i, i + by) for i in range(n) if 0 <= i + by < n])
+    pairs = [(i, i + 1) for i in range(first, n - 1, 2)]
+    return lax.ppermute(value, "depth", pairs + [(j, i) for i, j in pairs])
 
 
 def per_device(velocity, stress, b, lam, mu, past, coefs, pre, mask):
@@ -381,22 +449,23 @@
     from_next = along_strike(to_prev, -1)
     v3, s5, q1, m3 = (3, 12, NY, EXT), (5, 12, NY, EXT), (12, NY, EXT), (3, 8, NY, EXT)
     edge, plane = (3, 2, NY, EXT), (ROWS, EXT)
-    v, s, q, m, fp, lists, up, down = call(
+    v, s, q, m, fp, lists, one, two = call(
         start_kernel,
-        [v3, s5, q1, m3, (2, *plane), (STEPS, *plane), (tiles(UP_FIRST) + 1, NY, LANES), (tiles(DOWN_FIRST), NY, LANES)],
+        [v3, s5, q1, m3, (2, *plane), (STEPS, *plane)] + [(FIRST_TILES, NY, LANES)] * 2,
         [fields, pre, mask, owed, from_prev, from_next],
     )
     edge_m = m
     for step in range(0, STEPS, 2):
         first = step == 0
-        got_up = along_depth(up, -1)
-        got_down = along_depth(down, 1)
+        one = swapped(one, 0)
+        two = swapped(two, 1)
         left = STEPS - step - 1
         more = call(
             functools.partial(meet_kernel, first),
             [(left, *plane)] + ([edge, (2, *plane), (STEPS, *plane)] if first else []),
-            [coefs, got_up, got_down, v, s, m, edge_m, fp, lists],
+            [coefs, one, two, v, s, m, edge_m, fp, lists],
             smem=(0,),
+            scratch=[pltpu.VMEM(plane, jnp.float32)],
         )
         if first:
             edge_m, fp, lists = more[1:]
@@ -404,14 +473,14 @@
         v, s, q, rates = call(
             functools.partial(two_steps_kernel, first),
             [v3, s5, q1, plane],
-            [m, edge_m, fp, lists, got_up, got_down, v, s, q],
+            [m, edge_m, fp, lists, one, two, v, s, q],
             {6: 0, 7: 1, 8: 2},
         )
         if step + 2 < STEPS:
             lists = along_strike(got[1:] + coefs[: left - 1, None, None] * rates[None], 1)
-            v, q, up, down = call(
+            v, q, one, two = call(
                 part_kernel,
-                [v3, q1, (tiles(UP), NY, LANES), (tiles(DOWN), NY, LANES)],
+                [v3, q1] + [(TILES, NY, LANES)] * 2,
                 [m, fp, got, s, v, q],
                 {4: 0, 5: 1},
             )

time: 104 us -> 93 us (0.89)
  starting transfers between devices: 37.2 us -> 29 us
  waiting for transfers between devices: 45 us -> 41.3 us
    ppermute x8, starting transfers between devices: 30.2 us -> 21.9 us  [swapped(): return lax.ppermute(value, 'depth', pairs + [(j, i) for i, j in pairs])]
    ppermute x8, waiting for transfers between devices: 11.3 us -> 7.17 us  [swapped(): return lax.ppermute(value, 'depth', pairs + [(j, i) for i, j in pairs])]
  transfers between devices with their start and end apart: 17 -> 17, of which waited for: 12 -> 10; matrix products, arithmetic and copies ran while one was open for 0% -> 0% of each run, Pallas kernels for 9% -> 10%
where the time goes in v2:
time: 93 us; the launch traced here: 92.1 us
  waiting for transfers between devices  41.3 us (44%)
  starting transfers between devices  29 us (31%)
  Pallas kernels  18.2 us (20%)
  local copies, waits for them, and re-layouts  2.34 us (3%)
  between operations  0.98 us (1%)
    ppermute x9, waiting for transfers between devices, along_strike(): return lax.ppermute(value, 'strike', [(i, (i + by) % n) for i in range(n)])  34.1 us
    ppermute x8, starting transfers between devices, swapped(): return lax.ppermute(value, 'depth', pairs + [(j, i) for i, j in pairs])  21.9 us
    pallas_call x15, Pallas kernels, call(): pl.pallas_call(body, out_shape=[jax.ShapeDtypeStruct(s, jnp.float32) for...  18.2 us
    ppermute x8, waiting for transfers between devices, swapped(): return lax.ppermute(value, 'depth', pairs + [(j, i) for i, j in pairs])  7.17 us
    ppermute x9, starting transfers between devices, along_strike(): return lax.ppermute(value, 'strike', [(i, (i + by) % n) for i in range(n)])  7.11 us
    unnamed x16, local copies, waits for them, and re-layouts  2.34 us
  transfers between devices with their start and end apart: 17, of which 10 were waited for; matrix products, arithmetic and copies ran while one was open for 0% of the time, Pallas kernels for 10%

profile of v2, /device:TPU:6, one launch (start us, length us, event | category | flops | bytes accessed | tf_op | source)
XLA Modules:
  0.0 92.1 jit_solution(12770251501079420083)
XLA Ops:
  0.7 1.1 %constant_dynamic-update-slice_fusion.1 = f32[12,8,32,128]{3,2,1,0:T(8,128)S(1)} fusion(f32[3,8,32,128]{3,2,1,0:T(8,128)} %param.9), kind=kLoop, calls=%fused_computation.7 | loop fusion | bytes 786432
  1.8 1.2 %constant_dynamic-update-slice_fusion = f32[12,8,32,128]{3,2,1,0:T(8,128)S(1)} fusion(f32[12,8,32,128]{3,2,1,0:T(8,128)S(1)} %constant_dynamic-update-slice_fusion.1, f32[6,8,32,128]{3,2,1,0:T(8,128)} %param.10), kind=kLoop, calls=%fused_computation.6 | loop fusion | bytes 1572864
  3.1 0.7 shard_map.104.owed
  3.9 0.9 shard_map.105
  4.8 0.1 collective-permute-start
  4.9 6.4 %collective-permute-start.1 = (f32[7,32,128]{2,1,0:T(8,128)S(1)}, f32[7,32,128]{2,1,0:T(8,128)S(1)}, u32[]{:S(2)}, u32[]{:S(2)}) collective-permute-start(f32[7,32,128]{2,1,0:T(8,128)S(1)} %get-tuple-element.44), channel_id=1, source_target_pairs={{0,248},{8,0},{16,8},{24,16},{32,24},{40,32},{48,40},{56,48},{64,5... | collective-permute-start | bytes 344072 | tf_op jit(solution)/shard_map/ppermute | solution.py:434
  11.3 2.4 %collective-permute-done.from_prev = f32[7,32,128]{2,1,0:T(8,128)S(1)} collective-permute-done((f32[7,32,128]{2,1,0:T(8,128)S(1)}, f32[7,32,128]{2,1,0:T(8,128)S(1)}, u32[]{:S(2)}, u32[]{:S(2)}) %collective-permute-start) | collective-permute-done | bytes 114720 | tf_op jit(solution)/shard_map/ppermute | solution.py:434
  13.6 0.0 collective-permute-done.1.from_next
  13.6 1.7 %shard_map.106 = (f32[3,12,32,256]{3,2,1,0:T(8,128)S(1)}, f32[5,12,32,256]{3,2,1,0:T(8,128)S(1)}, f32[12,32,256]{2,1,0:T(8,128)S(1)}, f32[3,8,32,256]{3,2,1,0:T(...) custom-call(f32[12,8,32,128]{3,2,1,0:T(8,128)S(1)} %bitcast_dynamic-, ...), custom_call_target="tpu_custom_call" | custom-call | flops 4000000 | bytes 4000000 | tf_op jit(solution)/shard_map/pallas_call | solution.py:34
  15.3 3.0 %collective-permute-start.2 = (f32[12,32,128]{2,1,0:T(8,128)S(1)}, f32[12,32,128]{2,1,0:T(8,128)S(1)}, u32[]{:S(2)}, u32[]{:S(2)}) collective-permute-start(f32[12,32,128]{2,1,0:T(8,128)S(1)} %get-tuple-element.45), channel_id=1, source_target_pairs={{0,1},{2,3},{4,5},{6,7},{1,0},{3,2},{5,4},{7,6},{8,9},{10,11},{12,... | collective-permute-start | bytes 589832 | tf_op jit(solution)/shard_map/ppermute | solution.py:440
  18.3 2.8 %collective-permute-start.3 = (f32[12,32,128]{2,1,0:T(8,128)S(1)}, f32[12,32,128]{2,1,0:T(8,128)S(1)}, u32[]{:S(2)}, u32[]{:S(2)}) collective-permute-start(f32[12,32,128]{2,1,0:T(8,128)S(1)} %get-tuple-element.46), channel_id=1, source_target_pairs={{1,2},{3,4},{5,6},{2,1},{4,3},{6,5},{9,10},{11,12},{13,14},{10,9},... | collective-permute-start | bytes 589832 | tf_op jit(solution)/shard_map/ppermute | solution.py:440
  21.1 1.5 %collective-permute-done.2.one = f32[12,32,128]{2,1,0:T(8,128)S(1)} collective-permute-done((f32[12,32,128]{2,1,0:T(8,128)S(1)}, f32[12,32,128]{2,1,0:T(8,128)S(1)}, u32[]{:S(2)}, u32[]{:S(2)}) %collective-permute-start.2) | collective-permute-done | bytes 196640 | tf_op jit(solution)/shard_map/ppermute | solution.py:440
  22.6 5.7 %collective-permute-done.3.two = f32[12,32,128]{2,1,0:T(8,128)S(1)} collective-permute-done((f32[12,32,128]{2,1,0:T(8,128)S(1)}, f32[12,32,128]{2,1,0:T(8,128)S(1)}, u32[]{:S(2)}, u32[]{:S(2)}) %collective-permute-start.3) | collective-permute-done | bytes 196640 | tf_op jit(solution)/shard_map/ppermute | solution.py:440
  28.3 0.6 shard_map.107
  28.9 0.1 collective-permute-start.4
  29.0 2.0 %shard_map.108 = (f32[3,12,32,256]{3,2,1,0:T(8,128)S(1)}, f32[5,12,32,256]{3,2,1,0:T(8,128)S(1)}, f32[12,32,256]{2,1,0:T(8,128)S(1)}, f32[16,256]{1,0:T(8,128)S(1)}) custom-call(f32[3,8,32,256]{3,2,1,0:T(8,128)S(1)} %get-tuple-element.49.m.edge_m, ...), custom_call_target="tpu_custom_call", output_to_operand_aliasing={{0}: (6, {}), {1}: (7, {}), {2}: (8, {})} | custom-call | flops 4000000 | bytes 4000000 | tf_op jit(solution)/shard_map/pallas_call | solution.py:34
  31.1 4.3 %collective-permute-done.4.lists = f32[7,16,256]{2,1,0:T(8,128)S(1)} collective-permute-done((f32[7,16,256]{2,1,0:T(8,128)S(1)}, f32[7,16,256]{2,1,0:T(8,128)S(1)}, u32[]{:S(2)}, u32[]{:S(2)}) %collective-permute-start.4) | collective-permute-done | bytes 114720 | tf_op jit(solution)/shard_map/ppermute | solution.py:434
  35.3 0.8 shard_map.109
  36.2 0.1 collective-permute-start.5
  36.3 5.8 %collective-permute-start.6 = (f32[7,32,128]{2,1,0:T(8,128)S(1)}, f32[7,32,128]{2,1,0:T(8,128)S(1)}, u32[]{:S(2)}, u32[]{:S(2)}) collective-permute-start(f32[7,32,128]{2,1,0:T(8,128)S(1)} %get-tuple-element.61), channel_id=1, source_target_pairs={{1,2},{3,4},{5,6},{2,1},{4,3},{6,5},{9,10},{11,12},{13,14},{10,9},... | collective-permute-start | bytes 344072 | tf_op jit(solution)/shard_map/ppermute | solution.py:440
  42.1 0.1 slice_add_fusion
  42.1 0.1 collective-permute-start.7
  42.2 6.1 %collective-permute-done.7.lists = f32[6,16,256]{2,1,0:T(8,128)S(1)} collective-permute-done((f32[6,16,256]{2,1,0:T(8,128)S(1)}, f32[6,16,256]{2,1,0:T(8,128)S(1)}, u32[]{:S(2)}, u32[]{:S(2)}) %collective-permute-start.7) | collective-permute-done | bytes 98336 | tf_op jit(solution)/shard_map/ppermute | solution.py:434
  48.4 0.6 shard_map.110
  49.0 0.1 collective-permute-start.8
  49.1 2.0 %shard_map.111 = (f32[3,12,32,256]{3,2,1,0:T(8,128)S(1)}, f32[5,12,32,256]{3,2,1,0:T(8,128)S(1)}, f32[12,32,256]{2,1,0:T(8,128)S(1)}, f32[16,256]{1,0:T(8,128)S(1)}) custom-call(f32[3,8,32,256]{3,2,1,0:T(8,128)S(1)} %get-tuple-element.49.m.edge_m, ...), custom_call_target="tpu_custom_call", output_to_operand_aliasing={{0}: (6, {}), {1}: (7, {}), {2}: (8, {})} | custom-call | flops 4000000 | bytes 4000000 | tf_op jit(solution)/shard_map/pallas_call | solution.py:34
  51.2 3.9 %collective-permute-done.8.lists = f32[5,16,256]{2,1,0:T(8,128)S(1)} collective-permute-done((f32[5,16,256]{2,1,0:T(8,128)S(1)}, f32[5,16,256]{2,1,0:T(8,128)S(1)}, u32[]{:S(2)}, u32[]{:S(2)}) %collective-permute-start.8) | collective-permute-done | bytes 81952 | tf_op jit(solution)/shard_map/ppermute | solution.py:434
  55.1 0.8 shard_map.112
  55.9 0.1 collective-permute-start.9
  56.0 5.5 %collective-permute-start.10 = (f32[7,32,128]{2,1,0:T(8,128)S(1)}, f32[7,32,128]{2,1,0:T(8,128)S(1)}, u32[]{:S(2)}, u32[]{:S(2)}) collective-permute-start(f32[7,32,128]{2,1,0:T(8,128)S(1)} %get-tuple-element.69), channel_id=1, source_target_pairs={{1,2},{3,4},{5,6},{2,1},{4,3},{6,5},{9,10},{11,12},{13,14},{10,9},... | collective-permute-start | bytes 344072 | tf_op jit(solution)/shard_map/ppermute | solution.py:440
  61.5 0.1 slice_add_fusion.1
  61.6 0.0 collective-permute-start.11
  61.6 5.8 %collective-permute-done.11.lists = f32[4,16,256]{2,1,0:T(8,128)S(1)} collective-permute-done((f32[4,16,256]{2,1,0:T(8,128)S(1)}, f32[4,16,256]{2,1,0:T(8,128)S(1)}, u32[]{:S(2)}, u32[]{:S(2)}) %collective-permute-start.11) | collective-permute-done | bytes 65568 | tf_op jit(solution)/shard_map/ppermute | solution.py:434
  67.4 0.6 shard_map.113
  68.0 0.3 collective-permute-start.12
  68.3 2.0 %shard_map.114 = (f32[3,12,32,256]{3,2,1,0:T(8,128)S(1)}, f32[5,12,32,256]{3,2,1,0:T(8,128)S(1)}, f32[12,32,256]{2,1,0:T(8,128)S(1)}, f32[16,256]{1,0:T(8,128)S(1)}) custom-call(f32[3,8,32,256]{3,2,1,0:T(8,128)S(1)} %get-tuple-element.49.m.edge_m, ...), custom_call_target="tpu_custom_call", output_to_operand_aliasing={{0}: (6, {}), {1}: (7, {}), {2}: (8, {})} | custom-call | flops 4000000 | bytes 4000000 | tf_op jit(solution)/shard_map/pallas_call | solution.py:34
  70.4 3.6 %collective-permute-done.12.lists = f32[3,16,256]{2,1,0:T(8,128)S(1)} collective-permute-done((f32[3,16,256]{2,1,0:T(8,128)S(1)}, f32[3,16,256]{2,1,0:T(8,128)S(1)}, u32[]{:S(2)}, u32[]{:S(2)}) %collective-permute-start.12) | collective-permute-done | bytes 49184 | tf_op jit(solution)/shard_map/ppermute | solution.py:434
  73.9 0.8 shard_map.115
  74.7 0.1 collective-permute-start.13
  74.9 4.6 %collective-permute-start.14 = (f32[7,32,128]{2,1,0:T(8,128)S(1)}, f32[7,32,128]{2,1,0:T(8,128)S(1)}, u32[]{:S(2)}, u32[]{:S(2)}) collective-permute-start(f32[7,32,128]{2,1,0:T(8,128)S(1)} %get-tuple-element.77), channel_id=1, source_target_pairs={{1,2},{3,4},{5,6},{2,1},{4,3},{6,5},{9,10},{11,12},{13,14},{10,9},... | collective-permute-start | bytes 344072 | tf_op jit(solution)/shard_map/ppermute | solution.py:440
  79.4 0.1 slice_add_fusion.2
  79.5 0.0 collective-permute-start.15
  79.5 5.4 %collective-permute-done.15.lists = f32[2,16,256]{2,1,0:T(8,128)S(1)} collective-permute-done((f32[2,16,256]{2,1,0:T(8,128)S(1)}, f32[2,16,256]{2,1,0:T(8,128)S(1)}, u32[]{:S(2)}, u32[]{:S(2)}) %collective-permute-start.15) | collective-permute-done | bytes 32800 | tf_op jit(solution)/shard_map/ppermute | solution.py:434
  85.0 0.6 shard_map.116
  85.6 0.1 collective-permute-start.16
  85.7 2.6 %shard_map.117 = (f32[3,12,32,256]{3,2,1,0:T(8,128)S(1)}, f32[5,12,32,256]{3,2,1,0:T(8,128)S(1)}, f32[12,32,256]{2,1,0:T(8,128)S(1)}, f32[16,256]{1,0:T(8,128)}) custom-call(f32[3,8,32,256]{3,2,1,0:T(8,128)S(1)} %get-tuple-element.49.m.edge_m, ...), custom_call_target="tpu_custom_call", output_to_operand_aliasing={{0}: (6, {}), {1}: (7, {}), {2}: (8, {})} | custom-call | flops 4000000 | bytes 4000000 | tf_op jit(solution)/shard_map/pallas_call | solution.py:34
  88.4 2.6 %collective-permute-done.16.lists = f32[1,16,256]{2,1,0:T(8,128)S(1)} collective-permute-done((f32[1,16,256]{2,1,0:T(8,128)S(1)}, f32[1,16,256]{2,1,0:T(8,128)S(1)}, u32[]{:S(2)}, u32[]{:S(2)}) %collective-permute-start.16) | collective-permute-done | bytes 16416 | tf_op jit(solution)/shard_map/ppermute | solution.py:434
  91.0 1.1 %shard_map.118 = (f32[3,8,32,128]{3,2,1,0:T(8,128)}, f32[6,8,32,128]{3,2,1,0:T(8,128)}) custom-call(f32[2,16,256]{2,1,0:T(8,128)S(1)} %get-tuple-element.52.fp, f32[1,16,256]{2,1,0:T(8,128)S(1)} %collective-permute-done.16.lists, f32[3,12,32,256]{3,2,1,0:T(8,128)S(1)} %get-tuple-element.81.v, f32[5,12,32,256]{3,2,1,0:T(8,128)S(1)} %get-tuple-element.82.s, ...), custom_call_target="tpu_custom_call" | custom-call | flops 4000000 | bytes 4000000 | tf_op jit(solution)/shard_map/pallas_call | solution.py:34
  (23 shorter events, 0.1 us)
Async XLA Ops:
  0.6 2.4 %copy-start.4 = (f32[8,32,128]{2,1,0:T(8,128)S(1)}, f32[8,32,128]{2,1,0:T(8,128)}, u32[]{:S(2)}) copy-start(f32[8,32,128]{2,1,0:T(8,128)} %param.11) | copy-start | bytes 393220
  0.6 2.4 %copy-start.5 = (f32[8,32,128]{2,1,0:T(8,128)S(1)}, f32[8,32,128]{2,1,0:T(8,128)}, u32[]{:S(2)}) copy-start(f32[8,32,128]{2,1,0:T(8,128)} %param.12) | copy-start | bytes 393220
  0.7 2.4 %copy-start.6 = (f32[8,32,128]{2,1,0:T(8,128)S(1)}, f32[8,32,128]{2,1,0:T(8,128)}, u32[]{:S(2)}) copy-start(f32[8,32,128]{2,1,0:T(8,128)} %param.13) | copy-start | bytes 393220
  0.7 2.5 %copy-start.1 = (f32[64]{0:T(128)S(1)}, f32[64]{0:T(128)}, u32[]{:S(2)}) copy-start(f32[64]{0:T(128)} %coefs.9) | copy-start | bytes 772
  0.7 2.5 %copy-start = (f32[64,8,128]{2,1,0:T(8,128)S(1)}, f32[64,8,128]{2,1,0:T(8,128)}, u32[]{:S(2)}) copy-start(f32[64,8,128]{2,1,0:T(8,128)} %past.1) | copy-start | bytes 786436
  0.7 3.2 %copy-start.2 = (f32[8,128]{1,0:T(8,128)S(1)}, f32[8,128]{1,0:T(8,128)}, u32[]{:S(2)}) copy-start(f32[8,128]{1,0:T(8,128)} %pre.3) | copy-start | bytes 12292
  0.7 3.2 %copy-start.3 = (s32[8,128]{1,0:T(8,128)S(1)}, s32[8,128]{1,0:T(8,128)}, u32[]{:S(2)}) copy-start(s32[8,128]{1,0:T(8,128)} %mask.3) | copy-start | bytes 12292
  4.8 8.9 %collective-permute-start = (f32[7,32,128]{2,1,0:T(8,128)S(1)}, f32[7,32,128]{2,1,0:T(8,128)S(1)}, u32[]{:S(2)}, u32[]{:S(2)}) collective-permute-start(f32[7,32,128]{2,1,0:T(8,128)S(1)} %get-tuple-element.43), channel_id=1, source_target_pairs={{0,8},{8,16},{16,24},{24,32},{32,40},{40,48},{48,56},{56,64},{64,7... | collective-permute-start | bytes 344072 | tf_op jit(solution)/shard_map/ppermute | solution.py:434
  4.9 8.8 %collective-permute-start.1 = (f32[7,32,128]{2,1,0:T(8,128)S(1)}, f32[7,32,128]{2,1,0:T(8,128)S(1)}, u32[]{:S(2)}, u32[]{:S(2)}) collective-permute-start(f32[7,32,128]{2,1,0:T(8,128)S(1)} %get-tuple-element.44), channel_id=1, source_target_pairs={{0,248},{8,0},{16,8},{24,16},{32,24},{40,32},{48,40},{56,48},{64,5... | collective-permute-start | bytes 344072 | tf_op jit(solution)/shard_map/ppermute | solution.py:434
  15.3 7.3 %collective-permute-start.2 = (f32[12,32,128]{2,1,0:T(8,128)S(1)}, f32[12,32,128]{2,1,0:T(8,128)S(1)}, u32[]{:S(2)}, u32[]{:S(2)}) collective-permute-start(f32[12,32,128]{2,1,0:T(8,128)S(1)} %get-tuple-element.45), channel_id=1, source_target_pairs={{0,1},{2,3},{4,5},{6,7},{1,0},{3,2},{5,4},{7,6},{8,9},{10,11},{12,... | collective-permute-start | bytes 589832 | tf_op jit(solution)/shard_map/ppermute | solution.py:440
  18.3 10.0 %collective-permute-start.3 = (f32[12,32,128]{2,1,0:T(8,128)S(1)}, f32[12,32,128]{2,1,0:T(8,128)S(1)}, u32[]{:S(2)}, u32[]{:S(2)}) collective-permute-start(f32[12,32,128]{2,1,0:T(8,128)S(1)} %get-tuple-element.46), channel_id=1, source_target_pairs={{1,2},{3,4},{5,6},{2,1},{4,3},{6,5},{9,10},{11,12},{13,14},{10,9},... | collective-permute-start | bytes 589832 | tf_op jit(solution)/shard_map/ppermute | solution.py:440
  28.9 6.4 %collective-permute-start.4 = (f32[7,16,256]{2,1,0:T(8,128)S(1)}, f32[7,16,256]{2,1,0:T(8,128)S(1)}, u32[]{:S(2)}, u32[]{:S(2)}) collective-permute-start(f32[7,16,256]{2,1,0:T(8,128)S(1)} %get-tuple-element.53), channel_id=1, source_target_pairs={{0,8},{8,16},{16,24},{24,32},{32,40},{40,48},{48,56},{56,64},{64,7... | collective-permute-start | bytes 344072 | tf_op jit(solution)/shard_map/ppermute | solution.py:434
  36.2 12.2 %collective-permute-start.5 = (f32[7,32,128]{2,1,0:T(8,128)S(1)}, f32[7,32,128]{2,1,0:T(8,128)S(1)}, u32[]{:S(2)}, u32[]{:S(2)}) collective-permute-start(f32[7,32,128]{2,1,0:T(8,128)S(1)} %get-tuple-element.60), channel_id=1, source_target_pairs={{0,1},{2,3},{4,5},{6,7},{1,0},{3,2},{5,4},{7,6},{8,9},{10,11},{12,... | collective-permute-start | bytes 344072 | tf_op jit(solution)/shard_map/ppermute | solution.py:440
  36.3 12.1 %collective-permute-start.6 = (f32[7,32,128]{2,1,0:T(8,128)S(1)}, f32[7,32,128]{2,1,0:T(8,128)S(1)}, u32[]{:S(2)}, u32[]{:S(2)}) collective-permute-start(f32[7,32,128]{2,1,0:T(8,128)S(1)} %get-tuple-element.61), channel_id=1, source_target_pairs={{1,2},{3,4},{5,6},{2,1},{4,3},{6,5},{9,10},{11,12},{13,14},{10,9},... | collective-permute-start | bytes 344072 | tf_op jit(solution)/shard_map/ppermute | solution.py:440
  42.1 6.2 %collective-permute-start.7 = (f32[6,16,256]{2,1,0:T(8,128)S(1)}, f32[6,16,256]{2,1,0:T(8,128)S(1)}, u32[]{:S(2)}, u32[]{:S(2)}) collective-permute-start(f32[6,16,256]{2,1,0:T(8,128)S(1)} %slice_add_fusion), channel_id=1, source_target_pairs={{0,8},{8,16},{16,24},{24,32},{32,40},{40,48},{48,56},{56,64},{64,7... | collective-permute-start | bytes 294920 | tf_op jit(solution)/shard_map/ppermute | solution.py:434
  49.0 6.1 %collective-permute-start.8 = (f32[5,16,256]{2,1,0:T(8,128)S(1)}, f32[5,16,256]{2,1,0:T(8,128)S(1)}, u32[]{:S(2)}, u32[]{:S(2)}) collective-permute-start(f32[5,16,256]{2,1,0:T(8,128)S(1)} %shard_map.110), channel_id=1, source_target_pairs={{0,8},{8,16},{16,24},{24,32},{32,40},{40,48},{48,56},{56,64},{64,7... | collective-permute-start | bytes 245768 | tf_op jit(solution)/shard_map/ppermute | solution.py:434
  55.9 11.5 %collective-permute-start.9 = (f32[7,32,128]{2,1,0:T(8,128)S(1)}, f32[7,32,128]{2,1,0:T(8,128)S(1)}, u32[]{:S(2)}, u32[]{:S(2)}) collective-permute-start(f32[7,32,128]{2,1,0:T(8,128)S(1)} %get-tuple-element.68), channel_id=1, source_target_pairs={{0,1},{2,3},{4,5},{6,7},{1,0},{3,2},{5,4},{7,6},{8,9},{10,11},{12,... | collective-permute-start | bytes 344072 | tf_op jit(solution)/shard_map/ppermute | solution.py:440
  56.0 11.4 %collective-permute-start.10 = (f32[7,32,128]{2,1,0:T(8,128)S(1)}, f32[7,32,128]{2,1,0:T(8,128)S(1)}, u32[]{:S(2)}, u32[]{:S(2)}) collective-permute-start(f32[7,32,128]{2,1,0:T(8,128)S(1)} %get-tuple-element.69), channel_id=1, source_target_pairs={{1,2},{3,4},{5,6},{2,1},{4,3},{6,5},{9,10},{11,12},{13,14},{10,9},... | collective-permute-start | bytes 344072 | tf_op jit(solution)/shard_map/ppermute | solution.py:440
  61.6 5.8 %collective-permute-start.11 = (f32[4,16,256]{2,1,0:T(8,128)S(1)}, f32[4,16,256]{2,1,0:T(8,128)S(1)}, u32[]{:S(2)}, u32[]{:S(2)}) collective-permute-start(f32[4,16,256]{2,1,0:T(8,128)S(1)} %slice_add_fusion.1), channel_id=1, source_target_pairs={{0,8},{8,16},{16,24},{24,32},{32,40},{40,48},{48,56},{56,64},{64,7... | collective-permute-start | bytes 196616 | tf_op jit(solution)/shard_map/ppermute | solution.py:434
  68.0 5.9 %collective-permute-start.12 = (f32[3,16,256]{2,1,0:T(8,128)S(1)}, f32[3,16,256]{2,1,0:T(8,128)S(1)}, u32[]{:S(2)}, u32[]{:S(2)}) collective-permute-start(f32[3,16,256]{2,1,0:T(8,128)S(1)} %shard_map.113), channel_id=1, source_target_pairs={{0,8},{8,16},{16,24},{24,32},{32,40},{40,48},{48,56},{56,64},{64,7... | collective-permute-start | bytes 147464 | tf_op jit(solution)/shard_map/ppermute | solution.py:434
  74.7 10.2 %collective-permute-start.13 = (f32[7,32,128]{2,1,0:T(8,128)S(1)}, f32[7,32,128]{2,1,0:T(8,128)S(1)}, u32[]{:S(2)}, u32[]{:S(2)}) collective-permute-start(f32[7,32,128]{2,1,0:T(8,128)S(1)} %get-tuple-element.76), channel_id=1, source_target_pairs={{0,1},{2,3},{4,5},{6,7},{1,0},{3,2},{5,4},{7,6},{8,9},{10,11},{12,... | collective-permute-start | bytes 344072 | tf_op jit(solution)/shard_map/ppermute | solution.py:440
  74.9 10.1 %collective-permute-start.14 = (f32[7,32,128]{2,1,0:T(8,128)S(1)}, f32[7,32,128]{2,1,0:T(8,128)S(1)}, u32[]{:S(2)}, u32[]{:S(2)}) collective-permute-start(f32[7,32,128]{2,1,0:T(8,128)S(1)} %get-tuple-element.77), channel_id=1, source_target_pairs={{1,2},{3,4},{5,6},{2,1},{4,3},{6,5},{9,10},{11,12},{13,14},{10,9},... | collective-permute-start | bytes 344072 | tf_op jit(solution)/shard_map/ppermute | solution.py:440
  79.5 5.5 %collective-permute-start.15 = (f32[2,16,256]{2,1,0:T(8,128)S(1)}, f32[2,16,256]{2,1,0:T(8,128)S(1)}, u32[]{:S(2)}, u32[]{:S(2)}) collective-permute-start(f32[2,16,256]{2,1,0:T(8,128)S(1)} %slice_add_fusion.2), channel_id=1, source_target_pairs={{0,8},{8,16},{16,24},{24,32},{32,40},{40,48},{48,56},{56,64},{64,7... | collective-permute-start | bytes 98312 | tf_op jit(solution)/shard_map/ppermute | solution.py:434
  85.6 5.3 %collective-permute-start.16 = (f32[1,16,256]{2,1,0:T(8,128)S(1)}, f32[1,16,256]{2,1,0:T(8,128)S(1)}, u32[]{:S(2)}, u32[]{:S(2)}) collective-permute-start(f32[1,16,256]{2,1,0:T(8,128)S(1)} %shard_map.116), channel_id=1, source_target_pairs={{0,8},{8,16},{16,24},{24,32},{32,40},{40,48},{48,56},{56,64},{64,7... | collective-permute-start | bytes 49160 | tf_op jit(solution)/shard_map/ppermute | solution.py:434

commit v3 on v2

--- a/solution.py
+++ b/solution.py
@@ -198,6 +198,7 @@
             term = coefs[j + k] * past[k]
             parts[k % 4] = term if parts[k % 4] is None else parts[k % 4] + term
         owed[j] = (parts[0] + parts[1]) + (parts[2] + parts[3])
+    owed[STEPS] = jnp.full((8, LANES), coefs[0])
 
 
 def edges_kernel(fields, pre, mask, owed, to_next, to_prev):
@@ -234,7 +235,7 @@
     return velocity_change(stress, z, m[0, z - 2], ALL_V)
 
 
-def start_kernel(fields, pre, mask, owed, from_prev, from_next, v, s, q, m, fp, lists, one, two):
+def start_kernel(fields, pre, mask, owed, from_prev, from_next, v, s, q, m, fp, lists, one, two, ahead):
     lane = lane_of(NY)
     lane8 = lane_of(8)
     empty = jnp.zeros((NY, EXT), jnp.float32)
@@ -272,6 +273,10 @@
         return carry
 
     lax.fori_loop(2, 10, step, 0, unroll=4)
+    scale = jnp.concatenate([owed[STEPS, 0:1, :]] * 2, axis=1)
+    ahead[...] = lists[1]
+    for z in range(3, 10):
+        ahead[z : z + 1, :] = lists[1, z : z + 1, :] + scale * rate_at(v, z)
     up, down = traces(refs, fp)
     up = packed(up + [m[k, 0] for k in range(3)])
     down = packed(down + [m[k, 7] for k in range(3)])
@@ -286,7 +291,18 @@
             out[last, 16 + i : 17 + i, :] = to[j, 2:3, LANES:]
 
 
-def meet_kernel(first, coefs, one, two, v, s, m, edge_m, fp, lists, sent, *more):
+def late_traction(fp, late, z):
+    return jnp.where(fp[1, z : z + 1, :] > 0.5, -late[0, z : z + 1, :], 0.0)
+
+
+def late_velocity(b, lack):
+    row = lax.broadcasted_iota(jnp.int32, b.shape, 0)
+    lack = jnp.broadcast_to(lack, b.shape)
+    vx = jnp.where(row == Y0, b * lack, jnp.where(row == Y0 + 1, -(b * lack), 0.0))
+    return vx, jnp.where(row == Y0, b * (lack - behind_x(lack)), 0.0)
+
+
+def meet_kernel(first, coefs, one, two, v, s, m, edge_m, fp, lists, late, sent, *more):
     *more, rates = more
     got = Got(one, two, FIRST if first else TRACES)
     if first:
@@ -310,15 +326,22 @@
             vx = got.plane(True, 0, rows) - edge_m[0, 1, rows, :] * s[SXZ - SXX, 9, rows, :]
         if z == 2:
             vx = vx - m[0, 0, rows, :] * got.plane(False, 0, rows)
-        rates[z : z + 1, :] = vx[1:2, :] - vx[0:1, :]
-    for j in range(lists.shape[0] - 1):
+        rate = vx[1:2, :] - vx[0:1, :]
+        if not first and z in (2, 10):
+            b = m[0, 0, rows, :] if z == 2 else edge_m[0, 1, rows, :]
+            rate = rate - (b[1:2, :] + b[0:1, :]) * late_traction(fp, late, z)
+        rates[z : z + 1, :] = rate
+    for j in range(sent.shape[0]):
         sent[j] = lists[j + 1] + coefs[j] * rates[...]
 
 
-def two_steps_kernel(first, m, edge_m, fp, lists, one, two, v_in, s_in, q_in, v, s, q, rates):
+def two_steps_kernel(first, m, edge_m, fp, lists, late, one, two, v_in, s_in, q_in, v, s, q, rates):
     got = Got(one, two, FIRST if first else TRACES)
     sxz, syz, szz = SXZ - SXX, SYZ - SXX, SZZ - SXX
     nothing = jnp.zeros((NY, EXT), jnp.float32)
+    if not first:
+        late_own = late_velocity(m[0, 0], late_traction(fp, late, 2))
+        late_above = late_velocity(edge_m[0, 1], late_traction(fp, late, 10))
     for z in range(2, 10):
         for f in ALL_V:
             plane = v_in[f, z]
@@ -328,9 +351,13 @@
                 plane = plane - m[0, 0] * got.plane(False, 1)
             if z == 9 and f == VZ:
                 plane = plane + m[0, 7] * got.plane(True, 2)
+            if z == 2 and f < VZ and not first:
+                plane = plane + late_own[f]
             v[f, z] = plane
     above = {VX: -(edge_m[0, 1] * s_in[sxz, 9]), VY: -(edge_m[0, 1] * s_in[syz, 9])}
     below = {VZ: edge_m[0, 0] * s_in[szz, 2]}
+    if not first:
+        above = {f: plane + late_above[f] for f, plane in above.items()}
     v[VX, 10] = got.plane(True, 0) + above[VX]
     v[VY, 10] = got.plane(True, 1) + above[VY]
     v[VZ, 1] = got.plane(False, 2) + below[VZ]
@@ -403,12 +430,15 @@
     s[szz, 10] = nothing
 
 
-def part_kernel(m, fp, lists, s, v_in, q_in, v, q, one, two):
+def part_kernel(coefs, m, fp, ahead, near, s, v_in, q_in, v, q, one, two, rates):
     refs = (v, s, q, m)
+    memory = ahead[...] if near is None else ahead[...] + coefs[0] * near[...]
+    row = lax.broadcasted_iota(jnp.int32, memory.shape, 0)
+    rates[...] = jnp.where(row > 2, memory, 0.0)
 
     def step(z, carry):
         q[z] = q_in[z]
-        slide(q, fp, z, q[z, Y0 : Y0 + 1, :] - lists[0, pl.ds(z, 1), :])
+        slide(q, fp, z, q[z, Y0 : Y0 + 1, :] - rates[pl.ds(z, 1), :])
         for f, change in move_first(refs, z).items():
             v[f, z] = v_in[f, z] + change
         return carry
@@ -416,6 +446,12 @@
     lax.fori_loop(2, 10, step, 0, unroll=4)
     up, down = traces(refs, fp)
     post(packed(up), packed(down), one, two)
+    for z in range(3, 10):
+        rates[z : z + 1, :] = rate_at(v, z)
+
+
+def first_part_kernel(coefs, m, fp, ahead, *rest):
+    part_kernel(coefs, m, fp, ahead, None, *rest)
 
 
 def end_kernel(fp, lists, v, s, q, vel, str_):
@@ -442,19 +478,21 @@
 
 def per_device(velocity, stress, b, lam, mu, past, coefs, pre, mask):
     edge = (7, NY, LANES)
-    (owed,) = call(owed_kernel, [(STEPS, 8, LANES)], [coefs, past], smem=(0,))
+    (owed,) = call(owed_kernel, [(STEPS + 1, 8, LANES)], [coefs, past], smem=(0,))
     fields = jnp.concatenate([velocity, stress, DT * b[None], DT * lam[None], DT * mu[None]])
     to_next, to_prev = call(edges_kernel, [edge, edge], [fields, pre, mask, owed])
     from_prev = along_strike(to_next, 1)
     from_next = along_strike(to_prev, -1)
     v3, s5, q1, m3 = (3, 12, NY, EXT), (5, 12, NY, EXT), (12, NY, EXT), (3, 8, NY, EXT)
     edge, plane = (3, 2, NY, EXT), (ROWS, EXT)
-    v, s, q, m, fp, lists, one, two = call(
+    v, s, q, m, fp, lists, one, two, ahead = call(
         start_kernel,
-        [v3, s5, q1, m3, (2, *plane), (STEPS, *plane)] + [(FIRST_TILES, NY, LANES)] * 2,
+        [v3, s5, q1, m3, (2, *plane), (STEPS, *plane)] + [(FIRST_TILES, NY, LANES)] * 2 + [plane],
         [fields, pre, mask, owed, from_prev, from_next],
     )
     edge_m = m
+    late = lists
+    ahead = along_strike(ahead, 1)
     for step in range(0, STEPS, 2):
         first = step == 0
         one = swapped(one, 0)
@@ -463,7 +501,7 @@
         more = call(
             functools.partial(meet_kernel, first),
             [(left, *plane)] + ([edge, (2, *plane), (STEPS, *plane)] if first else []),
-            [coefs, one, two, v, s, m, edge_m, fp, lists],
+            [coefs, one, two, v, s, m, edge_m, fp, lists, late],
             smem=(0,),
             scratch=[pltpu.VMEM(plane, jnp.float32)],
         )
@@ -473,17 +511,23 @@
         v, s, q, rates = call(
             functools.partial(two_steps_kernel, first),
             [v3, s5, q1, plane],
-            [m, edge_m, fp, lists, one, two, v, s, q],
-            {6: 0, 7: 1, 8: 2},
+            [m, edge_m, fp, lists, late, one, two, v, s, q],
+            {7: 0, 8: 1, 9: 2},
         )
         if step + 2 < STEPS:
-            lists = along_strike(got[1:] + coefs[: left - 1, None, None] * rates[None], 1)
-            v, q, one, two = call(
-                part_kernel,
-                [v3, q1] + [(TILES, NY, LANES)] * 2,
-                [m, fp, got, s, v, q],
-                {4: 0, 5: 1},
+            v, q, one, two, ahead = call(
+                first_part_kernel if first else part_kernel,
+                [v3, q1] + [(TILES, NY, LANES)] * 2 + [plane],
+                [coefs, m, fp, ahead] + ([] if first else [near]) + [s, v, q],
+                {5: 0, 6: 1} if first else {6: 0, 7: 1},
+                smem=(0,),
             )
+        if step + 2 < STEPS:
+            owed = got[1:] + coefs[: left - 1, None, None] * rates[None]
+            lists = along_strike(jnp.concatenate([owed, ahead[None]]), 1)
+            near = lists[left - 1]
+            ahead = along_strike(owed[1], 2)
+            late = got
     return tuple(call(end_kernel, [velocity.shape, stress.shape], [fp, got, v, s, q]))
 
 

time: 93 us -> 89.9 us (0.967)
  waiting for transfers between devices: 41.3 us -> 34.7 us
  Pallas kernels: 18.2 us -> 19.8 us
  local copies, waits for them, and re-layouts: 2.34 us -> 3.92 us
    ppermute x9 -> x12, waiting for transfers between devices: 34.1 us -> 20.3 us  [along_strike(): return lax.ppermute(value, 'strike', [(i, (i + by) % n) for i in range(n)])]
    ppermute x8, waiting for transfers between devices: 7.17 us -> 14.4 us  [swapped(): return lax.ppermute(value, 'depth', pairs + [(j, i) for i, j in pairs])]
    unnamed x16 -> x18, local copies, waits for them, and re-layouts: 2.34 us -> 3.91 us
    pallas_call x15, Pallas kernels: 18.2 us -> 19.8 us  [call(): pl.pallas_call(body, out_shape=[jax.ShapeDtypeStruct(s, jnp.float32) for...]
    ppermute x9 -> x12, starting transfers between devices: 7.11 us -> 7.29 us  [along_strike(): return lax.ppermute(value, 'strike', [(i, (i + by) % n) for i in range(n)])]
  transfers between devices with their start and end apart: 17 -> 20, of which waited for: 10 -> 12; matrix products, arithmetic and copies ran while one was open for 0% -> 0% of each run, Pallas kernels for 10% -> 16%
where the time goes in v3:
time: 89.9 us; the launch traced here: 88.8 us
  waiting for transfers between devices  34.7 us (39%)
  starting transfers between devices  29 us (32%)
  Pallas kernels  19.8 us (22%)
  local copies, waits for them, and re-layouts  3.92 us (4%)
  between operations  1.08 us (1%)
    ppermute x8, starting transfers between devices, swapped(): return lax.ppermute(value, 'depth', pairs + [(j, i) for i, j in pairs])  21.7 us
    ppermute x12, waiting for transfers between devices, along_strike(): return lax.ppermute(value, 'strike', [(i, (i + by) % n) for i in range(n)])  20.3 us
    pallas_call x15, Pallas kernels, call(): pl.pallas_call(body, out_shape=[jax.ShapeDtypeStruct(s, jnp.float32) for...  19.8 us
    ppermute x8, waiting for transfers between devices, swapped(): return lax.ppermute(value, 'depth', pairs + [(j, i) for i, j in pairs])  14.4 us
    ppermute x12, starting transfers between devices, along_strike(): return lax.ppermute(value, 'strike', [(i, (i + by) % n) for i in range(n)])  7.29 us
    unnamed x18, local copies, waits for them, and re-layouts  3.91 us
  transfers between devices with their start and end apart: 20, of which 12 were waited for; matrix products, arithmetic and copies ran while one was open for 0% of the time, Pallas kernels for 16%

profile of v3, /device:TPU:6, one launch (start us, length us, event | category | flops | bytes accessed | tf_op | source)
XLA Modules:
  0.0 88.8 jit_solution(17407981085176750389)
XLA Ops:
  0.7 1.1 %constant_dynamic-update-slice_fusion.1 = f32[12,8,32,128]{3,2,1,0:T(8,128)S(1)} fusion(f32[3,8,32,128]{3,2,1,0:T(8,128)} %param.9), kind=kLoop, calls=%fused_computation.14 | loop fusion | bytes 786432
  1.8 0.9 %copy-done = f32[64,8,128]{2,1,0:T(8,128)S(1)} copy-done((f32[64,8,128]{2,1,0:T(8,128)S(1)}, f32[64,8,128]{2,1,0:T(8,128)}, u32[]{:S(2)}) %copy-start) | copy-done | bytes 262168
  2.7 0.7 copy-done.1
  3.4 0.7 shard_map.104.owed
  4.1 1.2 %constant_dynamic-update-slice_fusion = f32[12,8,32,128]{3,2,1,0:T(8,128)S(1)} fusion(f32[12,8,32,128]{3,2,1,0:T(8,128)S(1)} %constant_dynamic-update-slice_fusion.1, f32[6,8,32,128]{3,2,1,0:T(8,128)} %param.10), kind=kLoop, calls=%fused_computation.13 | loop fusion | bytes 1572864
  5.4 0.9 shard_map.105
  6.3 0.1 collective-permute-start
  6.4 6.4 %collective-permute-start.1 = (f32[7,32,128]{2,1,0:T(8,128)S(1)}, f32[7,32,128]{2,1,0:T(8,128)S(1)}, u32[]{:S(2)}, u32[]{:S(2)}) collective-permute-start(f32[7,32,128]{2,1,0:T(8,128)S(1)} %get-tuple-element.48), channel_id=1, source_target_pairs={{0,248},{8,0},{16,8},{24,16},{32,24},{40,32},{48,40},{56,48},{64,5... | collective-permute-start | bytes 344072 | tf_op jit(solution)/shard_map/ppermute | solution.py:470
  12.8 2.4 %collective-permute-done.from_prev = f32[7,32,128]{2,1,0:T(8,128)S(1)} collective-permute-done((f32[7,32,128]{2,1,0:T(8,128)S(1)}, f32[7,32,128]{2,1,0:T(8,128)S(1)}, u32[]{:S(2)}, u32[]{:S(2)}) %collective-permute-start) | collective-permute-done | bytes 114720 | tf_op jit(solution)/shard_map/ppermute | solution.py:470
  15.2 1.7 %shard_map.106 = (f32[3,12,32,256]{3,2,1,0:T(8,128)S(1)}, f32[5,12,32,256]{3,2,1,0:T(8,128)S(1)}, f32[12,32,256]{2,1,0:T(8,128)S(1)}, f32[3,8,32,256]{3,2,1,0:T(...) custom-call(f32[12,8,32,128]{3,2,1,0:T(8,128)S(1)} %bitcast_dynamic-, ...), custom_call_target="tpu_custom_call" | custom-call | flops 4000000 | bytes 4000000 | tf_op jit(solution)/shard_map/pallas_call | solution.py:34
  16.9 3.0 %collective-permute-start.2 = (f32[12,32,128]{2,1,0:T(8,128)S(1)}, f32[12,32,128]{2,1,0:T(8,128)S(1)}, u32[]{:S(2)}, u32[]{:S(2)}) collective-permute-start(f32[12,32,128]{2,1,0:T(8,128)S(1)} %get-tuple-element.49), channel_id=1, source_target_pairs={{0,1},{2,3},{4,5},{6,7},{1,0},{3,2},{5,4},{7,6},{8,9},{10,11},{12,... | collective-permute-start | bytes 589832 | tf_op jit(solution)/shard_map/ppermute | solution.py:476
  19.9 2.8 %collective-permute-start.3 = (f32[12,32,128]{2,1,0:T(8,128)S(1)}, f32[12,32,128]{2,1,0:T(8,128)S(1)}, u32[]{:S(2)}, u32[]{:S(2)}) collective-permute-start(f32[12,32,128]{2,1,0:T(8,128)S(1)} %get-tuple-element.50), channel_id=1, source_target_pairs={{1,2},{3,4},{5,6},{2,1},{4,3},{6,5},{9,10},{11,12},{13,14},{10,9},... | collective-permute-start | bytes 589832 | tf_op jit(solution)/shard_map/ppermute | solution.py:476
  22.7 1.5 %collective-permute-done.2.one = f32[12,32,128]{2,1,0:T(8,128)S(1)} collective-permute-done((f32[12,32,128]{2,1,0:T(8,128)S(1)}, f32[12,32,128]{2,1,0:T(8,128)S(1)}, u32[]{:S(2)}, u32[]{:S(2)}) %collective-permute-start.2) | collective-permute-done | bytes 196640 | tf_op jit(solution)/shard_map/ppermute | solution.py:476
  24.1 5.7 %collective-permute-done.3.two = f32[12,32,128]{2,1,0:T(8,128)S(1)} collective-permute-done((f32[12,32,128]{2,1,0:T(8,128)S(1)}, f32[12,32,128]{2,1,0:T(8,128)S(1)}, u32[]{:S(2)}, u32[]{:S(2)}) %collective-permute-start.3) | collective-permute-done | bytes 196640 | tf_op jit(solution)/shard_map/ppermute | solution.py:476
  29.8 0.7 shard_map.107
  30.5 0.1 collective-permute-start.7
  30.6 0.1 collective-permute-start.4
  30.7 2.0 %shard_map.108 = (f32[3,12,32,256]{3,2,1,0:T(8,128)S(1)}, f32[5,12,32,256]{3,2,1,0:T(8,128)S(1)}, f32[12,32,256]{2,1,0:T(8,128)S(1)}, f32[16,256]{1,0:T(8,128)S(1)}) custom-call(f32[3,8,32,256]{3,2,1,0:T(8,128)S(1)} %get-tuple-element.53.m.edge_m, ...), custom_call_target="tpu_custom_call", output_to_operand_aliasing={{0}: (7, {}), {1}: (8, {}), {2}: (9, {})} | custom-call | flops 4000000 | bytes 4000000 | tf_op jit(solution)/shard_map/pallas_call | solution.py:34
  32.7 4.5 %collective-permute-done.4.ahead = f32[16,256]{1,0:T(8,128)S(1)} collective-permute-done((f32[16,256]{1,0:T(8,128)S(1)}, f32[16,256]{1,0:T(8,128)S(1)}, u32[]{:S(2)}, u32[]{:S(2)}) %collective-permute-start.4) | collective-permute-done | bytes 16416 | tf_op jit(solution)/shard_map/ppermute | solution.py:470
  37.2 1.4 %shard_map.109 = (f32[3,12,32,256]{3,2,1,0:T(8,128)S(1)}, f32[12,32,256]{2,1,0:T(8,128)S(1)}, f32[7,32,128]{2,1,0:T(8,128)S(1)}, f32[7,32,128]{2,1,0:T(8,128)S(1)}, f32[16,256]{1,0:T(8,128)S(1)}) custom-call(f32[64]{0:T(128)S(1)} %copy-done.1, f32[3,8,32,256]{3,2,1,0:T(8,128)S(1)} %get-tuple-element.53.m.edge_m, ...), custom_call_target="tpu_custom_call", output_to_operand_aliasing={{0}: (5, {}), {1}: (6, {})} | custom-call | flops 4000000 | bytes 4000000 | tf_op jit(solution)/shard_map/pallas_call | solution.py:34
  38.5 0.1 collective-permute-start.5
  38.6 5.6 %collective-permute-start.6 = (f32[7,32,128]{2,1,0:T(8,128)S(1)}, f32[7,32,128]{2,1,0:T(8,128)S(1)}, u32[]{:S(2)}, u32[]{:S(2)}) collective-permute-start(f32[7,32,128]{2,1,0:T(8,128)S(1)} %get-tuple-element.65), channel_id=1, source_target_pairs={{1,2},{3,4},{5,6},{2,1},{4,3},{6,5},{9,10},{11,12},{13,14},{10,9},... | collective-permute-start | bytes 344072 | tf_op jit(solution)/shard_map/ppermute | solution.py:476
  44.4 0.1 collective-permute-start.8
  44.5 0.1 collective-permute-start.11
  44.6 0.3 collective-permute-done.5.one
  44.9 3.1 %collective-permute-done.6.two = f32[7,32,128]{2,1,0:T(8,128)S(1)} collective-permute-done((f32[7,32,128]{2,1,0:T(8,128)S(1)}, f32[7,32,128]{2,1,0:T(8,128)S(1)}, u32[]{:S(2)}, u32[]{:S(2)}) %collective-permute-start.6) | collective-permute-done | bytes 114720 | tf_op jit(solution)/shard_map/ppermute | solution.py:476
  48.0 3.0 %collective-permute-done.8.lists = f32[7,16,256]{2,1,0:T(8,128)S(1)} collective-permute-done((f32[7,16,256]{2,1,0:T(8,128)S(1)}, f32[7,16,256]{2,1,0:T(8,128)S(1)}, u32[]{:S(2)}, u32[]{:S(2)}) %collective-permute-start.8) | collective-permute-done | bytes 114720 | tf_op jit(solution)/shard_map/ppermute | solution.py:470
  51.0 0.6 shard_map.110
  51.7 2.0 %shard_map.111 = (f32[3,12,32,256]{3,2,1,0:T(8,128)S(1)}, f32[5,12,32,256]{3,2,1,0:T(8,128)S(1)}, f32[12,32,256]{2,1,0:T(8,128)S(1)}, f32[16,256]{1,0:T(8,128)S(1)}) custom-call(f32[3,8,32,256]{3,2,1,0:T(8,128)S(1)} %get-tuple-element.53.m.edge_m, ...), custom_call_target="tpu_custom_call", output_to_operand_aliasing={{0}: (7, {}), {1}: (8, {}), {2}: (9, {})} | custom-call | flops 4000000 | bytes 4000000 | tf_op jit(solution)/shard_map/pallas_call | solution.py:34
  53.8 1.4 %shard_map.112 = (f32[3,12,32,256]{3,2,1,0:T(8,128)S(1)}, f32[12,32,256]{2,1,0:T(8,128)S(1)}, f32[7,32,128]{2,1,0:T(8,128)S(1)}, f32[7,32,128]{2,1,0:T(8,128)S(1)}, f32[16,256]{1,0:T(8,128)S(1)}) custom-call(f32[64]{0:T(128)S(1)} %copy-done.2, f32[3,8,32,256]{3,2,1,0:T(8,128)S(1)} %get-tuple-element.53.m.edge_m, ...), custom_call_target="tpu_custom_call", output_to_operand_aliasing={{0}: (6, {}), {1}: (7, {})} | custom-call | flops 4000000 | bytes 4000000 | tf_op jit(solution)/shard_map/pallas_call | solution.py:34
  55.1 0.3 collective-permute-start.13
  55.4 5.4 %collective-permute-start.14 = (f32[7,32,128]{2,1,0:T(8,128)S(1)}, f32[7,32,128]{2,1,0:T(8,128)S(1)}, u32[]{:S(2)}, u32[]{:S(2)}) collective-permute-start(f32[7,32,128]{2,1,0:T(8,128)S(1)} %get-tuple-element.77), channel_id=1, source_target_pairs={{1,2},{3,4},{5,6},{2,1},{4,3},{6,5},{9,10},{11,12},{13,14},{10,9},... | collective-permute-start | bytes 344072 | tf_op jit(solution)/shard_map/ppermute | solution.py:476
  60.9 0.1 collective-permute-start.12
  61.0 0.1 collective-permute-start.10
  61.1 1.0 %collective-permute-done.13.one = f32[7,32,128]{2,1,0:T(8,128)S(1)} collective-permute-done((f32[7,32,128]{2,1,0:T(8,128)S(1)}, f32[7,32,128]{2,1,0:T(8,128)S(1)}, u32[]{:S(2)}, u32[]{:S(2)}) %collective-permute-start.13) | collective-permute-done | bytes 114720 | tf_op jit(solution)/shard_map/ppermute | solution.py:476
  62.1 2.8 %collective-permute-done.14.two = f32[7,32,128]{2,1,0:T(8,128)S(1)} collective-permute-done((f32[7,32,128]{2,1,0:T(8,128)S(1)}, f32[7,32,128]{2,1,0:T(8,128)S(1)}, u32[]{:S(2)}, u32[]{:S(2)}) %collective-permute-start.14) | collective-permute-done | bytes 114720 | tf_op jit(solution)/shard_map/ppermute | solution.py:476
  64.9 2.2 %collective-permute-done.12.lists = f32[5,16,256]{2,1,0:T(8,128)S(1)} collective-permute-done((f32[5,16,256]{2,1,0:T(8,128)S(1)}, f32[5,16,256]{2,1,0:T(8,128)S(1)}, u32[]{:S(2)}, u32[]{:S(2)}) %collective-permute-start.12) | collective-permute-done | bytes 81952 | tf_op jit(solution)/shard_map/ppermute | solution.py:470
  67.1 0.6 shard_map.115
  67.9 2.0 %shard_map.113 = (f32[3,12,32,256]{3,2,1,0:T(8,128)S(1)}, f32[5,12,32,256]{3,2,1,0:T(8,128)S(1)}, f32[12,32,256]{2,1,0:T(8,128)S(1)}, f32[16,256]{1,0:T(8,128)S(1)}) custom-call(f32[3,8,32,256]{3,2,1,0:T(8,128)S(1)} %get-tuple-element.53.m.edge_m, ...), custom_call_target="tpu_custom_call", output_to_operand_aliasing={{0}: (7, {}), {1}: (8, {}), {2}: (9, {})} | custom-call | flops 4000000 | bytes 4000000 | tf_op jit(solution)/shard_map/pallas_call | solution.py:34
  69.9 1.4 %shard_map.114 = (f32[3,12,32,256]{3,2,1,0:T(8,128)S(1)}, f32[12,32,256]{2,1,0:T(8,128)S(1)}, f32[7,32,128]{2,1,0:T(8,128)S(1)}, f32[7,32,128]{2,1,0:T(8,128)S(1)}, f32[16,256]{1,0:T(8,128)S(1)}) custom-call(f32[64]{0:T(128)S(1)} %copy-done.2, f32[3,8,32,256]{3,2,1,0:T(8,128)S(1)} %get-tuple-element.53.m.edge_m, ...), custom_call_target="tpu_custom_call", output_to_operand_aliasing={{0}: (6, {}), {1}: (7, {})} | custom-call | flops 4000000 | bytes 4000000 | tf_op jit(solution)/shard_map/pallas_call | solution.py:34
  71.3 0.1 collective-permute-start.15
  71.4 4.4 %collective-permute-start.16 = (f32[7,32,128]{2,1,0:T(8,128)S(1)}, f32[7,32,128]{2,1,0:T(8,128)S(1)}, u32[]{:S(2)}, u32[]{:S(2)}) collective-permute-start(f32[7,32,128]{2,1,0:T(8,128)S(1)} %get-tuple-element.84), channel_id=1, source_target_pairs={{1,2},{3,4},{5,6},{2,1},{4,3},{6,5},{9,10},{11,12},{13,14},{10,9},... | collective-permute-start | bytes 344072 | tf_op jit(solution)/shard_map/ppermute | solution.py:476
  76.0 0.1 collective-permute-start.18
  76.0 5.6 %collective-permute-done.18.lists = f32[3,16,256]{2,1,0:T(8,128)S(1)} collective-permute-done((f32[3,16,256]{2,1,0:T(8,128)S(1)}, f32[3,16,256]{2,1,0:T(8,128)S(1)}, u32[]{:S(2)}, u32[]{:S(2)}) %collective-permute-start.18) | collective-permute-done | bytes 49184 | tf_op jit(solution)/shard_map/ppermute | solution.py:470
  81.7 0.6 shard_map.116
  82.4 2.6 %shard_map.117 = (f32[3,12,32,256]{3,2,1,0:T(8,128)S(1)}, f32[5,12,32,256]{3,2,1,0:T(8,128)S(1)}, f32[12,32,256]{2,1,0:T(8,128)S(1)}, f32[16,256]{1,0:T(8,128)}) custom-call(f32[3,8,32,256]{3,2,1,0:T(8,128)S(1)} %get-tuple-element.53.m.edge_m, ...), custom_call_target="tpu_custom_call", output_to_operand_aliasing={{0}: (7, {}), {1}: (8, {}), {2}: (9, {})} | custom-call | flops 4000000 | bytes 4000000 | tf_op jit(solution)/shard_map/pallas_call | solution.py:34
  85.0 2.6 %collective-permute-done.19.lists = f32[1,16,256]{2,1,0:T(8,128)S(1)} collective-permute-done((f32[1,16,256]{2,1,0:T(8,128)S(1)}, f32[1,16,256]{2,1,0:T(8,128)S(1)}, u32[]{:S(2)}, u32[]{:S(2)}) %collective-permute-start.19) | collective-permute-done | bytes 16416 | tf_op jit(solution)/shard_map/ppermute | solution.py:470
  87.7 1.1 %shard_map.118 = (f32[3,8,32,128]{3,2,1,0:T(8,128)}, f32[6,8,32,128]{3,2,1,0:T(8,128)}) custom-call(f32[2,16,256]{2,1,0:T(8,128)S(1)} %get-tuple-element.56.fp, f32[1,16,256]{2,1,0:T(8,128)S(1)} %collective-permute-done.19.lists, f32[3,12,32,256]{3,2,1,0:T(8,128)S(1)} %get-tuple-element.89.v, f32[5,12,32,256]{3,2,1,0:T(8,128)S(1)} %get-tuple-element.90.s, ...), custom_call_target="tpu_custom_call" | custom-call | flops 4000000 | bytes 4000000 | tf_op jit(solution)/shard_map/pallas_call | solution.py:34
  (38 shorter events, 0.6 us)
Async XLA Ops:
  0.6 4.7 %copy-start.5 = (f32[8,32,128]{2,1,0:T(8,128)S(1)}, f32[8,32,128]{2,1,0:T(8,128)}, u32[]{:S(2)}) copy-start(f32[8,32,128]{2,1,0:T(8,128)} %param.11) | copy-start | bytes 393220
  0.6 4.7 %copy-start.6 = (f32[8,32,128]{2,1,0:T(8,128)S(1)}, f32[8,32,128]{2,1,0:T(8,128)}, u32[]{:S(2)}) copy-start(f32[8,32,128]{2,1,0:T(8,128)} %param.12) | copy-start | bytes 393220
  0.7 4.7 %copy-start.7 = (f32[8,32,128]{2,1,0:T(8,128)S(1)}, f32[8,32,128]{2,1,0:T(8,128)}, u32[]{:S(2)}) copy-start(f32[8,32,128]{2,1,0:T(8,128)} %param.13) | copy-start | bytes 393220
  0.7 4.8 %copy-start.4 = (s32[8,128]{1,0:T(8,128)S(1)}, s32[8,128]{1,0:T(8,128)}, u32[]{:S(2)}) copy-start(s32[8,128]{1,0:T(8,128)} %mask.3) | copy-start | bytes 12292
  0.7 4.8 %copy-start.3 = (f32[8,128]{1,0:T(8,128)S(1)}, f32[8,128]{1,0:T(8,128)}, u32[]{:S(2)}) copy-start(f32[8,128]{1,0:T(8,128)} %pre.3) | copy-start | bytes 12292
  1.8 1.0 %copy-start = (f32[64,8,128]{2,1,0:T(8,128)S(1)}, f32[64,8,128]{2,1,0:T(8,128)}, u32[]{:S(2)}) copy-start(f32[64,8,128]{2,1,0:T(8,128)} %past.1) | copy-start | bytes 786436
  2.7 0.7 copy-start.1
  6.3 8.9 %collective-permute-start = (f32[7,32,128]{2,1,0:T(8,128)S(1)}, f32[7,32,128]{2,1,0:T(8,128)S(1)}, u32[]{:S(2)}, u32[]{:S(2)}) collective-permute-start(f32[7,32,128]{2,1,0:T(8,128)S(1)} %get-tuple-element.47), channel_id=1, source_target_pairs={{0,8},{8,16},{16,24},{24,32},{32,40},{40,48},{48,56},{56,64},{64,7... | collective-permute-start | bytes 344072 | tf_op jit(solution)/shard_map/ppermute | solution.py:470
  6.4 8.8 %collective-permute-start.1 = (f32[7,32,128]{2,1,0:T(8,128)S(1)}, f32[7,32,128]{2,1,0:T(8,128)S(1)}, u32[]{:S(2)}, u32[]{:S(2)}) collective-permute-start(f32[7,32,128]{2,1,0:T(8,128)S(1)} %get-tuple-element.48), channel_id=1, source_target_pairs={{0,248},{8,0},{16,8},{24,16},{32,24},{40,32},{48,40},{56,48},{64,5... | collective-permute-start | bytes 344072 | tf_op jit(solution)/shard_map/ppermute | solution.py:470
  16.9 7.3 %collective-permute-start.2 = (f32[12,32,128]{2,1,0:T(8,128)S(1)}, f32[12,32,128]{2,1,0:T(8,128)S(1)}, u32[]{:S(2)}, u32[]{:S(2)}) collective-permute-start(f32[12,32,128]{2,1,0:T(8,128)S(1)} %get-tuple-element.49), channel_id=1, source_target_pairs={{0,1},{2,3},{4,5},{6,7},{1,0},{3,2},{5,4},{7,6},{8,9},{10,11},{12,... | collective-permute-start | bytes 589832 | tf_op jit(solution)/shard_map/ppermute | solution.py:476
  19.9 10.0 %collective-permute-start.3 = (f32[12,32,128]{2,1,0:T(8,128)S(1)}, f32[12,32,128]{2,1,0:T(8,128)S(1)}, u32[]{:S(2)}, u32[]{:S(2)}) collective-permute-start(f32[12,32,128]{2,1,0:T(8,128)S(1)} %get-tuple-element.50), channel_id=1, source_target_pairs={{1,2},{3,4},{5,6},{2,1},{4,3},{6,5},{9,10},{11,12},{13,14},{10,9},... | collective-permute-start | bytes 589832 | tf_op jit(solution)/shard_map/ppermute | solution.py:476
  30.5 13.8 %collective-permute-start.7 = (f32[7,16,256]{2,1,0:T(8,128)S(1)}, f32[7,16,256]{2,1,0:T(8,128)S(1)}, u32[]{:S(2)}, u32[]{:S(2)}) collective-permute-start(f32[7,16,256]{2,1,0:T(8,128)S(1)} %get-tuple-element.67), channel_id=1, source_target_pairs={{0,8},{8,16},{16,24},{24,32},{32,40},{40,48},{48,56},{56,64},{64,7... | collective-permute-start | bytes 344072 | tf_op jit(solution)/shard_map/ppermute | solution.py:470
  30.6 6.6 %collective-permute-start.4 = (f32[16,256]{1,0:T(8,128)S(1)}, f32[16,256]{1,0:T(8,128)S(1)}, u32[]{:S(2)}, u32[]{:S(2)}) collective-permute-start(f32[16,256]{1,0:T(8,128)S(1)} %get-tuple-element.57), channel_id=1, source_target_pairs={{0,8},{8,16},{16,24},{24,32},{32,40},{40,48},{48,56},{56,64},{64,7... | collective-permute-start | bytes 49160 | tf_op jit(solution)/shard_map/ppermute | solution.py:470
  37.2 7.1 %copy-start.2 = (f32[64]{0:T(128)S(1)}, f32[64]{0:T(128)}, u32[]{:S(2)}) copy-start(f32[64]{0:T(128)} %coefs.15) | copy-start | bytes 772
  38.5 6.4 %collective-permute-start.5 = (f32[7,32,128]{2,1,0:T(8,128)S(1)}, f32[7,32,128]{2,1,0:T(8,128)S(1)}, u32[]{:S(2)}, u32[]{:S(2)}) collective-permute-start(f32[7,32,128]{2,1,0:T(8,128)S(1)} %get-tuple-element.64), channel_id=1, source_target_pairs={{0,1},{2,3},{4,5},{6,7},{1,0},{3,2},{5,4},{7,6},{8,9},{10,11},{12,... | collective-permute-start | bytes 344072 | tf_op jit(solution)/shard_map/ppermute | solution.py:476
  38.6 9.4 %collective-permute-start.6 = (f32[7,32,128]{2,1,0:T(8,128)S(1)}, f32[7,32,128]{2,1,0:T(8,128)S(1)}, u32[]{:S(2)}, u32[]{:S(2)}) collective-permute-start(f32[7,32,128]{2,1,0:T(8,128)S(1)} %get-tuple-element.65), channel_id=1, source_target_pairs={{1,2},{3,4},{5,6},{2,1},{4,3},{6,5},{9,10},{11,12},{13,14},{10,9},... | collective-permute-start | bytes 344072 | tf_op jit(solution)/shard_map/ppermute | solution.py:476
  44.4 6.6 %collective-permute-start.8 = (f32[7,16,256]{2,1,0:T(8,128)S(1)}, f32[7,16,256]{2,1,0:T(8,128)S(1)}, u32[]{:S(2)}, u32[]{:S(2)}) collective-permute-start(f32[7,16,256]{2,1,0:T(8,128)S(1)} %pad_maximum_fusion), channel_id=1, source_target_pairs={{0,8},{8,16},{16,24},{24,32},{32,40},{40,48},{48,56},{56,64},{64,7... | collective-permute-start | bytes 344072 | tf_op jit(solution)/shard_map/ppermute | solution.py:470
  44.5 9.3 %collective-permute-start.11 = (f32[16,256]{1,0:T(8,128)S(1)}, f32[16,256]{1,0:T(8,128)S(1)}, u32[]{:S(2)}, u32[]{:S(2)}) collective-permute-start(f32[16,256]{1,0:T(8,128)S(1)} %slice_bitcast_fusion.2), channel_id=1, source_target_pairs={{0,16},{8,24},{16,32},{24,40},{32,48},{40,56},{48,64},{56,72},{64,... | collective-permute-start | bytes 49160 | tf_op jit(solution)/shard_map/ppermute | solution.py:470
  51.6 9.2 %collective-permute-start.9 = (f32[5,16,256]{2,1,0:T(8,128)S(1)}, f32[5,16,256]{2,1,0:T(8,128)S(1)}, u32[]{:S(2)}, u32[]{:S(2)}) collective-permute-start(f32[5,16,256]{2,1,0:T(8,128)S(1)} %shard_map.110), channel_id=1, source_target_pairs={{0,8},{8,16},{16,24},{24,32},{32,40},{40,48},{48,56},{56,64},{64,7... | collective-permute-start | bytes 245768 | tf_op jit(solution)/shard_map/ppermute | solution.py:470
  55.1 6.9 %collective-permute-start.13 = (f32[7,32,128]{2,1,0:T(8,128)S(1)}, f32[7,32,128]{2,1,0:T(8,128)S(1)}, u32[]{:S(2)}, u32[]{:S(2)}) collective-permute-start(f32[7,32,128]{2,1,0:T(8,128)S(1)} %get-tuple-element.76), channel_id=1, source_target_pairs={{0,1},{2,3},{4,5},{6,7},{1,0},{3,2},{5,4},{7,6},{8,9},{10,11},{12,... | collective-permute-start | bytes 344072 | tf_op jit(solution)/shard_map/ppermute | solution.py:476
  55.4 9.5 %collective-permute-start.14 = (f32[7,32,128]{2,1,0:T(8,128)S(1)}, f32[7,32,128]{2,1,0:T(8,128)S(1)}, u32[]{:S(2)}, u32[]{:S(2)}) collective-permute-start(f32[7,32,128]{2,1,0:T(8,128)S(1)} %get-tuple-element.77), channel_id=1, source_target_pairs={{1,2},{3,4},{5,6},{2,1},{4,3},{6,5},{9,10},{11,12},{13,14},{10,9},... | collective-permute-start | bytes 344072 | tf_op jit(solution)/shard_map/ppermute | solution.py:476
  60.9 6.2 %collective-permute-start.12 = (f32[5,16,256]{2,1,0:T(8,128)S(1)}, f32[5,16,256]{2,1,0:T(8,128)S(1)}, u32[]{:S(2)}, u32[]{:S(2)}) collective-permute-start(f32[5,16,256]{2,1,0:T(8,128)S(1)} %pad_maximum_fusion.1), channel_id=1, source_target_pairs={{0,8},{8,16},{16,24},{24,32},{32,40},{40,48},{48,56},{56,64},{64,7... | collective-permute-start | bytes 245768 | tf_op jit(solution)/shard_map/ppermute | solution.py:470
  61.0 8.9 %collective-permute-start.10 = (f32[16,256]{1,0:T(8,128)S(1)}, f32[16,256]{1,0:T(8,128)S(1)}, u32[]{:S(2)}, u32[]{:S(2)}) collective-permute-start(f32[16,256]{1,0:T(8,128)S(1)} %slice_bitcast_fusion.3), channel_id=1, source_target_pairs={{0,16},{8,24},{16,32},{24,40},{32,48},{40,56},{48,64},{56,72},{64,... | collective-permute-start | bytes 49160 | tf_op jit(solution)/shard_map/ppermute | solution.py:470
  67.8 8.1 %collective-permute-start.17 = (f32[3,16,256]{2,1,0:T(8,128)S(1)}, f32[3,16,256]{2,1,0:T(8,128)S(1)}, u32[]{:S(2)}, u32[]{:S(2)}) collective-permute-start(f32[3,16,256]{2,1,0:T(8,128)S(1)} %shard_map.115), channel_id=1, source_target_pairs={{0,8},{8,16},{16,24},{24,32},{32,40},{40,48},{48,56},{56,64},{64,7... | collective-permute-start | bytes 147464 | tf_op jit(solution)/shard_map/ppermute | solution.py:470
  71.3 10.4 %collective-permute-start.15 = (f32[7,32,128]{2,1,0:T(8,128)S(1)}, f32[7,32,128]{2,1,0:T(8,128)S(1)}, u32[]{:S(2)}, u32[]{:S(2)}) collective-permute-start(f32[7,32,128]{2,1,0:T(8,128)S(1)} %get-tuple-element.83), channel_id=1, source_target_pairs={{0,1},{2,3},{4,5},{6,7},{1,0},{3,2},{5,4},{7,6},{8,9},{10,11},{12,... | collective-permute-start | bytes 344072 | tf_op jit(solution)/shard_map/ppermute | solution.py:476
  71.4 10.3 %collective-permute-start.16 = (f32[7,32,128]{2,1,0:T(8,128)S(1)}, f32[7,32,128]{2,1,0:T(8,128)S(1)}, u32[]{:S(2)}, u32[]{:S(2)}) collective-permute-start(f32[7,32,128]{2,1,0:T(8,128)S(1)} %get-tuple-element.84), channel_id=1, source_target_pairs={{1,2},{3,4},{5,6},{2,1},{4,3},{6,5},{9,10},{11,12},{13,14},{10,9},... | collective-permute-start | bytes 344072 | tf_op jit(solution)/shard_map/ppermute | solution.py:476
  76.0 5.7 %collective-permute-start.18 = (f32[3,16,256]{2,1,0:T(8,128)S(1)}, f32[3,16,256]{2,1,0:T(8,128)S(1)}, u32[]{:S(2)}, u32[]{:S(2)}) collective-permute-start(f32[3,16,256]{2,1,0:T(8,128)S(1)} %pad_maximum_fusion.2), channel_id=1, source_target_pairs={{0,8},{8,16},{16,24},{24,32},{32,40},{40,48},{48,56},{56,64},{64,7... | collective-permute-start | bytes 147464 | tf_op jit(solution)/shard_map/ppermute | solution.py:470
  82.3 5.3 %collective-permute-start.19 = (f32[1,16,256]{2,1,0:T(8,128)S(1)}, f32[1,16,256]{2,1,0:T(8,128)S(1)}, u32[]{:S(2)}, u32[]{:S(2)}) collective-permute-start(f32[1,16,256]{2,1,0:T(8,128)S(1)} %shard_map.116), channel_id=1, source_target_pairs={{0,8},{8,16},{16,24},{24,32},{32,40},{40,48},{48,56},{56,64},{64,7... | collective-permute-start | bytes 49160 | tf_op jit(solution)/shard_map/ppermute | solution.py:470

commit v4 on v3

--- a/solution.py
+++ b/solution.py
@@ -192,13 +192,20 @@
 
 
 def owed_kernel(coefs, past, owed):
+    sums = [[None, None] for _ in range(STEPS)]
+    for k in range(HIST):
+        plane = past[k]
+        for j in range(min(STEPS, HIST - k)):
+            old = sums[j][k % 2]
+            term = coefs[j + k] * plane
+            sums[j][k % 2] = term if old is None else old + term
     for j in range(STEPS):
-        parts = [None] * 4
-        for k in range(HIST - j):
-            term = coefs[j + k] * past[k]
-            parts[k % 4] = term if parts[k % 4] is None else parts[k % 4] + term
-        owed[j] = (parts[0] + parts[1]) + (parts[2] + parts[3])
-    owed[STEPS] = jnp.full((8, LANES), coefs[0])
+        owed[j] = sums[j][0] + sums[j][1]
+        owed[STEPS + j] = jnp.full((8, LANES), coefs[j])
+
+
+def coef(owed, j):
+    return jnp.concatenate([owed[STEPS + j, 0:1, :]] * 2, axis=1)
 
 
 def edges_kernel(fields, pre, mask, owed, to_next, to_prev):
@@ -243,7 +250,7 @@
     s[SYZ - SXX, 1] = empty
     s[SZZ - SXX, 10] = empty
     refs = (v, s, q, m)
-    for k, f in enumerate((VX, VY, VZ, SXX, SXY, SXZ, SYZ, SZZ, SYY, B, LAM, MU)):
+    for k, f in enumerate((SXX, SXY, SXZ, SYZ, SZZ, SYY, VX, VY, VZ, B, LAM, MU)):
         for z in range(8):
             at = (k % 2) * 8 + z
             edge = jnp.where(
@@ -273,10 +280,9 @@
         return carry
 
     lax.fori_loop(2, 10, step, 0, unroll=4)
-    scale = jnp.concatenate([owed[STEPS, 0:1, :]] * 2, axis=1)
     ahead[...] = lists[1]
     for z in range(3, 10):
-        ahead[z : z + 1, :] = lists[1, z : z + 1, :] + scale * rate_at(v, z)
+        ahead[z : z + 1, :] = lists[1, z : z + 1, :] + coef(owed, 0) * rate_at(v, z)
     up, down = traces(refs, fp)
     up = packed(up + [m[k, 0] for k in range(3)])
     down = packed(down + [m[k, 7] for k in range(3)])
@@ -302,7 +308,7 @@
     return vx, jnp.where(row == Y0, b * (lack - behind_x(lack)), 0.0)
 
 
-def meet_kernel(first, coefs, one, two, v, s, m, edge_m, fp, lists, late, sent, *more):
+def meet_kernel(first, owed, one, two, v, s, m, edge_m, fp, lists, late, sent, *more):
     *more, rates = more
     got = Got(one, two, FIRST if first else TRACES)
     if first:
@@ -332,7 +338,7 @@
             rate = rate - (b[1:2, :] + b[0:1, :]) * late_traction(fp, late, z)
         rates[z : z + 1, :] = rate
     for j in range(sent.shape[0]):
-        sent[j] = lists[j + 1] + coefs[j] * rates[...]
+        sent[j] = lists[j + 1] + coef(owed, j) * rates[...]
 
 
 def two_steps_kernel(first, m, edge_m, fp, lists, late, one, two, v_in, s_in, q_in, v, s, q, rates):
@@ -430,9 +436,9 @@
     s[szz, 10] = nothing
 
 
-def part_kernel(coefs, m, fp, ahead, near, s, v_in, q_in, v, q, one, two, rates):
+def part_kernel(owed, m, fp, ahead, near, s, v_in, q_in, v, q, one, two, rates):
     refs = (v, s, q, m)
-    memory = ahead[...] if near is None else ahead[...] + coefs[0] * near[...]
+    memory = ahead[...] if near is None else ahead[...] + coef(owed, 0) * near[...]
     row = lax.broadcasted_iota(jnp.int32, memory.shape, 0)
     rates[...] = jnp.where(row > 2, memory, 0.0)
 
@@ -450,8 +456,8 @@
         rates[z : z + 1, :] = rate_at(v, z)
 
 
-def first_part_kernel(coefs, m, fp, ahead, *rest):
-    part_kernel(coefs, m, fp, ahead, None, *rest)
+def first_part_kernel(owed, m, fp, ahead, *rest):
+    part_kernel(owed, m, fp, ahead, None, *rest)
 
 
 def end_kernel(fp, lists, v, s, q, vel, str_):
@@ -478,8 +484,8 @@
 
 def per_device(velocity, stress, b, lam, mu, past, coefs, pre, mask):
     edge = (7, NY, LANES)
-    (owed,) = call(owed_kernel, [(STEPS + 1, 8, LANES)], [coefs, past], smem=(0,))
-    fields = jnp.concatenate([velocity, stress, DT * b[None], DT * lam[None], DT * mu[None]])
+    (owed,) = call(owed_kernel, [(2 * STEPS, 8, LANES)], [coefs, past], smem=(0,))
+    fields = jnp.concatenate([stress, velocity, DT * b[None], DT * lam[None], DT * mu[None]])
     to_next, to_prev = call(edges_kernel, [edge, edge], [fields, pre, mask, owed])
     from_prev = along_strike(to_next, 1)
     from_next = along_strike(to_prev, -1)
@@ -501,8 +507,7 @@
         more = call(
             functools.partial(meet_kernel, first),
             [(left, *plane)] + ([edge, (2, *plane), (STEPS, *plane)] if first else []),
-            [coefs, one, two, v, s, m, edge_m, fp, lists, late],
-            smem=(0,),
+            [owed, one, two, v, s, m, edge_m, fp, lists, late],
             scratch=[pltpu.VMEM(plane, jnp.float32)],
         )
         if first:
@@ -518,15 +523,14 @@
             v, q, one, two, ahead = call(
                 first_part_kernel if first else part_kernel,
                 [v3, q1] + [(TILES, NY, LANES)] * 2 + [plane],
-                [coefs, m, fp, ahead] + ([] if first else [near]) + [s, v, q],
+                [owed, m, fp, ahead] + ([] if first else [near]) + [s, v, q],
                 {5: 0, 6: 1} if first else {6: 0, 7: 1},
-                smem=(0,),
             )
         if step + 2 < STEPS:
-            owed = got[1:] + coefs[: left - 1, None, None] * rates[None]
-            lists = along_strike(jnp.concatenate([owed, ahead[None]]), 1)
+            next_lists = got[1:] + coefs[: left - 1, None, None] * rates[None]
+            lists = along_strike(jnp.concatenate([next_lists, ahead[None]]), 1)
             near = lists[left - 1]
-            ahead = along_strike(owed[1], 2)
+            ahead = along_strike(next_lists[1], 2)
             late = got
     return tuple(call(end_kernel, [velocity.shape, stress.shape], [fp, got, v, s, q]))
 

time: 89.9 us -> 83.6 us (0.930)
  Pallas kernels: 19.8 us -> 16 us
  local copies, waits for them, and re-layouts: 3.92 us -> 1.34 us
    pallas_call x15, Pallas kernels: 19.8 us -> 16 us  [call(): pl.pallas_call(body, out_shape=[jax.ShapeDtypeStruct(s, jnp.float32) for...]
    unnamed x18, local copies, waits for them, and re-layouts: 3.91 us -> 1.32 us
  transfers between devices with their start and end apart: 20 -> 20, of which waited for: 12 -> 12; matrix products, arithmetic and copies ran while one was open for 0% -> 0% of each run, Pallas kernels for 16% -> 14%
where the time goes in v4:
time: 83.6 us; the launch traced here: 82.5 us
  waiting for transfers between devices  34.7 us (42%)
  starting transfers between devices  29.1 us (35%)
  Pallas kernels  16 us (19%)
  local copies, waits for them, and re-layouts  1.34 us (2%)
  between operations  1.1 us (1%)
    ppermute x8, starting transfers between devices, swapped(): return lax.ppermute(value, 'depth', pairs + [(j, i) for i, j in pairs])  21.8 us
    ppermute x12, waiting for transfers between devices, along_strike(): return lax.ppermute(value, 'strike', [(i, (i + by) % n) for i in range(n)])  20.3 us
    pallas_call x15, Pallas kernels, call(): pl.pallas_call(body, out_shape=[jax.ShapeDtypeStruct(s, jnp.float32) for...  16 us
    ppermute x8, waiting for transfers between devices, swapped(): return lax.ppermute(value, 'depth', pairs + [(j, i) for i, j in pairs])  14.4 us
    ppermute x12, starting transfers between devices, along_strike(): return lax.ppermute(value, 'strike', [(i, (i + by) % n) for i in range(n)])  7.29 us
  transfers between devices with their start and end apart: 20, of which 12 were waited for; matrix products, arithmetic and copies ran while one was open for 0% of the time, Pallas kernels for 14%

profile of v4, /device:TPU:6, one launch (start us, length us, event | category | flops | bytes accessed | tf_op | source)
XLA Modules:
  0.0 82.5 jit_solution(7929269237710102632)
XLA Ops:
  0.7 1.3 %constant_dynamic-update-slice_fusion.1 = f32[12,8,32,128]{3,2,1,0:T(8,128)S(1)} fusion(f32[6,8,32,128]{3,2,1,0:T(8,128)} %param.10), kind=kLoop, calls=%fused_computation.14 | loop fusion | bytes 1572864
  2.0 0.7 shard_map.104.owed
  2.9 0.9 %shard_map.105 = (f32[7,32,128]{2,1,0:T(8,128)S(1)}, f32[7,32,128]{2,1,0:T(8,128)S(1)}) custom-call(f32[12,8,32,128]{3,2,1,0:T(8,128)S(1)} %bitcast_dynamic-update-slice_fusion.fields, f32[8,128]{1,0:T(8,128)S(1)} %copy-done.1, s32[8,128]{1,0:T(8,128)S(1)} %copy-done.2, f32[16,8,128]{2,1,0:T(8,128)S(1)} %shard_map.104.owed), custom_call_target="tpu_custom_call" | custom-call | flops 4000000 | bytes 4000000 | tf_op jit(solution)/shard_map/pallas_call | solution.py:34
  3.7 0.1 collective-permute-start
  3.8 6.4 %collective-permute-start.1 = (f32[7,32,128]{2,1,0:T(8,128)S(1)}, f32[7,32,128]{2,1,0:T(8,128)S(1)}, u32[]{:S(2)}, u32[]{:S(2)}) collective-permute-start(f32[7,32,128]{2,1,0:T(8,128)S(1)} %get-tuple-element.48), channel_id=1, source_target_pairs={{0,248},{8,0},{16,8},{24,16},{32,24},{40,32},{48,40},{56,48},{64,5... | collective-permute-start | bytes 344072 | tf_op jit(solution)/shard_map/ppermute | solution.py:476
  10.2 2.4 %collective-permute-done.from_prev = f32[7,32,128]{2,1,0:T(8,128)S(1)} collective-permute-done((f32[7,32,128]{2,1,0:T(8,128)S(1)}, f32[7,32,128]{2,1,0:T(8,128)S(1)}, u32[]{:S(2)}, u32[]{:S(2)}) %collective-permute-start) | collective-permute-done | bytes 114720 | tf_op jit(solution)/shard_map/ppermute | solution.py:476
  12.6 1.7 %shard_map.106 = (f32[3,12,32,256]{3,2,1,0:T(8,128)S(1)}, f32[5,12,32,256]{3,2,1,0:T(8,128)S(1)}, f32[12,32,256]{2,1,0:T(8,128)S(1)}, f32[3,8,32,256]{3,2,1,0:T(...) custom-call(f32[12,8,32,128]{3,2,1,0:T(8,128)S(1)} %bitcast_dynamic-, ...), custom_call_target="tpu_custom_call" | custom-call | flops 4000000 | bytes 4000000 | tf_op jit(solution)/shard_map/pallas_call | solution.py:34
  14.3 3.0 %collective-permute-start.2 = (f32[12,32,128]{2,1,0:T(8,128)S(1)}, f32[12,32,128]{2,1,0:T(8,128)S(1)}, u32[]{:S(2)}, u32[]{:S(2)}) collective-permute-start(f32[12,32,128]{2,1,0:T(8,128)S(1)} %get-tuple-element.49), channel_id=1, source_target_pairs={{0,1},{2,3},{4,5},{6,7},{1,0},{3,2},{5,4},{7,6},{8,9},{10,11},{12,... | collective-permute-start | bytes 589832 | tf_op jit(solution)/shard_map/ppermute | solution.py:482
  17.3 2.8 %collective-permute-start.3 = (f32[12,32,128]{2,1,0:T(8,128)S(1)}, f32[12,32,128]{2,1,0:T(8,128)S(1)}, u32[]{:S(2)}, u32[]{:S(2)}) collective-permute-start(f32[12,32,128]{2,1,0:T(8,128)S(1)} %get-tuple-element.50), channel_id=1, source_target_pairs={{1,2},{3,4},{5,6},{2,1},{4,3},{6,5},{9,10},{11,12},{13,14},{10,9},... | collective-permute-start | bytes 589832 | tf_op jit(solution)/shard_map/ppermute | solution.py:482
  20.1 1.5 %collective-permute-done.2.one = f32[12,32,128]{2,1,0:T(8,128)S(1)} collective-permute-done((f32[12,32,128]{2,1,0:T(8,128)S(1)}, f32[12,32,128]{2,1,0:T(8,128)S(1)}, u32[]{:S(2)}, u32[]{:S(2)}) %collective-permute-start.2) | collective-permute-done | bytes 196640 | tf_op jit(solution)/shard_map/ppermute | solution.py:482
  21.6 5.7 %collective-permute-done.3.two = f32[12,32,128]{2,1,0:T(8,128)S(1)} collective-permute-done((f32[12,32,128]{2,1,0:T(8,128)S(1)}, f32[12,32,128]{2,1,0:T(8,128)S(1)}, u32[]{:S(2)}, u32[]{:S(2)}) %collective-permute-start.3) | collective-permute-done | bytes 196640 | tf_op jit(solution)/shard_map/ppermute | solution.py:482
  27.2 0.1 shard_map.107
  27.4 0.1 collective-permute-start.7
  27.5 0.1 collective-permute-start.4
  27.5 2.0 %shard_map.108 = (f32[3,12,32,256]{3,2,1,0:T(8,128)S(1)}, f32[5,12,32,256]{3,2,1,0:T(8,128)S(1)}, f32[12,32,256]{2,1,0:T(8,128)S(1)}, f32[16,256]{1,0:T(8,128)S(1)}) custom-call(f32[3,8,32,256]{3,2,1,0:T(8,128)S(1)} %get-tuple-element.53.m.edge_m, ...), custom_call_target="tpu_custom_call", output_to_operand_aliasing={{0}: (7, {}), {1}: (8, {}), {2}: (9, {})} | custom-call | flops 4000000 | bytes 4000000 | tf_op jit(solution)/shard_map/pallas_call | solution.py:34
  29.6 4.4 %collective-permute-done.4.ahead = f32[16,256]{1,0:T(8,128)S(1)} collective-permute-done((f32[16,256]{1,0:T(8,128)S(1)}, f32[16,256]{1,0:T(8,128)S(1)}, u32[]{:S(2)}, u32[]{:S(2)}) %collective-permute-start.4) | collective-permute-done | bytes 16416 | tf_op jit(solution)/shard_map/ppermute | solution.py:476
  34.0 0.8 shard_map.109
  34.9 0.1 collective-permute-start.5
  35.0 5.7 %collective-permute-start.6 = (f32[7,32,128]{2,1,0:T(8,128)S(1)}, f32[7,32,128]{2,1,0:T(8,128)S(1)}, u32[]{:S(2)}, u32[]{:S(2)}) collective-permute-start(f32[7,32,128]{2,1,0:T(8,128)S(1)} %get-tuple-element.65), channel_id=1, source_target_pairs={{1,2},{3,4},{5,6},{2,1},{4,3},{6,5},{9,10},{11,12},{13,14},{10,9},... | collective-permute-start | bytes 344072 | tf_op jit(solution)/shard_map/ppermute | solution.py:482
  40.7 0.1 slice_add_fusion
  40.8 0.1 collective-permute-start.8
  40.9 0.1 collective-permute-start.11
  41.0 0.3 collective-permute-done.5.one
  41.3 3.1 %collective-permute-done.6.two = f32[7,32,128]{2,1,0:T(8,128)S(1)} collective-permute-done((f32[7,32,128]{2,1,0:T(8,128)S(1)}, f32[7,32,128]{2,1,0:T(8,128)S(1)}, u32[]{:S(2)}, u32[]{:S(2)}) %collective-permute-start.6) | collective-permute-done | bytes 114720 | tf_op jit(solution)/shard_map/ppermute | solution.py:482
  44.4 3.0 %collective-permute-done.8.lists = f32[7,16,256]{2,1,0:T(8,128)S(1)} collective-permute-done((f32[7,16,256]{2,1,0:T(8,128)S(1)}, f32[7,16,256]{2,1,0:T(8,128)S(1)}, u32[]{:S(2)}, u32[]{:S(2)}) %collective-permute-start.8) | collective-permute-done | bytes 114720 | tf_op jit(solution)/shard_map/ppermute | solution.py:476
  47.3 0.1 shard_map.110
  47.5 0.1 collective-permute-start.9
  47.6 2.0 %shard_map.111 = (f32[3,12,32,256]{3,2,1,0:T(8,128)S(1)}, f32[5,12,32,256]{3,2,1,0:T(8,128)S(1)}, f32[12,32,256]{2,1,0:T(8,128)S(1)}, f32[16,256]{1,0:T(8,128)S(1)}) custom-call(f32[3,8,32,256]{3,2,1,0:T(8,128)S(1)} %get-tuple-element.53.m.edge_m, ...), custom_call_target="tpu_custom_call", output_to_operand_aliasing={{0}: (7, {}), {1}: (8, {}), {2}: (9, {})} | custom-call | flops 4000000 | bytes 4000000 | tf_op jit(solution)/shard_map/pallas_call | solution.py:34
  49.6 0.8 shard_map.112
  50.5 0.3 collective-permute-start.13
  50.7 5.4 %collective-permute-start.14 = (f32[7,32,128]{2,1,0:T(8,128)S(1)}, f32[7,32,128]{2,1,0:T(8,128)S(1)}, u32[]{:S(2)}, u32[]{:S(2)}) collective-permute-start(f32[7,32,128]{2,1,0:T(8,128)S(1)} %get-tuple-element.77), channel_id=1, source_target_pairs={{1,2},{3,4},{5,6},{2,1},{4,3},{6,5},{9,10},{11,12},{13,14},{10,9},... | collective-permute-start | bytes 344072 | tf_op jit(solution)/shard_map/ppermute | solution.py:482
  56.2 0.1 collective-permute-start.12
  56.3 0.1 collective-permute-start.10
  56.4 1.5 %collective-permute-done.13.one = f32[7,32,128]{2,1,0:T(8,128)S(1)} collective-permute-done((f32[7,32,128]{2,1,0:T(8,128)S(1)}, f32[7,32,128]{2,1,0:T(8,128)S(1)}, u32[]{:S(2)}, u32[]{:S(2)}) %collective-permute-start.13) | collective-permute-done | bytes 114720 | tf_op jit(solution)/shard_map/ppermute | solution.py:482
  57.9 2.3 %collective-permute-done.14.two = f32[7,32,128]{2,1,0:T(8,128)S(1)} collective-permute-done((f32[7,32,128]{2,1,0:T(8,128)S(1)}, f32[7,32,128]{2,1,0:T(8,128)S(1)}, u32[]{:S(2)}, u32[]{:S(2)}) %collective-permute-start.14) | collective-permute-done | bytes 114720 | tf_op jit(solution)/shard_map/ppermute | solution.py:482
  60.2 2.3 %collective-permute-done.12.lists = f32[5,16,256]{2,1,0:T(8,128)S(1)} collective-permute-done((f32[5,16,256]{2,1,0:T(8,128)S(1)}, f32[5,16,256]{2,1,0:T(8,128)S(1)}, u32[]{:S(2)}, u32[]{:S(2)}) %collective-permute-start.12) | collective-permute-done | bytes 81952 | tf_op jit(solution)/shard_map/ppermute | solution.py:476
  62.5 0.1 shard_map.115
  62.6 0.1 collective-permute-start.17
  62.7 2.0 %shard_map.113 = (f32[3,12,32,256]{3,2,1,0:T(8,128)S(1)}, f32[5,12,32,256]{3,2,1,0:T(8,128)S(1)}, f32[12,32,256]{2,1,0:T(8,128)S(1)}, f32[16,256]{1,0:T(8,128)S(1)}) custom-call(f32[3,8,32,256]{3,2,1,0:T(8,128)S(1)} %get-tuple-element.53.m.edge_m, ...), custom_call_target="tpu_custom_call", output_to_operand_aliasing={{0}: (7, {}), {1}: (8, {}), {2}: (9, {})} | custom-call | flops 4000000 | bytes 4000000 | tf_op jit(solution)/shard_map/pallas_call | solution.py:34
  64.7 0.8 shard_map.114
  65.6 0.1 collective-permute-start.15
  65.7 4.5 %collective-permute-start.16 = (f32[7,32,128]{2,1,0:T(8,128)S(1)}, f32[7,32,128]{2,1,0:T(8,128)S(1)}, u32[]{:S(2)}, u32[]{:S(2)}) collective-permute-start(f32[7,32,128]{2,1,0:T(8,128)S(1)} %get-tuple-element.84), channel_id=1, source_target_pairs={{1,2},{3,4},{5,6},{2,1},{4,3},{6,5},{9,10},{11,12},{13,14},{10,9},... | collective-permute-start | bytes 344072 | tf_op jit(solution)/shard_map/ppermute | solution.py:482
  70.2 0.1 collective-permute-start.18
  70.3 5.6 %collective-permute-done.18.lists = f32[3,16,256]{2,1,0:T(8,128)S(1)} collective-permute-done((f32[3,16,256]{2,1,0:T(8,128)S(1)}, f32[3,16,256]{2,1,0:T(8,128)S(1)}, u32[]{:S(2)}, u32[]{:S(2)}) %collective-permute-start.18) | collective-permute-done | bytes 49184 | tf_op jit(solution)/shard_map/ppermute | solution.py:476
  75.9 0.1 shard_map.116
  76.1 2.6 %shard_map.117 = (f32[3,12,32,256]{3,2,1,0:T(8,128)S(1)}, f32[5,12,32,256]{3,2,1,0:T(8,128)S(1)}, f32[12,32,256]{2,1,0:T(8,128)S(1)}, f32[16,256]{1,0:T(8,128)}) custom-call(f32[3,8,32,256]{3,2,1,0:T(8,128)S(1)} %get-tuple-element.53.m.edge_m, ...), custom_call_target="tpu_custom_call", output_to_operand_aliasing={{0}: (7, {}), {1}: (8, {}), {2}: (9, {})} | custom-call | flops 4000000 | bytes 4000000 | tf_op jit(solution)/shard_map/pallas_call | solution.py:34
  78.8 2.6 %collective-permute-done.19.lists = f32[1,16,256]{2,1,0:T(8,128)S(1)} collective-permute-done((f32[1,16,256]{2,1,0:T(8,128)S(1)}, f32[1,16,256]{2,1,0:T(8,128)S(1)}, u32[]{:S(2)}, u32[]{:S(2)}) %collective-permute-start.19) | collective-permute-done | bytes 16416 | tf_op jit(solution)/shard_map/ppermute | solution.py:476
  81.4 1.1 %shard_map.118 = (f32[3,8,32,128]{3,2,1,0:T(8,128)}, f32[6,8,32,128]{3,2,1,0:T(8,128)}) custom-call(f32[2,16,256]{2,1,0:T(8,128)S(1)} %get-tuple-element.56.fp, f32[1,16,256]{2,1,0:T(8,128)S(1)} %collective-permute-done.19.lists, f32[3,12,32,256]{3,2,1,0:T(8,128)S(1)} %get-tuple-element.89.v, f32[5,12,32,256]{3,2,1,0:T(8,128)S(1)} %get-tuple-element.90.s, ...), custom_call_target="tpu_custom_call" | custom-call | flops 4000000 | bytes 4000000 | tf_op jit(solution)/shard_map/pallas_call | solution.py:34
  (38 shorter events, 0.4 us)
Async XLA Ops:
  0.6 1.3 %copy-start.3 = (f32[64]{0:T(128)S(1)}, f32[64]{0:T(128)}, u32[]{:S(2)}) copy-start(f32[64]{0:T(128)} %coefs.1) | copy-start | bytes 772
  0.6 1.3 %copy-start = (f32[64,8,128]{2,1,0:T(8,128)S(1)}, f32[64,8,128]{2,1,0:T(8,128)}, u32[]{:S(2)}) copy-start(f32[64,8,128]{2,1,0:T(8,128)} %past.1) | copy-start | bytes 786436
  0.7 2.1 %copy-start.4 = (f32[3,8,32,128]{3,2,1,0:T(8,128)S(1)}, f32[3,8,32,128]{3,2,1,0:T(8,128)}, u32[]{:S(2)}) copy-start(f32[3,8,32,128]{3,2,1,0:T(8,128)} %param.9) | copy-start | bytes 1179652
  0.7 2.1 %copy-start.5 = (f32[8,32,128]{2,1,0:T(8,128)S(1)}, f32[8,32,128]{2,1,0:T(8,128)}, u32[]{:S(2)}) copy-start(f32[8,32,128]{2,1,0:T(8,128)} %param.11) | copy-start | bytes 393220
  0.7 2.1 %copy-start.6 = (f32[8,32,128]{2,1,0:T(8,128)S(1)}, f32[8,32,128]{2,1,0:T(8,128)}, u32[]{:S(2)}) copy-start(f32[8,32,128]{2,1,0:T(8,128)} %param.12) | copy-start | bytes 393220
  0.7 2.1 %copy-start.7 = (f32[8,32,128]{2,1,0:T(8,128)S(1)}, f32[8,32,128]{2,1,0:T(8,128)}, u32[]{:S(2)}) copy-start(f32[8,32,128]{2,1,0:T(8,128)} %param.13) | copy-start | bytes 393220
  0.7 2.2 %copy-start.2 = (s32[8,128]{1,0:T(8,128)S(1)}, s32[8,128]{1,0:T(8,128)}, u32[]{:S(2)}) copy-start(s32[8,128]{1,0:T(8,128)} %mask.3) | copy-start | bytes 12292
  0.7 2.2 %copy-start.1 = (f32[8,128]{1,0:T(8,128)S(1)}, f32[8,128]{1,0:T(8,128)}, u32[]{:S(2)}) copy-start(f32[8,128]{1,0:T(8,128)} %pre.3) | copy-start | bytes 12292
  3.7 8.9 %collective-permute-start = (f32[7,32,128]{2,1,0:T(8,128)S(1)}, f32[7,32,128]{2,1,0:T(8,128)S(1)}, u32[]{:S(2)}, u32[]{:S(2)}) collective-permute-start(f32[7,32,128]{2,1,0:T(8,128)S(1)} %get-tuple-element.47), channel_id=1, source_target_pairs={{0,8},{8,16},{16,24},{24,32},{32,40},{40,48},{48,56},{56,64},{64,7... | collective-permute-start | bytes 344072 | tf_op jit(solution)/shard_map/ppermute | solution.py:476
  3.8 8.8 %collective-permute-start.1 = (f32[7,32,128]{2,1,0:T(8,128)S(1)}, f32[7,32,128]{2,1,0:T(8,128)S(1)}, u32[]{:S(2)}, u32[]{:S(2)}) collective-permute-start(f32[7,32,128]{2,1,0:T(8,128)S(1)} %get-tuple-element.48), channel_id=1, source_target_pairs={{0,248},{8,0},{16,8},{24,16},{32,24},{40,32},{48,40},{56,48},{64,5... | collective-permute-start | bytes 344072 | tf_op jit(solution)/shard_map/ppermute | solution.py:476
  14.3 7.3 %collective-permute-start.2 = (f32[12,32,128]{2,1,0:T(8,128)S(1)}, f32[12,32,128]{2,1,0:T(8,128)S(1)}, u32[]{:S(2)}, u32[]{:S(2)}) collective-permute-start(f32[12,32,128]{2,1,0:T(8,128)S(1)} %get-tuple-element.49), channel_id=1, source_target_pairs={{0,1},{2,3},{4,5},{6,7},{1,0},{3,2},{5,4},{7,6},{8,9},{10,11},{12,... | collective-permute-start | bytes 589832 | tf_op jit(solution)/shard_map/ppermute | solution.py:482
  17.3 10.0 %collective-permute-start.3 = (f32[12,32,128]{2,1,0:T(8,128)S(1)}, f32[12,32,128]{2,1,0:T(8,128)S(1)}, u32[]{:S(2)}, u32[]{:S(2)}) collective-permute-start(f32[12,32,128]{2,1,0:T(8,128)S(1)} %get-tuple-element.50), channel_id=1, source_target_pairs={{1,2},{3,4},{5,6},{2,1},{4,3},{6,5},{9,10},{11,12},{13,14},{10,9},... | collective-permute-start | bytes 589832 | tf_op jit(solution)/shard_map/ppermute | solution.py:482
  27.4 13.3 %collective-permute-start.7 = (f32[7,16,256]{2,1,0:T(8,128)S(1)}, f32[7,16,256]{2,1,0:T(8,128)S(1)}, u32[]{:S(2)}, u32[]{:S(2)}) collective-permute-start(f32[7,16,256]{2,1,0:T(8,128)S(1)} %get-tuple-element.67), channel_id=1, source_target_pairs={{0,8},{8,16},{16,24},{24,32},{32,40},{40,48},{48,56},{56,64},{64,7... | collective-permute-start | bytes 344072 | tf_op jit(solution)/shard_map/ppermute | solution.py:476
  27.5 6.6 %collective-permute-start.4 = (f32[16,256]{1,0:T(8,128)S(1)}, f32[16,256]{1,0:T(8,128)S(1)}, u32[]{:S(2)}, u32[]{:S(2)}) collective-permute-start(f32[16,256]{1,0:T(8,128)S(1)} %get-tuple-element.57), channel_id=1, source_target_pairs={{0,8},{8,16},{16,24},{24,32},{32,40},{40,48},{48,56},{56,64},{64,7... | collective-permute-start | bytes 49160 | tf_op jit(solution)/shard_map/ppermute | solution.py:476
  34.9 6.4 %collective-permute-start.5 = (f32[7,32,128]{2,1,0:T(8,128)S(1)}, f32[7,32,128]{2,1,0:T(8,128)S(1)}, u32[]{:S(2)}, u32[]{:S(2)}) collective-permute-start(f32[7,32,128]{2,1,0:T(8,128)S(1)} %get-tuple-element.64), channel_id=1, source_target_pairs={{0,1},{2,3},{4,5},{6,7},{1,0},{3,2},{5,4},{7,6},{8,9},{10,11},{12,... | collective-permute-start | bytes 344072 | tf_op jit(solution)/shard_map/ppermute | solution.py:482
  35.0 9.4 %collective-permute-start.6 = (f32[7,32,128]{2,1,0:T(8,128)S(1)}, f32[7,32,128]{2,1,0:T(8,128)S(1)}, u32[]{:S(2)}, u32[]{:S(2)}) collective-permute-start(f32[7,32,128]{2,1,0:T(8,128)S(1)} %get-tuple-element.65), channel_id=1, source_target_pairs={{1,2},{3,4},{5,6},{2,1},{4,3},{6,5},{9,10},{11,12},{13,14},{10,9},... | collective-permute-start | bytes 344072 | tf_op jit(solution)/shard_map/ppermute | solution.py:482
  40.8 6.6 %collective-permute-start.8 = (f32[7,16,256]{2,1,0:T(8,128)S(1)}, f32[7,16,256]{2,1,0:T(8,128)S(1)}, u32[]{:S(2)}, u32[]{:S(2)}) collective-permute-start(f32[7,16,256]{2,1,0:T(8,128)S(1)} %pad_maximum_fusion), channel_id=1, source_target_pairs={{0,8},{8,16},{16,24},{24,32},{32,40},{40,48},{48,56},{56,64},{64,7... | collective-permute-start | bytes 344072 | tf_op jit(solution)/shard_map/ppermute | solution.py:476
  40.9 8.7 %collective-permute-start.11 = (f32[16,256]{1,0:T(8,128)S(1)}, f32[16,256]{1,0:T(8,128)S(1)}, u32[]{:S(2)}, u32[]{:S(2)}) collective-permute-start(f32[16,256]{1,0:T(8,128)S(1)} %slice_bitcast_fusion.2), channel_id=1, source_target_pairs={{0,16},{8,24},{16,32},{24,40},{32,48},{40,56},{48,64},{56,72},{64,... | collective-permute-start | bytes 49160 | tf_op jit(solution)/shard_map/ppermute | solution.py:476
  47.5 8.7 %collective-permute-start.9 = (f32[5,16,256]{2,1,0:T(8,128)S(1)}, f32[5,16,256]{2,1,0:T(8,128)S(1)}, u32[]{:S(2)}, u32[]{:S(2)}) collective-permute-start(f32[5,16,256]{2,1,0:T(8,128)S(1)} %shard_map.110), channel_id=1, source_target_pairs={{0,8},{8,16},{16,24},{24,32},{32,40},{40,48},{48,56},{56,64},{64,7... | collective-permute-start | bytes 245768 | tf_op jit(solution)/shard_map/ppermute | solution.py:476
  50.5 7.5 %collective-permute-start.13 = (f32[7,32,128]{2,1,0:T(8,128)S(1)}, f32[7,32,128]{2,1,0:T(8,128)S(1)}, u32[]{:S(2)}, u32[]{:S(2)}) collective-permute-start(f32[7,32,128]{2,1,0:T(8,128)S(1)} %get-tuple-element.76), channel_id=1, source_target_pairs={{0,1},{2,3},{4,5},{6,7},{1,0},{3,2},{5,4},{7,6},{8,9},{10,11},{12,... | collective-permute-start | bytes 344072 | tf_op jit(solution)/shard_map/ppermute | solution.py:482
  50.7 9.5 %collective-permute-start.14 = (f32[7,32,128]{2,1,0:T(8,128)S(1)}, f32[7,32,128]{2,1,0:T(8,128)S(1)}, u32[]{:S(2)}, u32[]{:S(2)}) collective-permute-start(f32[7,32,128]{2,1,0:T(8,128)S(1)} %get-tuple-element.77), channel_id=1, source_target_pairs={{1,2},{3,4},{5,6},{2,1},{4,3},{6,5},{9,10},{11,12},{13,14},{10,9},... | collective-permute-start | bytes 344072 | tf_op jit(solution)/shard_map/ppermute | solution.py:482
  56.2 6.2 %collective-permute-start.12 = (f32[5,16,256]{2,1,0:T(8,128)S(1)}, f32[5,16,256]{2,1,0:T(8,128)S(1)}, u32[]{:S(2)}, u32[]{:S(2)}) collective-permute-start(f32[5,16,256]{2,1,0:T(8,128)S(1)} %pad_maximum_fusion.1), channel_id=1, source_target_pairs={{0,8},{8,16},{16,24},{24,32},{32,40},{40,48},{48,56},{56,64},{64,7... | collective-permute-start | bytes 245768 | tf_op jit(solution)/shard_map/ppermute | solution.py:476
  56.3 8.4 %collective-permute-start.10 = (f32[16,256]{1,0:T(8,128)S(1)}, f32[16,256]{1,0:T(8,128)S(1)}, u32[]{:S(2)}, u32[]{:S(2)}) collective-permute-start(f32[16,256]{1,0:T(8,128)S(1)} %slice_bitcast_fusion.3), channel_id=1, source_target_pairs={{0,16},{8,24},{16,32},{24,40},{32,48},{40,56},{48,64},{56,72},{64,... | collective-permute-start | bytes 49160 | tf_op jit(solution)/shard_map/ppermute | solution.py:476
  62.6 7.6 %collective-permute-start.17 = (f32[3,16,256]{2,1,0:T(8,128)S(1)}, f32[3,16,256]{2,1,0:T(8,128)S(1)}, u32[]{:S(2)}, u32[]{:S(2)}) collective-permute-start(f32[3,16,256]{2,1,0:T(8,128)S(1)} %shard_map.115), channel_id=1, source_target_pairs={{0,8},{8,16},{16,24},{24,32},{32,40},{40,48},{48,56},{56,64},{64,7... | collective-permute-start | bytes 147464 | tf_op jit(solution)/shard_map/ppermute | solution.py:476
  65.6 10.4 %collective-permute-start.15 = (f32[7,32,128]{2,1,0:T(8,128)S(1)}, f32[7,32,128]{2,1,0:T(8,128)S(1)}, u32[]{:S(2)}, u32[]{:S(2)}) collective-permute-start(f32[7,32,128]{2,1,0:T(8,128)S(1)} %get-tuple-element.83), channel_id=1, source_target_pairs={{0,1},{2,3},{4,5},{6,7},{1,0},{3,2},{5,4},{7,6},{8,9},{10,11},{12,... | collective-permute-start | bytes 344072 | tf_op jit(solution)/shard_map/ppermute | solution.py:482
  65.7 10.3 %collective-permute-start.16 = (f32[7,32,128]{2,1,0:T(8,128)S(1)}, f32[7,32,128]{2,1,0:T(8,128)S(1)}, u32[]{:S(2)}, u32[]{:S(2)}) collective-permute-start(f32[7,32,128]{2,1,0:T(8,128)S(1)} %get-tuple-element.84), channel_id=1, source_target_pairs={{1,2},{3,4},{5,6},{2,1},{4,3},{6,5},{9,10},{11,12},{13,14},{10,9},... | collective-permute-start | bytes 344072 | tf_op jit(solution)/shard_map/ppermute | solution.py:482
  70.2 5.7 %collective-permute-start.18 = (f32[3,16,256]{2,1,0:T(8,128)S(1)}, f32[3,16,256]{2,1,0:T(8,128)S(1)}, u32[]{:S(2)}, u32[]{:S(2)}) collective-permute-start(f32[3,16,256]{2,1,0:T(8,128)S(1)} %pad_maximum_fusion.2), channel_id=1, source_target_pairs={{0,8},{8,16},{16,24},{24,32},{32,40},{40,48},{48,56},{56,64},{64,7... | collective-permute-start | bytes 147464 | tf_op jit(solution)/shard_map/ppermute | solution.py:476
  76.0 5.3 %collective-permute-start.19 = (f32[1,16,256]{2,1,0:T(8,128)S(1)}, f32[1,16,256]{2,1,0:T(8,128)S(1)}, u32[]{:S(2)}, u32[]{:S(2)}) collective-permute-start(f32[1,16,256]{2,1,0:T(8,128)S(1)} %shard_map.116), channel_id=1, source_target_pairs={{0,8},{8,16},{16,24},{24,32},{32,40},{40,48},{48,56},{56,64},{64,7... | collective-permute-start | bytes 49160 | tf_op jit(solution)/shard_map/ppermute | solution.py:476

commit v5 on v4

--- a/solution.py
+++ b/solution.py
@@ -197,11 +197,11 @@
         plane = past[k]
         for j in range(min(STEPS, HIST - k)):
             old = sums[j][k % 2]
-            term = coefs[j + k] * plane
+            term = coefs[j + k : j + k + 1, :] * plane
             sums[j][k % 2] = term if old is None else old + term
     for j in range(STEPS):
         owed[j] = sums[j][0] + sums[j][1]
-        owed[STEPS + j] = jnp.full((8, LANES), coefs[j])
+        owed[STEPS + j] = jnp.broadcast_to(coefs[j : j + 1, :], (8, LANES))
 
 
 def coef(owed, j):
@@ -279,7 +279,7 @@
             v[f, z] += change
         return carry
 
-    lax.fori_loop(2, 10, step, 0, unroll=4)
+    lax.fori_loop(2, 10, step, 0, unroll=8)
     ahead[...] = lists[1]
     for z in range(3, 10):
         ahead[z : z + 1, :] = lists[1, z : z + 1, :] + coef(owed, 0) * rate_at(v, z)
@@ -416,7 +416,7 @@
         slide(q, fp, z, fp[0, pl.ds(z, 1), :] + FRIC * rate_at(v, z))
         return carry
 
-    lax.fori_loop(2, 10, own_stress_a, 0, unroll=4)
+    lax.fori_loop(2, 10, own_stress_a, 0, unroll=8)
     change = velocity_change(
         lambda f, z: more_above[f] if z == 10 else s[f - SXX, 9], 10, edge_m[0, 1], (VX, VY)
     )
@@ -426,11 +426,11 @@
         lambda f, z: more_below.get(f, nothing) if z == 1 else s[f - SXX, 2], 1, edge_m[0, 0], (VZ,)
     )
     v[VZ, 1] = got.plane(False, 5) + below[VZ] + change[VZ]
-    lax.fori_loop(2, 10, own_velocity_b, 0, unroll=4)
+    lax.fori_loop(2, 10, own_velocity_b, 0, unroll=8)
     rates[...] = jnp.zeros_like(rates)
     for z in range(2, 11):
         rates[z : z + 1, :] = rate_at(v, z)
-    lax.fori_loop(2, 10, own_stress_b, 0, unroll=4)
+    lax.fori_loop(2, 10, own_stress_b, 0, unroll=8)
     s[sxz, 1] = nothing
     s[syz, 1] = nothing
     s[szz, 10] = nothing
@@ -449,7 +449,7 @@
             v[f, z] = v_in[f, z] + change
         return carry
 
-    lax.fori_loop(2, 10, step, 0, unroll=4)
+    lax.fori_loop(2, 10, step, 0, unroll=8)
     up, down = traces(refs, fp)
     post(packed(up), packed(down), one, two)
     for z in range(3, 10):
@@ -484,7 +484,8 @@
 
 def per_device(velocity, stress, b, lam, mu, past, coefs, pre, mask):
     edge = (7, NY, LANES)
-    (owed,) = call(owed_kernel, [(2 * STEPS, 8, LANES)], [coefs, past], smem=(0,))
+    rows = jnp.broadcast_to(coefs[:, None], (HIST, LANES))
+    (owed,) = call(owed_kernel, [(2 * STEPS, 8, LANES)], [rows, past])
     fields = jnp.concatenate([stress, velocity, DT * b[None], DT * lam[None], DT * mu[None]])
     to_next, to_prev = call(edges_kernel, [edge, edge], [fields, pre, mask, owed])
     from_prev = along_strike(to_next, 1)

time: 83.6 us -> 82.2 us (0.983)
  Pallas kernels: 16 us -> 14 us
    pallas_call x15, Pallas kernels: 16 us -> 14 us  [call(): pl.pallas_call(body, out_shape=[jax.ShapeDtypeStruct(s, jnp.float32) for...]
    ppermute x12, waiting for transfers between devices: 20.3 us -> 21.3 us  [along_strike(): return lax.ppermute(value, 'strike', [(i, (i + by) % n) for i in range(n)])]
  transfers between devices with their start and end apart: 20 -> 20, of which waited for: 12 -> 12; matrix products, arithmetic and copies ran while one was open for 0% -> 0% of each run, Pallas kernels for 14% -> 12%
where the time goes in v5:
time: 82.2 us; the launch traced here: 81.5 us
  waiting for transfers between devices  35.5 us (43%)
  starting transfers between devices  29.1 us (35%)
  Pallas kernels  14 us (17%)
  local copies, waits for them, and re-layouts  1.41 us (2%)
  between operations  1.08 us (1%)
    ppermute x8, starting transfers between devices, swapped(): return lax.ppermute(value, 'depth', pairs + [(j, i) for i, j in pairs])  21.7 us
    ppermute x12, waiting for transfers between devices, along_strike(): return lax.ppermute(value, 'strike', [(i, (i + by) % n) for i in range(n)])  21.3 us
    ppermute x8, waiting for transfers between devices, swapped(): return lax.ppermute(value, 'depth', pairs + [(j, i) for i, j in pairs])  14.2 us
    pallas_call x15, Pallas kernels, call(): pl.pallas_call(body, out_shape=[jax.ShapeDtypeStruct(s, jnp.float32) for...  14 us
    ppermute x12, starting transfers between devices, along_strike(): return lax.ppermute(value, 'strike', [(i, (i + by) % n) for i in range(n)])  7.47 us
  transfers between devices with their start and end apart: 20, of which 12 were waited for; matrix products, arithmetic and copies ran while one was open for 0% of the time, Pallas kernels for 12%

profile of v5, /device:TPU:6, one launch (start us, length us, event | category | flops | bytes accessed | tf_op | source)
XLA Modules:
  0.0 81.5 jit_solution(8852884257658784812)
XLA Ops:
  0.7 1.3 %constant_dynamic-update-slice_fusion.1 = f32[12,8,32,128]{3,2,1,0:T(8,128)S(1)} fusion(f32[6,8,32,128]{3,2,1,0:T(8,128)} %param.10), kind=kLoop, calls=%fused_computation.14 | loop fusion | bytes 1572864
  2.1 0.2 shard_map.104.owed
  2.4 0.9 %shard_map.105 = (f32[7,32,128]{2,1,0:T(8,128)S(1)}, f32[7,32,128]{2,1,0:T(8,128)S(1)}) custom-call(f32[12,8,32,128]{3,2,1,0:T(8,128)S(1)} %bitcast_dynamic-update-slice_fusion.fields, f32[8,128]{1,0:T(8,128)S(1)} %copy-done.1, s32[8,128]{1,0:T(8,128)S(1)} %copy-done.2, f32[16,8,128]{2,1,0:T(8,128)S(1)} %shard_map.104.owed), custom_call_target="tpu_custom_call" | custom-call | flops 4000000 | bytes 4000000 | tf_op jit(solution)/shard_map/pallas_call | solution.py:34
  3.3 0.1 collective-permute-start
  3.4 6.4 %collective-permute-start.1 = (f32[7,32,128]{2,1,0:T(8,128)S(1)}, f32[7,32,128]{2,1,0:T(8,128)S(1)}, u32[]{:S(2)}, u32[]{:S(2)}) collective-permute-start(f32[7,32,128]{2,1,0:T(8,128)S(1)} %get-tuple-element.48), channel_id=1, source_target_pairs={{0,248},{8,0},{16,8},{24,16},{32,24},{40,32},{48,40},{56,48},{64,5... | collective-permute-start | bytes 344072 | tf_op jit(solution)/shard_map/ppermute | solution.py:476
  9.7 2.4 %collective-permute-done.from_prev = f32[7,32,128]{2,1,0:T(8,128)S(1)} collective-permute-done((f32[7,32,128]{2,1,0:T(8,128)S(1)}, f32[7,32,128]{2,1,0:T(8,128)S(1)}, u32[]{:S(2)}, u32[]{:S(2)}) %collective-permute-start) | collective-permute-done | bytes 114720 | tf_op jit(solution)/shard_map/ppermute | solution.py:476
  12.1 1.6 %shard_map.106 = (f32[3,12,32,256]{3,2,1,0:T(8,128)S(1)}, f32[5,12,32,256]{3,2,1,0:T(8,128)S(1)}, f32[12,32,256]{2,1,0:T(8,128)S(1)}, f32[3,8,32,256]{3,2,1,0:T(...) custom-call(f32[12,8,32,128]{3,2,1,0:T(8,128)S(1)} %bitcast_dynamic-, ...), custom_call_target="tpu_custom_call" | custom-call | flops 4000000 | bytes 4000000 | tf_op jit(solution)/shard_map/pallas_call | solution.py:34
  13.7 3.0 %collective-permute-start.2 = (f32[12,32,128]{2,1,0:T(8,128)S(1)}, f32[12,32,128]{2,1,0:T(8,128)S(1)}, u32[]{:S(2)}, u32[]{:S(2)}) collective-permute-start(f32[12,32,128]{2,1,0:T(8,128)S(1)} %get-tuple-element.49), channel_id=1, source_target_pairs={{0,1},{2,3},{4,5},{6,7},{1,0},{3,2},{5,4},{7,6},{8,9},{10,11},{12,... | collective-permute-start | bytes 589832 | tf_op jit(solution)/shard_map/ppermute | solution.py:482
  16.7 2.8 %collective-permute-start.3 = (f32[12,32,128]{2,1,0:T(8,128)S(1)}, f32[12,32,128]{2,1,0:T(8,128)S(1)}, u32[]{:S(2)}, u32[]{:S(2)}) collective-permute-start(f32[12,32,128]{2,1,0:T(8,128)S(1)} %get-tuple-element.50), channel_id=1, source_target_pairs={{1,2},{3,4},{5,6},{2,1},{4,3},{6,5},{9,10},{11,12},{13,14},{10,9},... | collective-permute-start | bytes 589832 | tf_op jit(solution)/shard_map/ppermute | solution.py:482
  19.5 1.5 %collective-permute-done.2.one = f32[12,32,128]{2,1,0:T(8,128)S(1)} collective-permute-done((f32[12,32,128]{2,1,0:T(8,128)S(1)}, f32[12,32,128]{2,1,0:T(8,128)S(1)}, u32[]{:S(2)}, u32[]{:S(2)}) %collective-permute-start.2) | collective-permute-done | bytes 196640 | tf_op jit(solution)/shard_map/ppermute | solution.py:482
  21.0 5.7 %collective-permute-done.3.two = f32[12,32,128]{2,1,0:T(8,128)S(1)} collective-permute-done((f32[12,32,128]{2,1,0:T(8,128)S(1)}, f32[12,32,128]{2,1,0:T(8,128)S(1)}, u32[]{:S(2)}, u32[]{:S(2)}) %collective-permute-start.3) | collective-permute-done | bytes 196640 | tf_op jit(solution)/shard_map/ppermute | solution.py:482
  26.7 0.1 shard_map.107
  26.8 0.1 collective-permute-start.7
  26.9 0.1 collective-permute-start.4
  27.0 1.8 %shard_map.108 = (f32[3,12,32,256]{3,2,1,0:T(8,128)S(1)}, f32[5,12,32,256]{3,2,1,0:T(8,128)S(1)}, f32[12,32,256]{2,1,0:T(8,128)S(1)}, f32[16,256]{1,0:T(8,128)S(1)}) custom-call(f32[3,8,32,256]{3,2,1,0:T(8,128)S(1)} %get-tuple-element.53.m.edge_m, ...), custom_call_target="tpu_custom_call", output_to_operand_aliasing={{0}: (7, {}), {1}: (8, {}), {2}: (9, {})} | custom-call | flops 4000000 | bytes 4000000 | tf_op jit(solution)/shard_map/pallas_call | solution.py:34
  28.8 4.6 %collective-permute-done.4.ahead = f32[16,256]{1,0:T(8,128)S(1)} collective-permute-done((f32[16,256]{1,0:T(8,128)S(1)}, f32[16,256]{1,0:T(8,128)S(1)}, u32[]{:S(2)}, u32[]{:S(2)}) %collective-permute-start.4) | collective-permute-done | bytes 16416 | tf_op jit(solution)/shard_map/ppermute | solution.py:476
  33.4 0.8 shard_map.109
  34.2 0.1 collective-permute-start.5
  34.3 5.7 %collective-permute-start.6 = (f32[7,32,128]{2,1,0:T(8,128)S(1)}, f32[7,32,128]{2,1,0:T(8,128)S(1)}, u32[]{:S(2)}, u32[]{:S(2)}) collective-permute-start(f32[7,32,128]{2,1,0:T(8,128)S(1)} %get-tuple-element.65), channel_id=1, source_target_pairs={{1,2},{3,4},{5,6},{2,1},{4,3},{6,5},{9,10},{11,12},{13,14},{10,9},... | collective-permute-start | bytes 344072 | tf_op jit(solution)/shard_map/ppermute | solution.py:482
  40.1 0.1 slice_add_fusion
  40.2 0.1 collective-permute-start.8
  40.3 0.1 collective-permute-start.11
  40.4 0.2 collective-permute-done.5.one
  40.6 3.1 %collective-permute-done.6.two = f32[7,32,128]{2,1,0:T(8,128)S(1)} collective-permute-done((f32[7,32,128]{2,1,0:T(8,128)S(1)}, f32[7,32,128]{2,1,0:T(8,128)S(1)}, u32[]{:S(2)}, u32[]{:S(2)}) %collective-permute-start.6) | collective-permute-done | bytes 114720 | tf_op jit(solution)/shard_map/ppermute | solution.py:482
  43.7 3.1 %collective-permute-done.8.lists = f32[7,16,256]{2,1,0:T(8,128)S(1)} collective-permute-done((f32[7,16,256]{2,1,0:T(8,128)S(1)}, f32[7,16,256]{2,1,0:T(8,128)S(1)}, u32[]{:S(2)}, u32[]{:S(2)}) %collective-permute-start.8) | collective-permute-done | bytes 114720 | tf_op jit(solution)/shard_map/ppermute | solution.py:476
  46.7 0.1 shard_map.110
  46.8 0.3 collective-permute-start.9
  47.1 1.8 %shard_map.111 = (f32[3,12,32,256]{3,2,1,0:T(8,128)S(1)}, f32[5,12,32,256]{3,2,1,0:T(8,128)S(1)}, f32[12,32,256]{2,1,0:T(8,128)S(1)}, f32[16,256]{1,0:T(8,128)S(1)}) custom-call(f32[3,8,32,256]{3,2,1,0:T(8,128)S(1)} %get-tuple-element.53.m.edge_m, ...), custom_call_target="tpu_custom_call", output_to_operand_aliasing={{0}: (7, {}), {1}: (8, {}), {2}: (9, {})} | custom-call | flops 4000000 | bytes 4000000 | tf_op jit(solution)/shard_map/pallas_call | solution.py:34
  49.0 0.8 %shard_map.112 = (f32[3,12,32,256]{3,2,1,0:T(8,128)S(1)}, f32[12,32,256]{2,1,0:T(8,128)S(1)}, f32[7,32,128]{2,1,0:T(8,128)S(1)}, f32[7,32,128]{2,1,0:T(8,128)S(1)}, f32[16,256]{1,0:T(8,128)S(1)}) custom-call(f32[16,8,128]{2,1,0:T(8,128)S(1)} %shard_map.104.owed, ...), custom_call_target="tpu_custom_call", output_to_operand_aliasing={{0}: (6, {}), {1}: (7, {})} | custom-call | flops 4000000 | bytes 4000000 | tf_op jit(solution)/shard_map/pallas_call | solution.py:34
  49.8 0.1 collective-permute-start.13
  49.9 5.4 %collective-permute-start.14 = (f32[7,32,128]{2,1,0:T(8,128)S(1)}, f32[7,32,128]{2,1,0:T(8,128)S(1)}, u32[]{:S(2)}, u32[]{:S(2)}) collective-permute-start(f32[7,32,128]{2,1,0:T(8,128)S(1)} %get-tuple-element.77), channel_id=1, source_target_pairs={{1,2},{3,4},{5,6},{2,1},{4,3},{6,5},{9,10},{11,12},{13,14},{10,9},... | collective-permute-start | bytes 344072 | tf_op jit(solution)/shard_map/ppermute | solution.py:482
  55.4 0.1 collective-permute-start.12
  55.5 0.1 collective-permute-start.10
  55.6 1.5 %collective-permute-done.13.one = f32[7,32,128]{2,1,0:T(8,128)S(1)} collective-permute-done((f32[7,32,128]{2,1,0:T(8,128)S(1)}, f32[7,32,128]{2,1,0:T(8,128)S(1)}, u32[]{:S(2)}, u32[]{:S(2)}) %collective-permute-start.13) | collective-permute-done | bytes 114720 | tf_op jit(solution)/shard_map/ppermute | solution.py:482
  57.1 2.2 %collective-permute-done.14.two = f32[7,32,128]{2,1,0:T(8,128)S(1)} collective-permute-done((f32[7,32,128]{2,1,0:T(8,128)S(1)}, f32[7,32,128]{2,1,0:T(8,128)S(1)}, u32[]{:S(2)}, u32[]{:S(2)}) %collective-permute-start.14) | collective-permute-done | bytes 114720 | tf_op jit(solution)/shard_map/ppermute | solution.py:482
  59.3 2.3 %collective-permute-done.12.lists = f32[5,16,256]{2,1,0:T(8,128)S(1)} collective-permute-done((f32[5,16,256]{2,1,0:T(8,128)S(1)}, f32[5,16,256]{2,1,0:T(8,128)S(1)}, u32[]{:S(2)}, u32[]{:S(2)}) %collective-permute-start.12) | collective-permute-done | bytes 81952 | tf_op jit(solution)/shard_map/ppermute | solution.py:476
  61.6 0.1 shard_map.115
  61.8 1.8 %shard_map.113 = (f32[3,12,32,256]{3,2,1,0:T(8,128)S(1)}, f32[5,12,32,256]{3,2,1,0:T(8,128)S(1)}, f32[12,32,256]{2,1,0:T(8,128)S(1)}, f32[16,256]{1,0:T(8,128)S(1)}) custom-call(f32[3,8,32,256]{3,2,1,0:T(8,128)S(1)} %get-tuple-element.53.m.edge_m, ...), custom_call_target="tpu_custom_call", output_to_operand_aliasing={{0}: (7, {}), {1}: (8, {}), {2}: (9, {})} | custom-call | flops 4000000 | bytes 4000000 | tf_op jit(solution)/shard_map/pallas_call | solution.py:34
  63.7 0.8 %shard_map.114 = (f32[3,12,32,256]{3,2,1,0:T(8,128)S(1)}, f32[12,32,256]{2,1,0:T(8,128)S(1)}, f32[7,32,128]{2,1,0:T(8,128)S(1)}, f32[7,32,128]{2,1,0:T(8,128)S(1)}, f32[16,256]{1,0:T(8,128)S(1)}) custom-call(f32[16,8,128]{2,1,0:T(8,128)S(1)} %shard_map.104.owed, ...), custom_call_target="tpu_custom_call", output_to_operand_aliasing={{0}: (6, {}), {1}: (7, {})} | custom-call | flops 4000000 | bytes 4000000 | tf_op jit(solution)/shard_map/pallas_call | solution.py:34
  64.5 0.1 collective-permute-start.15
  64.6 4.5 %collective-permute-start.16 = (f32[7,32,128]{2,1,0:T(8,128)S(1)}, f32[7,32,128]{2,1,0:T(8,128)S(1)}, u32[]{:S(2)}, u32[]{:S(2)}) collective-permute-start(f32[7,32,128]{2,1,0:T(8,128)S(1)} %get-tuple-element.84), channel_id=1, source_target_pairs={{1,2},{3,4},{5,6},{2,1},{4,3},{6,5},{9,10},{11,12},{13,14},{10,9},... | collective-permute-start | bytes 344072 | tf_op jit(solution)/shard_map/ppermute | solution.py:482
  69.2 0.1 collective-permute-start.18
  69.3 5.6 %collective-permute-done.18.lists = f32[3,16,256]{2,1,0:T(8,128)S(1)} collective-permute-done((f32[3,16,256]{2,1,0:T(8,128)S(1)}, f32[3,16,256]{2,1,0:T(8,128)S(1)}, u32[]{:S(2)}, u32[]{:S(2)}) %collective-permute-start.18) | collective-permute-done | bytes 49184 | tf_op jit(solution)/shard_map/ppermute | solution.py:476
  74.9 0.1 shard_map.116
  75.0 0.1 collective-permute-start.19
  75.1 2.0 %shard_map.117 = (f32[3,12,32,256]{3,2,1,0:T(8,128)S(1)}, f32[5,12,32,256]{3,2,1,0:T(8,128)S(1)}, f32[12,32,256]{2,1,0:T(8,128)S(1)}, f32[16,256]{1,0:T(8,128)}) custom-call(f32[3,8,32,256]{3,2,1,0:T(8,128)S(1)} %get-tuple-element.53.m.edge_m, ...), custom_call_target="tpu_custom_call", output_to_operand_aliasing={{0}: (7, {}), {1}: (8, {}), {2}: (9, {})} | custom-call | flops 4000000 | bytes 4000000 | tf_op jit(solution)/shard_map/pallas_call | solution.py:34
  77.1 3.3 %collective-permute-done.19.lists = f32[1,16,256]{2,1,0:T(8,128)S(1)} collective-permute-done((f32[1,16,256]{2,1,0:T(8,128)S(1)}, f32[1,16,256]{2,1,0:T(8,128)S(1)}, u32[]{:S(2)}, u32[]{:S(2)}) %collective-permute-start.19) | collective-permute-done | bytes 16416 | tf_op jit(solution)/shard_map/ppermute | solution.py:476
  80.4 1.1 %shard_map.118 = (f32[3,8,32,128]{3,2,1,0:T(8,128)}, f32[6,8,32,128]{3,2,1,0:T(8,128)}) custom-call(f32[2,16,256]{2,1,0:T(8,128)S(1)} %get-tuple-element.56.fp, f32[1,16,256]{2,1,0:T(8,128)S(1)} %collective-permute-done.19.lists, f32[3,12,32,256]{3,2,1,0:T(8,128)S(1)} %get-tuple-element.89.v, f32[5,12,32,256]{3,2,1,0:T(8,128)S(1)} %get-tuple-element.90.s, ...), custom_call_target="tpu_custom_call" | custom-call | flops 4000000 | bytes 4000000 | tf_op jit(solution)/shard_map/pallas_call | solution.py:34
  (39 shorter events, 0.5 us)
Async XLA Ops:
  0.6 1.4 %copy-start = (f32[64,8,128]{2,1,0:T(8,128)S(1)}, f32[64,8,128]{2,1,0:T(8,128)}, u32[]{:S(2)}) copy-start(f32[64,8,128]{2,1,0:T(8,128)} %past.1) | copy-start | bytes 786436
  0.6 1.3 %copy-start.7 = (f32[64]{0:T(128)S(1)}, f32[64]{0:T(128)}, u32[]{:S(2)}) copy-start(f32[64]{0:T(128)} %param.15) | copy-start | bytes 772
  0.7 1.6 %copy-start.3 = (f32[3,8,32,128]{3,2,1,0:T(8,128)S(1)}, f32[3,8,32,128]{3,2,1,0:T(8,128)}, u32[]{:S(2)}) copy-start(f32[3,8,32,128]{3,2,1,0:T(8,128)} %param.9) | copy-start | bytes 1179652
  0.7 1.6 %copy-start.4 = (f32[8,32,128]{2,1,0:T(8,128)S(1)}, f32[8,32,128]{2,1,0:T(8,128)}, u32[]{:S(2)}) copy-start(f32[8,32,128]{2,1,0:T(8,128)} %param.11) | copy-start | bytes 393220
  0.7 1.6 %copy-start.5 = (f32[8,32,128]{2,1,0:T(8,128)S(1)}, f32[8,32,128]{2,1,0:T(8,128)}, u32[]{:S(2)}) copy-start(f32[8,32,128]{2,1,0:T(8,128)} %param.12) | copy-start | bytes 393220
  0.7 1.7 %copy-start.6 = (f32[8,32,128]{2,1,0:T(8,128)S(1)}, f32[8,32,128]{2,1,0:T(8,128)}, u32[]{:S(2)}) copy-start(f32[8,32,128]{2,1,0:T(8,128)} %param.13) | copy-start | bytes 393220
  0.7 1.7 %copy-start.2 = (s32[8,128]{1,0:T(8,128)S(1)}, s32[8,128]{1,0:T(8,128)}, u32[]{:S(2)}) copy-start(s32[8,128]{1,0:T(8,128)} %mask.3) | copy-start | bytes 12292
  0.7 1.7 %copy-start.1 = (f32[8,128]{1,0:T(8,128)S(1)}, f32[8,128]{1,0:T(8,128)}, u32[]{:S(2)}) copy-start(f32[8,128]{1,0:T(8,128)} %pre.3) | copy-start | bytes 12292
  3.3 8.9 %collective-permute-start = (f32[7,32,128]{2,1,0:T(8,128)S(1)}, f32[7,32,128]{2,1,0:T(8,128)S(1)}, u32[]{:S(2)}, u32[]{:S(2)}) collective-permute-start(f32[7,32,128]{2,1,0:T(8,128)S(1)} %get-tuple-element.47), channel_id=1, source_target_pairs={{0,8},{8,16},{16,24},{24,32},{32,40},{40,48},{48,56},{56,64},{64,7... | collective-permute-start | bytes 344072 | tf_op jit(solution)/shard_map/ppermute | solution.py:476
  3.4 8.8 %collective-permute-start.1 = (f32[7,32,128]{2,1,0:T(8,128)S(1)}, f32[7,32,128]{2,1,0:T(8,128)S(1)}, u32[]{:S(2)}, u32[]{:S(2)}) collective-permute-start(f32[7,32,128]{2,1,0:T(8,128)S(1)} %get-tuple-element.48), channel_id=1, source_target_pairs={{0,248},{8,0},{16,8},{24,16},{32,24},{40,32},{48,40},{56,48},{64,5... | collective-permute-start | bytes 344072 | tf_op jit(solution)/shard_map/ppermute | solution.py:476
  13.7 7.3 %collective-permute-start.2 = (f32[12,32,128]{2,1,0:T(8,128)S(1)}, f32[12,32,128]{2,1,0:T(8,128)S(1)}, u32[]{:S(2)}, u32[]{:S(2)}) collective-permute-start(f32[12,32,128]{2,1,0:T(8,128)S(1)} %get-tuple-element.49), channel_id=1, source_target_pairs={{0,1},{2,3},{4,5},{6,7},{1,0},{3,2},{5,4},{7,6},{8,9},{10,11},{12,... | collective-permute-start | bytes 589832 | tf_op jit(solution)/shard_map/ppermute | solution.py:482
  16.7 10.0 %collective-permute-start.3 = (f32[12,32,128]{2,1,0:T(8,128)S(1)}, f32[12,32,128]{2,1,0:T(8,128)S(1)}, u32[]{:S(2)}, u32[]{:S(2)}) collective-permute-start(f32[12,32,128]{2,1,0:T(8,128)S(1)} %get-tuple-element.50), channel_id=1, source_target_pairs={{1,2},{3,4},{5,6},{2,1},{4,3},{6,5},{9,10},{11,12},{13,14},{10,9},... | collective-permute-start | bytes 589832 | tf_op jit(solution)/shard_map/ppermute | solution.py:482
  26.8 13.3 %collective-permute-start.7 = (f32[7,16,256]{2,1,0:T(8,128)S(1)}, f32[7,16,256]{2,1,0:T(8,128)S(1)}, u32[]{:S(2)}, u32[]{:S(2)}) collective-permute-start(f32[7,16,256]{2,1,0:T(8,128)S(1)} %get-tuple-element.67), channel_id=1, source_target_pairs={{0,8},{8,16},{16,24},{24,32},{32,40},{40,48},{48,56},{56,64},{64,7... | collective-permute-start | bytes 344072 | tf_op jit(solution)/shard_map/ppermute | solution.py:476
  26.9 6.5 %collective-permute-start.4 = (f32[16,256]{1,0:T(8,128)S(1)}, f32[16,256]{1,0:T(8,128)S(1)}, u32[]{:S(2)}, u32[]{:S(2)}) collective-permute-start(f32[16,256]{1,0:T(8,128)S(1)} %get-tuple-element.57), channel_id=1, source_target_pairs={{0,8},{8,16},{16,24},{24,32},{32,40},{40,48},{48,56},{56,64},{64,7... | collective-permute-start | bytes 49160 | tf_op jit(solution)/shard_map/ppermute | solution.py:476
  34.2 6.4 %collective-permute-start.5 = (f32[7,32,128]{2,1,0:T(8,128)S(1)}, f32[7,32,128]{2,1,0:T(8,128)S(1)}, u32[]{:S(2)}, u32[]{:S(2)}) collective-permute-start(f32[7,32,128]{2,1,0:T(8,128)S(1)} %get-tuple-element.64), channel_id=1, source_target_pairs={{0,1},{2,3},{4,5},{6,7},{1,0},{3,2},{5,4},{7,6},{8,9},{10,11},{12,... | collective-permute-start | bytes 344072 | tf_op jit(solution)/shard_map/ppermute | solution.py:482
  34.3 9.4 %collective-permute-start.6 = (f32[7,32,128]{2,1,0:T(8,128)S(1)}, f32[7,32,128]{2,1,0:T(8,128)S(1)}, u32[]{:S(2)}, u32[]{:S(2)}) collective-permute-start(f32[7,32,128]{2,1,0:T(8,128)S(1)} %get-tuple-element.65), channel_id=1, source_target_pairs={{1,2},{3,4},{5,6},{2,1},{4,3},{6,5},{9,10},{11,12},{13,14},{10,9},... | collective-permute-start | bytes 344072 | tf_op jit(solution)/shard_map/ppermute | solution.py:482
  40.2 6.6 %collective-permute-start.8 = (f32[7,16,256]{2,1,0:T(8,128)S(1)}, f32[7,16,256]{2,1,0:T(8,128)S(1)}, u32[]{:S(2)}, u32[]{:S(2)}) collective-permute-start(f32[7,16,256]{2,1,0:T(8,128)S(1)} %pad_maximum_fusion), channel_id=1, source_target_pairs={{0,8},{8,16},{16,24},{24,32},{32,40},{40,48},{48,56},{56,64},{64,7... | collective-permute-start | bytes 344072 | tf_op jit(solution)/shard_map/ppermute | solution.py:476
  40.3 8.7 %collective-permute-start.11 = (f32[16,256]{1,0:T(8,128)S(1)}, f32[16,256]{1,0:T(8,128)S(1)}, u32[]{:S(2)}, u32[]{:S(2)}) collective-permute-start(f32[16,256]{1,0:T(8,128)S(1)} %slice_bitcast_fusion.2), channel_id=1, source_target_pairs={{0,16},{8,24},{16,32},{24,40},{32,48},{40,56},{48,64},{56,72},{64,... | collective-permute-start | bytes 49160 | tf_op jit(solution)/shard_map/ppermute | solution.py:476
  46.8 8.5 %collective-permute-start.9 = (f32[5,16,256]{2,1,0:T(8,128)S(1)}, f32[5,16,256]{2,1,0:T(8,128)S(1)}, u32[]{:S(2)}, u32[]{:S(2)}) collective-permute-start(f32[5,16,256]{2,1,0:T(8,128)S(1)} %shard_map.110), channel_id=1, source_target_pairs={{0,8},{8,16},{16,24},{24,32},{32,40},{40,48},{48,56},{56,64},{64,7... | collective-permute-start | bytes 245768 | tf_op jit(solution)/shard_map/ppermute | solution.py:476
  49.8 7.3 %collective-permute-start.13 = (f32[7,32,128]{2,1,0:T(8,128)S(1)}, f32[7,32,128]{2,1,0:T(8,128)S(1)}, u32[]{:S(2)}, u32[]{:S(2)}) collective-permute-start(f32[7,32,128]{2,1,0:T(8,128)S(1)} %get-tuple-element.76), channel_id=1, source_target_pairs={{0,1},{2,3},{4,5},{6,7},{1,0},{3,2},{5,4},{7,6},{8,9},{10,11},{12,... | collective-permute-start | bytes 344072 | tf_op jit(solution)/shard_map/ppermute | solution.py:482
  49.9 9.4 %collective-permute-start.14 = (f32[7,32,128]{2,1,0:T(8,128)S(1)}, f32[7,32,128]{2,1,0:T(8,128)S(1)}, u32[]{:S(2)}, u32[]{:S(2)}) collective-permute-start(f32[7,32,128]{2,1,0:T(8,128)S(1)} %get-tuple-element.77), channel_id=1, source_target_pairs={{1,2},{3,4},{5,6},{2,1},{4,3},{6,5},{9,10},{11,12},{13,14},{10,9},... | collective-permute-start | bytes 344072 | tf_op jit(solution)/shard_map/ppermute | solution.py:482
  55.4 6.2 %collective-permute-start.12 = (f32[5,16,256]{2,1,0:T(8,128)S(1)}, f32[5,16,256]{2,1,0:T(8,128)S(1)}, u32[]{:S(2)}, u32[]{:S(2)}) collective-permute-start(f32[5,16,256]{2,1,0:T(8,128)S(1)} %pad_maximum_fusion.1), channel_id=1, source_target_pairs={{0,8},{8,16},{16,24},{24,32},{32,40},{40,48},{48,56},{56,64},{64,7... | collective-permute-start | bytes 245768 | tf_op jit(solution)/shard_map/ppermute | solution.py:476
  55.5 8.2 %collective-permute-start.10 = (f32[16,256]{1,0:T(8,128)S(1)}, f32[16,256]{1,0:T(8,128)S(1)}, u32[]{:S(2)}, u32[]{:S(2)}) collective-permute-start(f32[16,256]{1,0:T(8,128)S(1)} %slice_bitcast_fusion.3), channel_id=1, source_target_pairs={{0,16},{8,24},{16,32},{24,40},{32,48},{40,56},{48,64},{56,72},{64,... | collective-permute-start | bytes 49160 | tf_op jit(solution)/shard_map/ppermute | solution.py:476
  61.7 7.4 %collective-permute-start.17 = (f32[3,16,256]{2,1,0:T(8,128)S(1)}, f32[3,16,256]{2,1,0:T(8,128)S(1)}, u32[]{:S(2)}, u32[]{:S(2)}) collective-permute-start(f32[3,16,256]{2,1,0:T(8,128)S(1)} %shard_map.115), channel_id=1, source_target_pairs={{0,8},{8,16},{16,24},{24,32},{32,40},{40,48},{48,56},{56,64},{64,7... | collective-permute-start | bytes 147464 | tf_op jit(solution)/shard_map/ppermute | solution.py:476
  64.5 10.4 %collective-permute-start.15 = (f32[7,32,128]{2,1,0:T(8,128)S(1)}, f32[7,32,128]{2,1,0:T(8,128)S(1)}, u32[]{:S(2)}, u32[]{:S(2)}) collective-permute-start(f32[7,32,128]{2,1,0:T(8,128)S(1)} %get-tuple-element.83), channel_id=1, source_target_pairs={{0,1},{2,3},{4,5},{6,7},{1,0},{3,2},{5,4},{7,6},{8,9},{10,11},{12,... | collective-permute-start | bytes 344072 | tf_op jit(solution)/shard_map/ppermute | solution.py:482
  64.6 10.3 %collective-permute-start.16 = (f32[7,32,128]{2,1,0:T(8,128)S(1)}, f32[7,32,128]{2,1,0:T(8,128)S(1)}, u32[]{:S(2)}, u32[]{:S(2)}) collective-permute-start(f32[7,32,128]{2,1,0:T(8,128)S(1)} %get-tuple-element.84), channel_id=1, source_target_pairs={{1,2},{3,4},{5,6},{2,1},{4,3},{6,5},{9,10},{11,12},{13,14},{10,9},... | collective-permute-start | bytes 344072 | tf_op jit(solution)/shard_map/ppermute | solution.py:482
  69.2 5.7 %collective-permute-start.18 = (f32[3,16,256]{2,1,0:T(8,128)S(1)}, f32[3,16,256]{2,1,0:T(8,128)S(1)}, u32[]{:S(2)}, u32[]{:S(2)}) collective-permute-start(f32[3,16,256]{2,1,0:T(8,128)S(1)} %pad_maximum_fusion.2), channel_id=1, source_target_pairs={{0,8},{8,16},{16,24},{24,32},{32,40},{40,48},{48,56},{56,64},{64,7... | collective-permute-start | bytes 147464 | tf_op jit(solution)/shard_map/ppermute | solution.py:476
  75.0 5.3 %collective-permute-start.19 = (f32[1,16,256]{2,1,0:T(8,128)S(1)}, f32[1,16,256]{2,1,0:T(8,128)S(1)}, u32[]{:S(2)}, u32[]{:S(2)}) collective-permute-start(f32[1,16,256]{2,1,0:T(8,128)S(1)} %shard_map.116), channel_id=1, source_target_pairs={{0,8},{8,16},{16,24},{24,32},{32,40},{40,48},{48,56},{56,64},{64,7... | collective-permute-start | bytes 49160 | tf_op jit(solution)/shard_map/ppermute | solution.py:476

commit v6 on v5

--- a/solution.py
+++ b/solution.py
@@ -52,6 +52,11 @@
     return tile if by == 0 else pltpu.roll(tile, by, 1)
 
 
+def in_slot(lane, i):
+    first = W * i % LANES
+    return (lane >= first) & (lane < first + W)
+
+
 def ahead_x(f):
     return pltpu.roll(f, f.shape[1] - 1, 1)
 
@@ -61,13 +66,11 @@
 
 
 def ahead_y(f):
-    row = lax.broadcasted_iota(jnp.int32, f.shape, 0)
-    return jnp.where(row == NY - 1, 0.0, pltpu.roll(f, NY - 1, 0))
+    return jnp.concatenate([f[1:], jnp.zeros((1, f.shape[1]), jnp.float32)], axis=0)
 
 
 def behind_y(f):
-    row = lax.broadcasted_iota(jnp.int32, f.shape, 0)
-    return jnp.where(row == 0, 0.0, pltpu.roll(f, 1, 0))
+    return jnp.concatenate([jnp.zeros((1, f.shape[1]), jnp.float32), f[:-1]], axis=0)
 
 
 def plane_of(refs, f, z):
@@ -213,9 +216,9 @@
     nxt = jnp.zeros((8, LANES), jnp.float32)
     prv = jnp.zeros((8, LANES), jnp.float32)
     for i, plane in enumerate([owed[j] for j in range(STEPS)] + [pre[...], mask[...].astype(jnp.float32)]):
-        here = (lane8 >= W * i) & (lane8 < W * (i + 1))
-        nxt = jnp.where(here, rolled(plane, W * i - (LANES - W)), nxt)
-        prv = jnp.where(here, rolled(plane, W * i), prv)
+        moved = rolled(plane, W * (i + 1))
+        nxt = jnp.where(in_slot(lane8, i), moved, nxt)
+        prv = jnp.where(in_slot(lane8, i + 1), moved, prv)
     to_next[6] = jnp.zeros((NY, LANES), jnp.float32)
     to_prev[6] = jnp.zeros((NY, LANES), jnp.float32)
     to_next[6, 0:8, :] = nxt
@@ -226,9 +229,9 @@
         prv = jnp.zeros((NY, LANES), jnp.float32)
         for i in range(16):
             plane = fields[2 * t + i // 8, i % 8]
-            here = (lane >= W * i) & (lane < W * (i + 1))
-            nxt = jnp.where(here, rolled(plane, W * i - (LANES - W)), nxt)
-            prv = jnp.where(here, rolled(plane, W * i), prv)
+            moved = rolled(plane, W * (i + 1))
+            nxt = jnp.where(in_slot(lane, i), moved, nxt)
+            prv = jnp.where(in_slot(lane, i + 1), moved, prv)
         to_next[t] = nxt
         to_prev[t] = prv
 
@@ -253,11 +256,7 @@
     for k, f in enumerate((SXX, SXY, SXZ, SYZ, SZZ, SYY, VX, VY, VZ, B, LAM, MU)):
         for z in range(8):
             at = (k % 2) * 8 + z
-            edge = jnp.where(
-                lane < LANES // 2,
-                rolled(from_next[k // 2], -W * at),
-                rolled(from_prev[k // 2], LANES - W - W * at),
-            )
+            edge = rolled(jnp.where(in_slot(lane, at + 1), from_next[k // 2], from_prev[k // 2]), -W * (at + 1))
             to = plane_of(refs, f, z + 2)
             to[:, :LANES] = fields[k, z]
             to[:, LANES:] = edge
@@ -265,11 +264,7 @@
     lists[...] = jnp.zeros_like(lists)
     for i in range(STEPS + 2):
         plane = owed[i] if i < STEPS else (pre, mask)[i - STEPS][...].astype(jnp.float32)
-        edge = jnp.where(
-            lane8 < LANES // 2,
-            rolled(from_next[6, 0:8, :], -W * i),
-            rolled(from_prev[6, 0:8, :], LANES - W - W * i),
-        )
+        edge = rolled(jnp.where(in_slot(lane8, i + 1), from_next[6, 0:8, :], from_prev[6, 0:8, :]), -W * (i + 1))
         to, j = (lists, i) if i < STEPS else (fp, i - STEPS)
         to[j, 2:10, :LANES] = plane
         to[j, 2:10, LANES:] = edge
@@ -521,17 +516,22 @@
             {7: 0, 8: 1, 9: 2},
         )
         if step + 2 < STEPS:
-            v, q, one, two, ahead = call(
+            more_pairs = step + 4 < STEPS
+            v, q, one, two, *ahead_out = call(
                 first_part_kernel if first else part_kernel,
-                [v3, q1] + [(TILES, NY, LANES)] * 2 + [plane],
+                [v3, q1] + [(TILES, NY, LANES)] * 2 + [plane] * more_pairs,
                 [owed, m, fp, ahead] + ([] if first else [near]) + [s, v, q],
                 {5: 0, 6: 1} if first else {6: 0, 7: 1},
+                scratch=[] if more_pairs else [pltpu.VMEM(plane, jnp.float32)],
             )
         if step + 2 < STEPS:
             next_lists = got[1:] + coefs[: left - 1, None, None] * rates[None]
-            lists = along_strike(jnp.concatenate([next_lists, ahead[None]]), 1)
-            near = lists[left - 1]
-            ahead = along_strike(next_lists[1], 2)
+            if step + 4 < STEPS:
+                lists = along_strike(jnp.concatenate([next_lists, ahead_out[0][None]]), 1)
+                near = lists[left - 1]
+                ahead = along_strike(next_lists[1], 2)
+            else:
+                lists = along_strike(next_lists, 1)
             late = got
     return tuple(call(end_kernel, [velocity.shape, stress.shape], [fp, got, v, s, q]))
 

time: 82.2 us -> 81.4 us (level)
    pallas_call x15, Pallas kernels: 14 us -> 13.2 us  [call(): pl.pallas_call(body, out_shape=[jax.ShapeDtypeStruct(s, jnp.float32) for...]
  transfers between devices with their start and end apart: 20 -> 20, of which waited for: 12 -> 12; matrix products, arithmetic and copies ran while one was open for 0% -> 0% of each run, Pallas kernels for 12% -> 13%
where the time goes in v6:
time: 81.4 us; the launch traced here: 80.4 us
  waiting for transfers between devices  35.3 us (43%)
  starting transfers between devices  29.1 us (36%)
  Pallas kernels  13.2 us (16%)
  local copies, waits for them, and re-layouts  1.41 us (2%)
  between operations  1.07 us (1%)
    ppermute x8, starting transfers between devices, swapped(): return lax.ppermute(value, 'depth', pairs + [(j, i) for i, j in pairs])  21.7 us
    ppermute x12, waiting for transfers between devices, along_strike(): return lax.ppermute(value, 'strike', [(i, (i + by) % n) for i in range(n)])  21.1 us
    ppermute x8, waiting for transfers between devices, swapped(): return lax.ppermute(value, 'depth', pairs + [(j, i) for i, j in pairs])  14.2 us
    pallas_call x15, Pallas kernels, call(): pl.pallas_call(body, out_shape=[jax.ShapeDtypeStruct(s, jnp.float32) for...  13.2 us
    ppermute x12, starting transfers between devices, along_strike(): return lax.ppermute(value, 'strike', [(i, (i + by) % n) for i in range(n)])  7.41 us
  transfers between devices with their start and end apart: 20, of which 12 were waited for; matrix products, arithmetic and copies ran while one was open for 0% of the time, Pallas kernels for 13%

profile of v6, /device:TPU:6, one launch (start us, length us, event | category | flops | bytes accessed | tf_op | source)
XLA Modules:
  0.0 80.4 jit_solution(14885572490620089676)
XLA Ops:
  0.7 1.3 %constant_dynamic-update-slice_fusion.1 = f32[12,8,32,128]{3,2,1,0:T(8,128)S(1)} fusion(f32[6,8,32,128]{3,2,1,0:T(8,128)} %param.10), kind=kLoop, calls=%fused_computation.13 | loop fusion | bytes 1572864
  2.1 0.2 shard_map.104.owed
  2.4 0.5 shard_map.105
  2.9 0.1 collective-permute-start
  2.9 6.4 %collective-permute-start.1 = (f32[7,32,128]{2,1,0:T(8,128)S(1)}, f32[7,32,128]{2,1,0:T(8,128)S(1)}, u32[]{:S(2)}, u32[]{:S(2)}) collective-permute-start(f32[7,32,128]{2,1,0:T(8,128)S(1)} %get-tuple-element.47), channel_id=1, source_target_pairs={{0,248},{8,0},{16,8},{24,16},{32,24},{40,32},{48,40},{56,48},{64,5... | collective-permute-start | bytes 344072 | tf_op jit(solution)/shard_map/ppermute | solution.py:471
  9.3 2.4 %collective-permute-done.from_prev = f32[7,32,128]{2,1,0:T(8,128)S(1)} collective-permute-done((f32[7,32,128]{2,1,0:T(8,128)S(1)}, f32[7,32,128]{2,1,0:T(8,128)S(1)}, u32[]{:S(2)}, u32[]{:S(2)}) %collective-permute-start) | collective-permute-done | bytes 114720 | tf_op jit(solution)/shard_map/ppermute | solution.py:471
  11.7 1.2 %shard_map.106 = (f32[3,12,32,256]{3,2,1,0:T(8,128)S(1)}, f32[5,12,32,256]{3,2,1,0:T(8,128)S(1)}, f32[12,32,256]{2,1,0:T(8,128)S(1)}, f32[3,8,32,256]{3,2,1,0:T(...) custom-call(f32[12,8,32,128]{3,2,1,0:T(8,128)S(1)} %bitcast_dynamic-, ...), custom_call_target="tpu_custom_call" | custom-call | flops 4000000 | bytes 4000000 | tf_op jit(solution)/shard_map/pallas_call | solution.py:34
  12.9 3.0 %collective-permute-start.2 = (f32[12,32,128]{2,1,0:T(8,128)S(1)}, f32[12,32,128]{2,1,0:T(8,128)S(1)}, u32[]{:S(2)}, u32[]{:S(2)}) collective-permute-start(f32[12,32,128]{2,1,0:T(8,128)S(1)} %get-tuple-element.48), channel_id=1, source_target_pairs={{0,1},{2,3},{4,5},{6,7},{1,0},{3,2},{5,4},{7,6},{8,9},{10,11},{12,... | collective-permute-start | bytes 589832 | tf_op jit(solution)/shard_map/ppermute | solution.py:477
  15.9 2.8 %collective-permute-start.3 = (f32[12,32,128]{2,1,0:T(8,128)S(1)}, f32[12,32,128]{2,1,0:T(8,128)S(1)}, u32[]{:S(2)}, u32[]{:S(2)}) collective-permute-start(f32[12,32,128]{2,1,0:T(8,128)S(1)} %get-tuple-element.49), channel_id=1, source_target_pairs={{1,2},{3,4},{5,6},{2,1},{4,3},{6,5},{9,10},{11,12},{13,14},{10,9},... | collective-permute-start | bytes 589832 | tf_op jit(solution)/shard_map/ppermute | solution.py:477
  18.7 1.5 %collective-permute-done.2.one = f32[12,32,128]{2,1,0:T(8,128)S(1)} collective-permute-done((f32[12,32,128]{2,1,0:T(8,128)S(1)}, f32[12,32,128]{2,1,0:T(8,128)S(1)}, u32[]{:S(2)}, u32[]{:S(2)}) %collective-permute-start.2) | collective-permute-done | bytes 196640 | tf_op jit(solution)/shard_map/ppermute | solution.py:477
  20.2 5.7 %collective-permute-done.3.two = f32[12,32,128]{2,1,0:T(8,128)S(1)} collective-permute-done((f32[12,32,128]{2,1,0:T(8,128)S(1)}, f32[12,32,128]{2,1,0:T(8,128)S(1)}, u32[]{:S(2)}, u32[]{:S(2)}) %collective-permute-start.3) | collective-permute-done | bytes 196640 | tf_op jit(solution)/shard_map/ppermute | solution.py:477
  25.9 0.1 shard_map.107
  26.0 0.1 collective-permute-start.7
  26.1 0.1 collective-permute-start.4
  26.2 1.8 %shard_map.108 = (f32[3,12,32,256]{3,2,1,0:T(8,128)S(1)}, f32[5,12,32,256]{3,2,1,0:T(8,128)S(1)}, f32[12,32,256]{2,1,0:T(8,128)S(1)}, f32[16,256]{1,0:T(8,128)S(1)}) custom-call(f32[3,8,32,256]{3,2,1,0:T(8,128)S(1)} %get-tuple-element.52.m.edge_m, ...), custom_call_target="tpu_custom_call", output_to_operand_aliasing={{0}: (7, {}), {1}: (8, {}), {2}: (9, {})} | custom-call | flops 4000000 | bytes 4000000 | tf_op jit(solution)/shard_map/pallas_call | solution.py:34
  28.0 4.6 %collective-permute-done.4.ahead = f32[16,256]{1,0:T(8,128)S(1)} collective-permute-done((f32[16,256]{1,0:T(8,128)S(1)}, f32[16,256]{1,0:T(8,128)S(1)}, u32[]{:S(2)}, u32[]{:S(2)}) %collective-permute-start.4) | collective-permute-done | bytes 16416 | tf_op jit(solution)/shard_map/ppermute | solution.py:471
  32.6 0.8 shard_map.109
  33.4 0.1 collective-permute-start.5
  33.5 5.7 %collective-permute-start.6 = (f32[7,32,128]{2,1,0:T(8,128)S(1)}, f32[7,32,128]{2,1,0:T(8,128)S(1)}, u32[]{:S(2)}, u32[]{:S(2)}) collective-permute-start(f32[7,32,128]{2,1,0:T(8,128)S(1)} %get-tuple-element.64), channel_id=1, source_target_pairs={{1,2},{3,4},{5,6},{2,1},{4,3},{6,5},{9,10},{11,12},{13,14},{10,9},... | collective-permute-start | bytes 344072 | tf_op jit(solution)/shard_map/ppermute | solution.py:477
  39.3 0.1 slice_add_fusion
  39.4 0.1 collective-permute-start.8
  39.5 0.1 collective-permute-start.11
  39.6 0.2 collective-permute-done.5.one
  39.8 3.1 %collective-permute-done.6.two = f32[7,32,128]{2,1,0:T(8,128)S(1)} collective-permute-done((f32[7,32,128]{2,1,0:T(8,128)S(1)}, f32[7,32,128]{2,1,0:T(8,128)S(1)}, u32[]{:S(2)}, u32[]{:S(2)}) %collective-permute-start.6) | collective-permute-done | bytes 114720 | tf_op jit(solution)/shard_map/ppermute | solution.py:477
  42.8 3.1 %collective-permute-done.8.lists = f32[7,16,256]{2,1,0:T(8,128)S(1)} collective-permute-done((f32[7,16,256]{2,1,0:T(8,128)S(1)}, f32[7,16,256]{2,1,0:T(8,128)S(1)}, u32[]{:S(2)}, u32[]{:S(2)}) %collective-permute-start.8) | collective-permute-done | bytes 114720 | tf_op jit(solution)/shard_map/ppermute | solution.py:471
  45.9 0.1 shard_map.110
  46.0 0.3 collective-permute-start.9
  46.3 1.8 %shard_map.111 = (f32[3,12,32,256]{3,2,1,0:T(8,128)S(1)}, f32[5,12,32,256]{3,2,1,0:T(8,128)S(1)}, f32[12,32,256]{2,1,0:T(8,128)S(1)}, f32[16,256]{1,0:T(8,128)S(1)}) custom-call(f32[3,8,32,256]{3,2,1,0:T(8,128)S(1)} %get-tuple-element.52.m.edge_m, ...), custom_call_target="tpu_custom_call", output_to_operand_aliasing={{0}: (7, {}), {1}: (8, {}), {2}: (9, {})} | custom-call | flops 4000000 | bytes 4000000 | tf_op jit(solution)/shard_map/pallas_call | solution.py:34
  48.2 0.8 shard_map.112
  49.0 0.1 collective-permute-start.13
  49.1 5.4 %collective-permute-start.14 = (f32[7,32,128]{2,1,0:T(8,128)S(1)}, f32[7,32,128]{2,1,0:T(8,128)S(1)}, u32[]{:S(2)}, u32[]{:S(2)}) collective-permute-start(f32[7,32,128]{2,1,0:T(8,128)S(1)} %get-tuple-element.76), channel_id=1, source_target_pairs={{1,2},{3,4},{5,6},{2,1},{4,3},{6,5},{9,10},{11,12},{13,14},{10,9},... | collective-permute-start | bytes 344072 | tf_op jit(solution)/shard_map/ppermute | solution.py:477
  54.6 0.1 collective-permute-start.12
  54.7 0.1 collective-permute-start.10
  54.8 1.5 %collective-permute-done.13.one = f32[7,32,128]{2,1,0:T(8,128)S(1)} collective-permute-done((f32[7,32,128]{2,1,0:T(8,128)S(1)}, f32[7,32,128]{2,1,0:T(8,128)S(1)}, u32[]{:S(2)}, u32[]{:S(2)}) %collective-permute-start.13) | collective-permute-done | bytes 114720 | tf_op jit(solution)/shard_map/ppermute | solution.py:477
  56.3 2.2 %collective-permute-done.14.two = f32[7,32,128]{2,1,0:T(8,128)S(1)} collective-permute-done((f32[7,32,128]{2,1,0:T(8,128)S(1)}, f32[7,32,128]{2,1,0:T(8,128)S(1)}, u32[]{:S(2)}, u32[]{:S(2)}) %collective-permute-start.14) | collective-permute-done | bytes 114720 | tf_op jit(solution)/shard_map/ppermute | solution.py:477
  58.5 2.3 %collective-permute-done.12.lists = f32[5,16,256]{2,1,0:T(8,128)S(1)} collective-permute-done((f32[5,16,256]{2,1,0:T(8,128)S(1)}, f32[5,16,256]{2,1,0:T(8,128)S(1)}, u32[]{:S(2)}, u32[]{:S(2)}) %collective-permute-start.12) | collective-permute-done | bytes 81952 | tf_op jit(solution)/shard_map/ppermute | solution.py:471
  60.8 0.1 shard_map.115
  60.9 0.1 collective-permute-start.17
  61.0 1.8 %shard_map.113 = (f32[3,12,32,256]{3,2,1,0:T(8,128)S(1)}, f32[5,12,32,256]{3,2,1,0:T(8,128)S(1)}, f32[12,32,256]{2,1,0:T(8,128)S(1)}, f32[16,256]{1,0:T(8,128)S(1)}) custom-call(f32[3,8,32,256]{3,2,1,0:T(8,128)S(1)} %get-tuple-element.52.m.edge_m, ...), custom_call_target="tpu_custom_call", output_to_operand_aliasing={{0}: (7, {}), {1}: (8, {}), {2}: (9, {})} | custom-call | flops 4000000 | bytes 4000000 | tf_op jit(solution)/shard_map/pallas_call | solution.py:34
  62.9 0.8 shard_map.114
  63.7 0.1 collective-permute-start.15
  63.8 4.5 %collective-permute-start.16 = (f32[7,32,128]{2,1,0:T(8,128)S(1)}, f32[7,32,128]{2,1,0:T(8,128)S(1)}, u32[]{:S(2)}, u32[]{:S(2)}) collective-permute-start(f32[7,32,128]{2,1,0:T(8,128)S(1)} %get-tuple-element.83), channel_id=1, source_target_pairs={{1,2},{3,4},{5,6},{2,1},{4,3},{6,5},{9,10},{11,12},{13,14},{10,9},... | collective-permute-start | bytes 344072 | tf_op jit(solution)/shard_map/ppermute | solution.py:477
  68.4 5.4 %collective-permute-done.18.lists = f32[2,16,256]{2,1,0:T(8,128)S(1)} collective-permute-done((f32[2,16,256]{2,1,0:T(8,128)S(1)}, f32[2,16,256]{2,1,0:T(8,128)S(1)}, u32[]{:S(2)}, u32[]{:S(2)}) %collective-permute-start.18) | collective-permute-done | bytes 32800 | tf_op jit(solution)/shard_map/ppermute | solution.py:471
  73.8 0.1 shard_map.116
  73.9 0.1 collective-permute-start.19
  74.0 2.0 %shard_map.117 = (f32[3,12,32,256]{3,2,1,0:T(8,128)S(1)}, f32[5,12,32,256]{3,2,1,0:T(8,128)S(1)}, f32[12,32,256]{2,1,0:T(8,128)S(1)}, f32[16,256]{1,0:T(8,128)}) custom-call(f32[3,8,32,256]{3,2,1,0:T(8,128)S(1)} %get-tuple-element.52.m.edge_m, ...), custom_call_target="tpu_custom_call", output_to_operand_aliasing={{0}: (7, {}), {1}: (8, {}), {2}: (9, {})} | custom-call | flops 4000000 | bytes 4000000 | tf_op jit(solution)/shard_map/pallas_call | solution.py:34
  76.0 3.2 %collective-permute-done.19.lists = f32[1,16,256]{2,1,0:T(8,128)S(1)} collective-permute-done((f32[1,16,256]{2,1,0:T(8,128)S(1)}, f32[1,16,256]{2,1,0:T(8,128)S(1)}, u32[]{:S(2)}, u32[]{:S(2)}) %collective-permute-start.19) | collective-permute-done | bytes 16416 | tf_op jit(solution)/shard_map/ppermute | solution.py:471
  79.3 1.1 %shard_map.118 = (f32[3,8,32,128]{3,2,1,0:T(8,128)}, f32[6,8,32,128]{3,2,1,0:T(8,128)}) custom-call(f32[2,16,256]{2,1,0:T(8,128)S(1)} %get-tuple-element.55.fp, f32[1,16,256]{2,1,0:T(8,128)S(1)} %collective-permute-done.19.lists, f32[3,12,32,256]{3,2,1,0:T(8,128)S(1)} %get-tuple-element.87.v, f32[5,12,32,256]{3,2,1,0:T(8,128)S(1)} %get-tuple-element.88.s, ...), custom_call_target="tpu_custom_call" | custom-call | flops 4000000 | bytes 4000000 | tf_op jit(solution)/shard_map/pallas_call | solution.py:34
  (38 shorter events, 0.4 us)
Async XLA Ops:
  0.6 1.4 %copy-start = (f32[64,8,128]{2,1,0:T(8,128)S(1)}, f32[64,8,128]{2,1,0:T(8,128)}, u32[]{:S(2)}) copy-start(f32[64,8,128]{2,1,0:T(8,128)} %past.1) | copy-start | bytes 786436
  0.6 1.3 %copy-start.7 = (f32[64]{0:T(128)S(1)}, f32[64]{0:T(128)}, u32[]{:S(2)}) copy-start(f32[64]{0:T(128)} %param.15) | copy-start | bytes 772
  0.7 1.6 %copy-start.3 = (f32[3,8,32,128]{3,2,1,0:T(8,128)S(1)}, f32[3,8,32,128]{3,2,1,0:T(8,128)}, u32[]{:S(2)}) copy-start(f32[3,8,32,128]{3,2,1,0:T(8,128)} %param.9) | copy-start | bytes 1179652
  0.7 1.6 %copy-start.4 = (f32[8,32,128]{2,1,0:T(8,128)S(1)}, f32[8,32,128]{2,1,0:T(8,128)}, u32[]{:S(2)}) copy-start(f32[8,32,128]{2,1,0:T(8,128)} %param.11) | copy-start | bytes 393220
  0.7 1.6 %copy-start.5 = (f32[8,32,128]{2,1,0:T(8,128)S(1)}, f32[8,32,128]{2,1,0:T(8,128)}, u32[]{:S(2)}) copy-start(f32[8,32,128]{2,1,0:T(8,128)} %param.12) | copy-start | bytes 393220
  0.7 1.7 %copy-start.6 = (f32[8,32,128]{2,1,0:T(8,128)S(1)}, f32[8,32,128]{2,1,0:T(8,128)}, u32[]{:S(2)}) copy-start(f32[8,32,128]{2,1,0:T(8,128)} %param.13) | copy-start | bytes 393220
  0.7 1.7 %copy-start.2 = (s32[8,128]{1,0:T(8,128)S(1)}, s32[8,128]{1,0:T(8,128)}, u32[]{:S(2)}) copy-start(s32[8,128]{1,0:T(8,128)} %mask.3) | copy-start | bytes 12292
  0.7 1.7 %copy-start.1 = (f32[8,128]{1,0:T(8,128)S(1)}, f32[8,128]{1,0:T(8,128)}, u32[]{:S(2)}) copy-start(f32[8,128]{1,0:T(8,128)} %pre.3) | copy-start | bytes 12292
  2.9 8.9 %collective-permute-start = (f32[7,32,128]{2,1,0:T(8,128)S(1)}, f32[7,32,128]{2,1,0:T(8,128)S(1)}, u32[]{:S(2)}, u32[]{:S(2)}) collective-permute-start(f32[7,32,128]{2,1,0:T(8,128)S(1)} %get-tuple-element.46), channel_id=1, source_target_pairs={{0,8},{8,16},{16,24},{24,32},{32,40},{40,48},{48,56},{56,64},{64,7... | collective-permute-start | bytes 344072 | tf_op jit(solution)/shard_map/ppermute | solution.py:471
  2.9 8.8 %collective-permute-start.1 = (f32[7,32,128]{2,1,0:T(8,128)S(1)}, f32[7,32,128]{2,1,0:T(8,128)S(1)}, u32[]{:S(2)}, u32[]{:S(2)}) collective-permute-start(f32[7,32,128]{2,1,0:T(8,128)S(1)} %get-tuple-element.47), channel_id=1, source_target_pairs={{0,248},{8,0},{16,8},{24,16},{32,24},{40,32},{48,40},{56,48},{64,5... | collective-permute-start | bytes 344072 | tf_op jit(solution)/shard_map/ppermute | solution.py:471
  12.9 7.3 %collective-permute-start.2 = (f32[12,32,128]{2,1,0:T(8,128)S(1)}, f32[12,32,128]{2,1,0:T(8,128)S(1)}, u32[]{:S(2)}, u32[]{:S(2)}) collective-permute-start(f32[12,32,128]{2,1,0:T(8,128)S(1)} %get-tuple-element.48), channel_id=1, source_target_pairs={{0,1},{2,3},{4,5},{6,7},{1,0},{3,2},{5,4},{7,6},{8,9},{10,11},{12,... | collective-permute-start | bytes 589832 | tf_op jit(solution)/shard_map/ppermute | solution.py:477
  15.9 10.0 %collective-permute-start.3 = (f32[12,32,128]{2,1,0:T(8,128)S(1)}, f32[12,32,128]{2,1,0:T(8,128)S(1)}, u32[]{:S(2)}, u32[]{:S(2)}) collective-permute-start(f32[12,32,128]{2,1,0:T(8,128)S(1)} %get-tuple-element.49), channel_id=1, source_target_pairs={{1,2},{3,4},{5,6},{2,1},{4,3},{6,5},{9,10},{11,12},{13,14},{10,9},... | collective-permute-start | bytes 589832 | tf_op jit(solution)/shard_map/ppermute | solution.py:477
  26.0 13.3 %collective-permute-start.7 = (f32[7,16,256]{2,1,0:T(8,128)S(1)}, f32[7,16,256]{2,1,0:T(8,128)S(1)}, u32[]{:S(2)}, u32[]{:S(2)}) collective-permute-start(f32[7,16,256]{2,1,0:T(8,128)S(1)} %get-tuple-element.66), channel_id=1, source_target_pairs={{0,8},{8,16},{16,24},{24,32},{32,40},{40,48},{48,56},{56,64},{64,7... | collective-permute-start | bytes 344072 | tf_op jit(solution)/shard_map/ppermute | solution.py:471
  26.1 6.5 %collective-permute-start.4 = (f32[16,256]{1,0:T(8,128)S(1)}, f32[16,256]{1,0:T(8,128)S(1)}, u32[]{:S(2)}, u32[]{:S(2)}) collective-permute-start(f32[16,256]{1,0:T(8,128)S(1)} %get-tuple-element.56), channel_id=1, source_target_pairs={{0,8},{8,16},{16,24},{24,32},{32,40},{40,48},{48,56},{56,64},{64,7... | collective-permute-start | bytes 49160 | tf_op jit(solution)/shard_map/ppermute | solution.py:471
  33.4 6.4 %collective-permute-start.5 = (f32[7,32,128]{2,1,0:T(8,128)S(1)}, f32[7,32,128]{2,1,0:T(8,128)S(1)}, u32[]{:S(2)}, u32[]{:S(2)}) collective-permute-start(f32[7,32,128]{2,1,0:T(8,128)S(1)} %get-tuple-element.63), channel_id=1, source_target_pairs={{0,1},{2,3},{4,5},{6,7},{1,0},{3,2},{5,4},{7,6},{8,9},{10,11},{12,... | collective-permute-start | bytes 344072 | tf_op jit(solution)/shard_map/ppermute | solution.py:477
  33.5 9.3 %collective-permute-start.6 = (f32[7,32,128]{2,1,0:T(8,128)S(1)}, f32[7,32,128]{2,1,0:T(8,128)S(1)}, u32[]{:S(2)}, u32[]{:S(2)}) collective-permute-start(f32[7,32,128]{2,1,0:T(8,128)S(1)} %get-tuple-element.64), channel_id=1, source_target_pairs={{1,2},{3,4},{5,6},{2,1},{4,3},{6,5},{9,10},{11,12},{13,14},{10,9},... | collective-permute-start | bytes 344072 | tf_op jit(solution)/shard_map/ppermute | solution.py:477
  39.4 6.6 %collective-permute-start.8 = (f32[7,16,256]{2,1,0:T(8,128)S(1)}, f32[7,16,256]{2,1,0:T(8,128)S(1)}, u32[]{:S(2)}, u32[]{:S(2)}) collective-permute-start(f32[7,16,256]{2,1,0:T(8,128)S(1)} %pad_maximum_fusion), channel_id=1, source_target_pairs={{0,8},{8,16},{16,24},{24,32},{32,40},{40,48},{48,56},{56,64},{64,7... | collective-permute-start | bytes 344072 | tf_op jit(solution)/shard_map/ppermute | solution.py:471
  39.5 8.7 %collective-permute-start.11 = (f32[16,256]{1,0:T(8,128)S(1)}, f32[16,256]{1,0:T(8,128)S(1)}, u32[]{:S(2)}, u32[]{:S(2)}) collective-permute-start(f32[16,256]{1,0:T(8,128)S(1)} %slice_bitcast_fusion.2), channel_id=1, source_target_pairs={{0,16},{8,24},{16,32},{24,40},{32,48},{40,56},{48,64},{56,72},{64,... | collective-permute-start | bytes 49160 | tf_op jit(solution)/shard_map/ppermute | solution.py:471
  46.0 8.4 %collective-permute-start.9 = (f32[5,16,256]{2,1,0:T(8,128)S(1)}, f32[5,16,256]{2,1,0:T(8,128)S(1)}, u32[]{:S(2)}, u32[]{:S(2)}) collective-permute-start(f32[5,16,256]{2,1,0:T(8,128)S(1)} %shard_map.110), channel_id=1, source_target_pairs={{0,8},{8,16},{16,24},{24,32},{32,40},{40,48},{48,56},{56,64},{64,7... | collective-permute-start | bytes 245768 | tf_op jit(solution)/shard_map/ppermute | solution.py:471
  49.0 7.3 %collective-permute-start.13 = (f32[7,32,128]{2,1,0:T(8,128)S(1)}, f32[7,32,128]{2,1,0:T(8,128)S(1)}, u32[]{:S(2)}, u32[]{:S(2)}) collective-permute-start(f32[7,32,128]{2,1,0:T(8,128)S(1)} %get-tuple-element.75), channel_id=1, source_target_pairs={{0,1},{2,3},{4,5},{6,7},{1,0},{3,2},{5,4},{7,6},{8,9},{10,11},{12,... | collective-permute-start | bytes 344072 | tf_op jit(solution)/shard_map/ppermute | solution.py:477
  49.1 9.4 %collective-permute-start.14 = (f32[7,32,128]{2,1,0:T(8,128)S(1)}, f32[7,32,128]{2,1,0:T(8,128)S(1)}, u32[]{:S(2)}, u32[]{:S(2)}) collective-permute-start(f32[7,32,128]{2,1,0:T(8,128)S(1)} %get-tuple-element.76), channel_id=1, source_target_pairs={{1,2},{3,4},{5,6},{2,1},{4,3},{6,5},{9,10},{11,12},{13,14},{10,9},... | collective-permute-start | bytes 344072 | tf_op jit(solution)/shard_map/ppermute | solution.py:477
  54.6 6.2 %collective-permute-start.12 = (f32[5,16,256]{2,1,0:T(8,128)S(1)}, f32[5,16,256]{2,1,0:T(8,128)S(1)}, u32[]{:S(2)}, u32[]{:S(2)}) collective-permute-start(f32[5,16,256]{2,1,0:T(8,128)S(1)} %pad_maximum_fusion.1), channel_id=1, source_target_pairs={{0,8},{8,16},{16,24},{24,32},{32,40},{40,48},{48,56},{56,64},{64,7... | collective-permute-start | bytes 245768 | tf_op jit(solution)/shard_map/ppermute | solution.py:471
  54.7 8.2 %collective-permute-start.10 = (f32[16,256]{1,0:T(8,128)S(1)}, f32[16,256]{1,0:T(8,128)S(1)}, u32[]{:S(2)}, u32[]{:S(2)}) collective-permute-start(f32[16,256]{1,0:T(8,128)S(1)} %slice_bitcast_fusion.3), channel_id=1, source_target_pairs={{0,16},{8,24},{16,32},{24,40},{32,48},{40,56},{48,64},{56,72},{64,... | collective-permute-start | bytes 49160 | tf_op jit(solution)/shard_map/ppermute | solution.py:471
  60.9 7.3 %collective-permute-start.17 = (f32[3,16,256]{2,1,0:T(8,128)S(1)}, f32[3,16,256]{2,1,0:T(8,128)S(1)}, u32[]{:S(2)}, u32[]{:S(2)}) collective-permute-start(f32[3,16,256]{2,1,0:T(8,128)S(1)} %shard_map.115), channel_id=1, source_target_pairs={{0,8},{8,16},{16,24},{24,32},{32,40},{40,48},{48,56},{56,64},{64,7... | collective-permute-start | bytes 147464 | tf_op jit(solution)/shard_map/ppermute | solution.py:471
  63.7 10.2 %collective-permute-start.15 = (f32[7,32,128]{2,1,0:T(8,128)S(1)}, f32[7,32,128]{2,1,0:T(8,128)S(1)}, u32[]{:S(2)}, u32[]{:S(2)}) collective-permute-start(f32[7,32,128]{2,1,0:T(8,128)S(1)} %get-tuple-element.82), channel_id=1, source_target_pairs={{0,1},{2,3},{4,5},{6,7},{1,0},{3,2},{5,4},{7,6},{8,9},{10,11},{12,... | collective-permute-start | bytes 344072 | tf_op jit(solution)/shard_map/ppermute | solution.py:477
  63.8 10.1 %collective-permute-start.16 = (f32[7,32,128]{2,1,0:T(8,128)S(1)}, f32[7,32,128]{2,1,0:T(8,128)S(1)}, u32[]{:S(2)}, u32[]{:S(2)}) collective-permute-start(f32[7,32,128]{2,1,0:T(8,128)S(1)} %get-tuple-element.83), channel_id=1, source_target_pairs={{1,2},{3,4},{5,6},{2,1},{4,3},{6,5},{9,10},{11,12},{13,14},{10,9},... | collective-permute-start | bytes 344072 | tf_op jit(solution)/shard_map/ppermute | solution.py:477
  68.3 5.5 %collective-permute-start.18 = (f32[2,16,256]{2,1,0:T(8,128)S(1)}, f32[2,16,256]{2,1,0:T(8,128)S(1)}, u32[]{:S(2)}, u32[]{:S(2)}) collective-permute-start(f32[2,16,256]{2,1,0:T(8,128)S(1)} %slice_add_fusion.2), channel_id=1, source_target_pairs={{0,8},{8,16},{16,24},{24,32},{32,40},{40,48},{48,56},{56,64},{64,7... | collective-permute-start | bytes 98312 | tf_op jit(solution)/shard_map/ppermute | solution.py:471
  73.9 5.3 %collective-permute-start.19 = (f32[1,16,256]{2,1,0:T(8,128)S(1)}, f32[1,16,256]{2,1,0:T(8,128)S(1)}, u32[]{:S(2)}, u32[]{:S(2)}) collective-permute-start(f32[1,16,256]{2,1,0:T(8,128)S(1)} %shard_map.116), channel_id=1, source_target_pairs={{0,8},{8,16},{16,24},{24,32},{32,40},{40,48},{48,56},{56,64},{64,7... | collective-permute-start | bytes 49160 | tf_op jit(solution)/shard_map/ppermute | solution.py:471
